TPU v7x, 32 devices: a whole 2x2x4 slice. The times are simulated.
32 devices in a mesh: dom: 8 (over z, y), sub: 4 (over x, core).
Axes of the slice: x: 2, y: 2, z: 4, core: 2. Of those that a mesh axis runs over, the one named last changes fastest.
Arguments:
- basis: float32 [2, 16, 32768], P(None, None, ('dom', 'sub')), may hold values from -6 to 6
- compact: float32 [2, 32, 16], replicated, may hold values from -1 to 1
- weights: float32 [2, 2, 32], replicated, may hold values from -5 to 5
- fresh: float32 [2, 32], replicated, may hold values from -1 to 1
- shifts: float32 [2, 2], replicated, may hold values from -1 to 1
- k_tiles: float32 [256, 3, 128, 128], P(('dom', 'sub'))
- pattern: int32 [256, 2], P(('dom', 'sub')), may hold values from 0 to 31
- mass: float32 [32768], P(('dom', 'sub')), may hold values from 0.5 to 2
- precond: float32 [256, 2, 128, 128], P(('dom', 'sub'))
- c_tiles: float32 [256, 128, 128], P(('dom', 'sub')), may hold values from -0.5 to 0.5
- c_rows: int32 [256], P(('dom', 'sub')), may hold values from 0 to 7
- c_side: int32 [256], P(('dom', 'sub')), may hold values from 0 to 1
- c_count: int32 [32], P(('dom', 'sub')), may hold values from 1 to 8, as said below
Outputs:
- new_basis: float32 [2, 2, 32768], P(None, None, ('dom', 'sub'))
- coeffs: float32 [2, 2, 18], replicated
Inputs may be any that keep to these rules, and one draw needn't show every extreme that they name: `pattern`: each tile row's coupled tiles lie in its own domain group. `c_rows`: a tile row of the device itself. `c_side`: 0 reads the domain below, 1 the domain above. The live slots of device d are its first c_count[d]; some device has all 8 live.
All inputs are finite; a program needn't handle non-finite values.
Results may differ from a plain program's by a relative error of at most 0.0003.
Values sent between devices are 32-bit elements; how exact they have to be, the bound alone decides.
No kernel may reach another device: no remote copies, remote signals or barrier semaphores. Data moves between devices by JAX's collectives and lax.ppermute only.
A program may use at most 64 MiB of HBM per device.

v0:
```python
import functools
import jax
import jax.numpy as jnp
from jax import lax
from jax.experimental import pallas as pl
from jax.experimental.pallas import tpu as pltpu
from jax.sharding import PartitionSpec as P

ITERS = 3
EPSILON = 1e-06
HIGH = lax.Precision.HIGHEST
F32 = jnp.float32
BF16 = jnp.bfloat16
NT_DIMS = (((1,), (1,)), ((), ()))
LANES = 128
AXES = ("dom", "sub")


def iota(shape, dim):
    return lax.broadcasted_iota(jnp.int32, shape, dim)


def split(x):
    high = x.astype(BF16).astype(F32)
    return high, x - high


def cmul(a, b):
    return a[0] * b[0] - a[1] * b[1], a[0] * b[1] + a[1] * b[0]


def conj(a):
    return a[0], -a[1]


def csub(a, b):
    return a[0] - b[0], a[1] - b[1]


def cadd(a, b):
    return a[0] + b[0], a[1] + b[1]


def scale(a, s):
    return a[0] * s, a[1] * s


def nt_dot(a, b, precision=None):
    return lax.dot_general(a, b, NT_DIMS, precision=precision, preferred_element_type=F32)


def store_parts(high_ref, low_ref, block, x):
    lanes = slice(block * LANES, (block + 1) * LANES)
    high, low = split(x)
    high_ref[:, lanes] = high.astype(BF16)
    low_ref[:, lanes] = low.astype(BF16)


def product(high_ref, low_ref, wide_ref, blocks):
    lanes = blocks * LANES
    wide = wide_ref[:, :lanes]
    total = nt_dot(high_ref[...], wide) + nt_dot(low_ref[...], wide)
    flipped = total.T
    rows = flipped.shape[0] // 4
    parts = [flipped[k * rows : (k + 1) * rows] for k in range(4)]
    return parts[0] + parts[2], parts[1] + parts[3]


def put(wide_ref, block, parts):
    wide_ref[:, block * LANES : (block + 1) * LANES] = jnp.concatenate(parts, axis=0).astype(BF16)


def parts_of(vector):
    real, imag = vector
    real_high, real_low = split(real)
    imag_high, imag_low = split(imag)
    return [real_high, imag_high, real_low, imag_low]


def precondition(vector, high_ref, low_ref, wide_ref):
    tiles = vector[0].shape[0]
    straight = parts_of(vector)
    turned = [-straight[1], straight[0], -straight[3], straight[2]]
    row = iota(vector[0].shape, 0)
    for tile in range(tiles):
        mask = row == tile
        put(wide_ref, 2 * tile, [jnp.where(mask, x, 0.0) for x in straight])
        put(wide_ref, 2 * tile + 1, [jnp.where(mask, x, 0.0) for x in turned])
    return product(high_ref, low_ref, wide_ref, 2 * tiles)


def load(ref):
    rows = ref.shape[0] // 2
    return ref[:rows], ref[rows:]


def save(ref, vector):
    ref[...] = jnp.concatenate(vector, axis=0)


def send(vector, first_ref, second_ref):
    even = lax.rem(lax.axis_index("dom"), 2) == 0
    rows = vector[0].shape[0]
    head = jnp.concatenate([vector[0][:1], vector[1][:1]], axis=0)
    tail = jnp.concatenate([vector[0][rows - 1 :], vector[1][rows - 1 :]], axis=0)
    first_ref[...] = jnp.where(even, tail, head)
    second_ref[...] = jnp.where(even, head, tail)


def mix_basis(coef, basis_ref):
    real, imag = coef
    tiles = basis_ref.shape[2] // LANES
    row = iota((tiles, LANES), 0)
    out_real = jnp.zeros((tiles, LANES), F32)
    out_imag = jnp.zeros((tiles, LANES), F32)
    for tile in range(tiles):
        lanes = slice(tile * LANES, (tile + 1) * LANES)
        base_real, base_imag = basis_ref[0, :, lanes], basis_ref[1, :, lanes]
        sum_real = jnp.sum(real * base_real - imag * base_imag, axis=0, keepdims=True)
        sum_imag = jnp.sum(real * base_imag + imag * base_real, axis=0, keepdims=True)
        out_real = jnp.where(row == tile, sum_real, out_real)
        out_imag = jnp.where(row == tile, sum_imag, out_imag)
    return out_real, out_imag


def coefficients(step, compact_ref, weights_ref, fresh_ref):
    beta = weights_ref[step]
    part_real = lax.dot_general(
        beta, compact_ref[0], (((1,), (0,)), ((), ())), precision=HIGH, preferred_element_type=F32
    )
    part_imag = lax.dot_general(
        beta, compact_ref[1], (((1,), (0,)), ((), ())), precision=HIGH, preferred_element_type=F32
    )
    row_real = part_real[0:1] - part_imag[1:2]
    row_imag = part_imag[0:1] + part_real[1:2]
    count = compact_ref.shape[2]
    same = iota((count, count), 0) == iota((count, count), 1)
    coef_real = jnp.sum(jnp.where(same, row_real, 0.0), axis=1, keepdims=True)
    coef_imag = jnp.sum(jnp.where(same, row_imag, 0.0), axis=1, keepdims=True)
    fresh = fresh_ref[...]
    gamma_real = jnp.sum(beta[0:1] * fresh[0:1] - beta[1:2] * fresh[1:2], axis=1, keepdims=True)
    gamma_imag = jnp.sum(beta[0:1] * fresh[1:2] + beta[1:2] * fresh[0:1], axis=1, keepdims=True)
    return (coef_real, coef_imag), (gamma_real, gamma_imag)


def start_kernel(
    basis_ref, compact_ref, weights_ref, fresh_ref, precond_ref,
    right_ref, image_ref, first_ref, second_ref, high_ref, low_ref,
    wide_ref,
):
    for tile in range(precond_ref.shape[0]):
        for part in range(2):
            store_parts(high_ref, low_ref, 2 * tile + part, precond_ref[tile, part])
    coef, _ = coefficients(0, compact_ref, weights_ref, fresh_ref)
    right = mix_basis(coef, basis_ref)
    save(right_ref, right)
    image = precondition(right, high_ref, low_ref, wide_ref)
    save(image_ref, image)
    send(image, first_ref, second_ref)


def prepare_kernel(
    n_dom, pattern_ref, rows_ref, side_ref, count_ref, basis_ref, k_ref, c_ref,
    high_ref, low_ref, pick_ref, below_ref, above_ref, inner_ref,
):
    tiles, slots_k = k_ref.shape[0], k_ref.shape[1]
    for tile in range(tiles):
        for slot in range(slots_k):
            store_parts(high_ref, low_ref, tile * slots_k + slot, k_ref[tile, slot])
    slots = c_ref.shape[0]
    for slot in range(slots):
        store_parts(high_ref, low_ref, tiles * slots_k + slot, c_ref[slot])
    mine = lax.axis_index("sub") * tiles
    row, lane = iota(pick_ref.shape, 0), iota(pick_ref.shape, 1)
    picked = jnp.zeros(pick_ref.shape, F32)
    for slot in range(slots_k - 1):
        for tile in range(tiles):
            column = pattern_ref[tile, slot] ^ mine
            picked = jnp.where((row == slot * tiles + tile) & (lane == column), 1.0, picked)
    pick_ref[...] = picked.astype(BF16)
    domain = lax.axis_index("dom")
    row = iota((tiles, LANES), 0)
    for slot in range(slots):
        live = slot < count_ref[0]
        side = side_ref[slot]
        here = row == rows_ref[slot]
        low_on = live & (side == 0) & (domain > 0)
        high_on = live & (side != 0) & (domain < n_dom - 1)
        below_ref[slot] = jnp.where(here & low_on, 1.0, 0.0)
        above_ref[slot] = jnp.where(here & high_on, 1.0, 0.0)
    real, imag = basis_ref[0], basis_ref[1]
    inner = nt_dot(real, jnp.concatenate([real, imag], axis=0), HIGH)
    inner = inner + nt_dot(imag, jnp.concatenate([imag, -real], axis=0), HIGH)
    inner_ref[...] = jnp.zeros(inner_ref.shape, F32)
    half, wide = inner_ref.shape[0], inner.shape[1]
    inner_ref[:, 6 * half : 6 * half + wide] = inner[:half]
    inner_ref[:, 6 * half + wide : 6 * half + 2 * wide] = inner[half:]


def operate(
    step, image_ref, blocks, first_ref, second_ref, shifts_ref, mass_ref,
    high_ref, low_ref, pick_ref, below_ref, above_ref, wide_ref,
):
    image = load(image_ref)
    tiles = image[0].shape[0]
    own = parts_of(image)
    gathered = [own] + [parts_of(load(block)) for block in blocks]
    table = jnp.concatenate(
        [jnp.concatenate([g[part] for g in gathered], axis=0) for part in range(4)], axis=1
    ).astype(BF16)
    chosen = jnp.dot(pick_ref[...], table, preferred_element_type=F32)
    others = chosen.shape[0] // tiles
    row = iota(image[0].shape, 0)
    for tile in range(tiles):
        mask = row == tile
        base = tile * (others + 1)
        put(wide_ref, base, [jnp.where(mask, x, 0.0) for x in own])
        for slot in range(others):
            rows = slice(slot * tiles, (slot + 1) * tiles)
            put(
                wide_ref,
                base + 1 + slot,
                [
                    jnp.where(mask, chosen[rows, part * LANES : (part + 1) * LANES], 0.0)
                    for part in range(4)
                ],
            )
    even = lax.rem(lax.axis_index("dom"), 2) == 0
    first, second = first_ref[...], second_ref[...]
    below = jnp.where(even, second, first)
    above = jnp.where(even, first, second)
    below = parts_of((below[0:1], below[1:2]))
    above = parts_of((above[0:1], above[1:2]))
    slots = below_ref.shape[0]
    base = tiles * (others + 1)
    for slot in range(slots):
        low_mask, high_mask = below_ref[slot], above_ref[slot]
        put(
            wide_ref,
            base + slot,
            [low_mask * below[part] + high_mask * above[part] for part in range(4)],
        )
    stiff = product(high_ref, low_ref, wide_ref, base + slots)
    mass = mass_ref[...]
    moved = (mass * image[0], mass * image[1])
    shift_real, shift_imag = shifts_ref[step, 0], shifts_ref[step, 1]
    real = stiff[0] - (shift_real * moved[0] - shift_imag * moved[1])
    imag = stiff[1] - (shift_real * moved[1] + shift_imag * moved[0])
    return real, imag


def level_kernel(step, others, image_ref, term_ref, *refs):
    blocks, refs = refs[:others], refs[others:]
    (
        first_in, second_in, shifts_ref, mass_ref, k_high, k_low, pick_ref, below_ref, above_ref,
        p_high, p_low, result_ref, next_ref, out_ref, first_ref, second_ref, wide_ref,
    ) = refs
    result = operate(
        step, image_ref, blocks, first_in, second_in, shifts_ref, mass_ref,
        k_high, k_low, pick_ref, below_ref, above_ref, wide_ref,
    )
    save(result_ref, result)
    term = csub(result, load(term_ref))
    save(next_ref, term)
    image = precondition(term, p_high, p_low, wide_ref)
    save(out_ref, image)
    send(image, first_ref, second_ref)


def last_kernel(step, others, image_ref, term_ref, *refs):
    blocks, refs = refs[:others], refs[others:]
    (
        first_in, second_in, shifts_ref, mass_ref, k_high, k_low, pick_ref, below_ref, above_ref,
        basis_ref, previous_ref, inner_ref,
    ) = refs[:12]
    earlier, refs = refs[12 : 12 + 2 * ITERS - 1], refs[12 + 2 * ITERS - 1 :]
    payload_ref, wide_ref, rows_ref = refs
    result = operate(
        step, image_ref, blocks, first_in, second_in, shifts_ref, mass_ref,
        k_high, k_low, pick_ref, below_ref, above_ref, wide_ref,
    )
    results = [load(ref) for ref in earlier[: ITERS - 1]] + [result]
    right = load(earlier[ITERS - 1])
    images = [load(ref) for ref in earlier[ITERS:]] + [load(image_ref)]
    vectors = results + [right] + images + [load(previous_ref)]
    count = len(vectors)
    for index, (real, imag) in enumerate(vectors):
        rows_ref[:, index, :] = real
        rows_ref[:, count + index, :] = imag
        rows_ref[:, 2 * count + index, :] = imag
        rows_ref[:, 3 * count + index, :] = -real
    tiles = rows_ref.shape[0]
    lefts, rights = [], []
    for tile in range(tiles):
        lanes = slice(tile * LANES, (tile + 1) * LANES)
        for part in range(2):
            left = rows_ref[tile, part * count : (part + 1) * count]
            lefts.append(jnp.concatenate([basis_ref[part, :, lanes], left], axis=0))
            rights.append(rows_ref[tile, 2 * part * count : 2 * (part + 1) * count])
    left = jnp.concatenate(lefts, axis=1)
    right_rows = jnp.concatenate(rights, axis=1)
    right_rows = jnp.concatenate([right_rows] * 3, axis=0)
    table = nt_dot(left, right_rows, HIGH)
    width = 2 * count
    lane = iota((count, 3 * width), 1)
    merged = jnp.where(
        lane < width, table[:count], jnp.where(lane < 2 * width, table[count : 2 * count], table[2 * count :])
    )
    total = jnp.concatenate(
        [merged, inner_ref[:, 3 * width :]], axis=1
    )

    @pl.loop(0, payload_ref.shape[0])
    def _(device):
        payload_ref[device] = total


def settle(
    total_rows, sums, inner, basis_ref, images, previous,
):
    count = sums.shape[0]
    width = 2 * count
    shape = sums.shape

    def column(lane, table=sums):
        return jnp.broadcast_to(table[:, lane : lane + 1], shape)

    def cell(row, lane):
        return jnp.broadcast_to(column(lane)[row : row + 1], shape)

    def entry(row, col):
        base = 2 * width
        return cell(row, base + col), cell(row, base + count + col)

    gram = {(a, b): entry(a, b) for a in range(ITERS) for b in range(a, ITERS)}
    target = [entry(a, ITERS) for a in range(ITERS)]
    lower, pivots = {}, []
    for col in range(ITERS):
        pivot = gram[col, col][0]
        for mid in range(col):
            real, imag = lower[col, mid]
            pivot = pivot - (real * real + imag * imag) * pivots[mid]
        pivots.append(pivot)
        for row in range(col + 1, ITERS):
            value = conj(gram[col, row])
            for mid in range(col):
                value = csub(value, scale(cmul(lower[row, mid], conj(lower[col, mid])), pivots[mid]))
            lower[row, col] = (value[0] / pivot, value[1] / pivot)
    forward = []
    for row in range(ITERS):
        value = target[row]
        for mid in range(row):
            value = csub(value, cmul(lower[row, mid], forward[mid]))
        forward.append(value)
    solved = [None] * ITERS
    for row in reversed(range(ITERS)):
        value = (forward[row][0] / pivots[row], forward[row][1] / pivots[row])
        for mid in range(row + 1, ITERS):
            value = csub(value, cmul(conj(lower[mid, row]), solved[mid]))
        solved[row] = value

    offset = ITERS + 1
    square = jnp.zeros(shape, F32)
    for a in range(ITERS):
        square = square + (solved[a][0] ** 2 + solved[a][1] ** 2) * entry(offset + a, offset + a)[0]
        for b in range(a + 1, ITERS):
            pair = cmul(conj(solved[a]), solved[b])
            square = square + 2.0 * cmul(pair, entry(offset + a, offset + b))[0]

    projections = []
    for block in range(2):
        base = block * width
        value = None
        for a in range(ITERS):
            term = cmul(solved[a], (column(base + offset + a), column(base + count + offset + a)))
            value = term if value is None else cadd(value, term)
        projections.append(scale(value, 1.0 / total_rows))
    value = None
    for a in range(ITERS):
        term = cmul(solved[a], entry(count - 1, offset + a))
        value = term if value is None else cadd(value, term)
    extra = scale(value, 1.0 / total_rows)

    row, lane = iota(shape, 0), iota(shape, 1)
    first = 3 * width
    span = 4 * count
    first_row = jnp.zeros(shape, F32)
    second_row = jnp.zeros(shape, F32)
    for block in range(2):
        real, imag = projections[block]
        at_real = (lane == first + block * count + row) | (lane == first + span + block * count + row)
        at_imag = (lane == first + 2 * count + block * count + row) | (
            lane == first + span + 2 * count + block * count + row
        )
        first_row = first_row + jnp.where(at_real, real, jnp.where(at_imag, -imag, 0.0))
        second_row = second_row + jnp.where(at_real, imag, jnp.where(at_imag, real, 0.0))
    first_row = jnp.sum(first_row, axis=0, keepdims=True)
    second_row = jnp.sum(second_row, axis=0, keepdims=True)
    upper = lane < first + span
    real_col = jnp.where(upper, projections[0][0], projections[1][0])
    imag_col = jnp.where(upper, projections[0][1], projections[1][1])
    quad = jnp.sum(inner * (real_col * first_row + imag_col * second_row), axis=1, keepdims=True)
    quad = jnp.broadcast_to(quad, shape)
    for block in range(2):
        base = block * width
        real, imag = projections[block]
        cross = cmul(
            cmul((real, -imag), extra), (column(base + count - 1), column(base + width - 1))
        )[0]
        quad = quad + 2.0 * cross - 2.0 * total_rows * (real * real + imag * imag)
    quad = jnp.broadcast_to(jnp.sum(quad, axis=0, keepdims=True), shape)
    extra_size = extra[0] * extra[0] + extra[1] * extra[1]
    quad = quad + extra_size * (entry(count - 1, count - 1)[0] - 2.0 * total_rows)
    norm = jnp.sqrt((square + quad) * (1.0 / total_rows) + EPSILON)

    coef = tuple(
        jnp.concatenate([projections[0][part], projections[1][part]], axis=0) for part in range(2)
    )
    mixed = cadd(mix_basis(coef, basis_ref), cmul(extra, previous))
    made = None
    for a in range(ITERS):
        term = cmul(solved[a], images[a])
        made = term if made is None else cadd(made, term)
    remain = csub(made, mixed)
    latest = (remain[0] / norm, remain[1] / norm)

    rows = []
    for part in range(2):
        spread = jnp.zeros(shape, F32)
        for block in range(2):
            spread = spread + jnp.where(lane == block * count + row, projections[block][part], 0.0)
        spread = jnp.sum(spread, axis=0, keepdims=True)
        spread = spread + jnp.where(lane[:1] == 2 * count, extra[part][:1], 0.0)
        if part == 0:
            spread = spread + jnp.where(lane[:1] == 2 * count + 1, norm[:1], 0.0)
        rows.append(spread)
    return latest, jnp.concatenate(rows, axis=0)


def reduce_sums(sums_ref):
    if sums_ref.shape[0] <= 64:
        values = [sums_ref[k] for k in range(sums_ref.shape[0])]
        while len(values) > 1:
            values = [
                values[k] + values[k + 1] if k + 1 < len(values) else values[k]
                for k in range(0, len(values), 2)
            ]
        return values[0]
    return jnp.sum(sums_ref[...], axis=0)


def between_kernel(
    total_rows, step, sums_ref, basis_ref, compact_ref, weights_ref, fresh_ref, p_high, p_low,
    *refs,
):
    images = [load(ref) for ref in refs[:ITERS]]
    previous_ref = refs[ITERS]
    (right_ref, image_ref, first_ref, second_ref, latest_ref, coeffs_ref, inner_ref, wide_ref) = refs[
        ITERS + 1 :
    ]
    sums = reduce_sums(sums_ref)
    inner_ref[...] = sums
    latest, coeffs = settle(total_rows, sums, sums, basis_ref, images, load(previous_ref))
    save(latest_ref, latest)
    coeffs_ref[...] = coeffs
    coef, gamma = coefficients(step + 1, compact_ref, weights_ref, fresh_ref)
    right = cadd(mix_basis(coef, basis_ref), cmul(gamma, latest))
    save(right_ref, right)
    image = precondition(right, p_high, p_low, wide_ref)
    save(image_ref, image)
    send(image, first_ref, second_ref)


def finish_kernel(total_rows, sums_ref, inner_ref, basis_ref, *refs):
    images = [load(ref) for ref in refs[:ITERS]]
    previous_ref, before_ref, made_ref, listed_ref = refs[ITERS:]
    sums = reduce_sums(sums_ref)
    previous = load(previous_ref)
    latest, coeffs = settle(total_rows, sums, inner_ref[...], basis_ref, images, previous)
    for step, vector in enumerate((previous, latest)):
        for part in range(2):
            for tile in range(vector[part].shape[0]):
                made_ref[step, part : part + 1, tile * LANES : (tile + 1) * LANES] = vector[part][
                    tile : tile + 1
                ]
    width = listed_ref.shape[2]
    listed_ref[0] = before_ref[:, :width]
    listed_ref[1] = coeffs[:, :width]


def vmem():
    return pl.BlockSpec(memory_space=pltpu.VMEM)


def smem():
    return pl.BlockSpec(memory_space=pltpu.SMEM)


def call(kernel, name, out_shape, in_specs, scratch, args, flops=10**7):
    return pl.pallas_call(
        kernel,
        name=name,
        out_shape=out_shape,
        in_specs=in_specs,
        out_specs=jax.tree.map(lambda _: vmem(), out_shape),
        scratch_shapes=scratch,
        cost_estimate=pl.CostEstimate(flops=flops, bytes_accessed=10**6, transcendentals=0),
    )(*args)


def local(
    n_dom,
    n_sub,
    basis,
    compact,
    weights,
    fresh,
    shifts,
    k_tiles,
    pattern,
    mass,
    precond,
    c_tiles,
    c_rows,
    c_side,
    c_count,
):
    tiles, slots_k, tile = k_tiles.shape[0], k_tiles.shape[1], k_tiles.shape[2]
    slots = c_tiles.shape[0]
    devices = n_dom * n_sub
    total_rows = float(tiles * tile * devices)
    steps = weights.shape[0]
    vec = jax.ShapeDtypeStruct((2 * tiles, tile), F32)
    edge = jax.ShapeDtypeStruct((2, tile), F32)
    square = jax.ShapeDtypeStruct((tiles, tile), F32)
    k_blocks = tiles * slots_k + slots
    p_blocks = 2 * tiles
    k_part = jax.ShapeDtypeStruct((tile, k_blocks * tile), BF16)
    p_part = jax.ShapeDtypeStruct((tile, p_blocks * tile), BF16)
    mask = jax.ShapeDtypeStruct((slots, tiles, tile), F32)
    pick = jax.ShapeDtypeStruct(((slots_k - 1) * tiles, tiles * n_sub), BF16)
    wide = pltpu.VMEM((4 * tiles, max(k_blocks, p_blocks) * tile), BF16)
    mass = mass.reshape(tiles, tile)
    zero = jnp.zeros((2 * tiles, tile), F32)

    even_swap = [(i, i ^ 1) for i in range(n_dom)]
    odd_swap = [(i, (i + 1 if i % 2 else i - 1) % n_dom) for i in range(n_dom)]

    def exchange(image, first, second):
        second = lax.ppermute(second, "dom", odd_swap)
        first = lax.ppermute(first, "dom", even_swap)
        blocks = [
            lax.ppermute(image, "sub", [(i, i ^ k) for i in range(n_sub)]) for k in range(1, n_sub)
        ]
        return blocks, first, second

    right, image, first, second, p_high, p_low = call(
        start_kernel, "start", (vec, vec, edge, edge, p_part, p_part), [vmem()] * 5, [wide],
        (basis, compact, weights, fresh, precond),
    )
    k_high, k_low, pick_table, below, above, inner = call(
        functools.partial(prepare_kernel, n_dom), "prepare",
        (k_part, k_part, pick, mask, mask, square), [smem()] * 4 + [vmem()] * 3, [],
        (pattern, c_rows, c_side, c_count, basis, k_tiles, c_tiles),
    )
    others = n_sub - 1
    previous = zero
    for step in range(steps):
        term = right
        images, results = [image], []
        for index in range(ITERS):
            blocks, first_in, second_in = exchange(images[-1], first, second)
            common = (
                images[-1], term, *blocks, first_in, second_in, shifts, mass, k_high, k_low,
                pick_table, below, above,
            )
            specs = [vmem()] * (4 + others) + [smem()] + [vmem()] * 6
            if index + 1 < ITERS:
                result, term, image, first, second = call(
                    functools.partial(level_kernel, step, others), "level",
                    (vec, vec, vec, edge, edge), specs + [vmem()] * 2, [wide],
                    common + (p_high, p_low),
                )
                results.append(result)
                images.append(image)
            else:
                earlier = (*results, right, *images[:-1])
                payload = call(
                    functools.partial(last_kernel, step, others), "last",
                    jax.ShapeDtypeStruct((devices, tiles, tile), F32),
                    specs + [vmem()] * (3 + len(earlier)),
                    [wide, pltpu.VMEM((tiles, 4 * (2 * ITERS + 2), tile), F32)],
                    common + (basis, previous, inner, *earlier),
                )
        sums = lax.all_to_all(payload, AXES, 0, 0)
        if step + 1 < steps:
            right, image, first, second, previous_next, coeffs, inner_sum = call(
                functools.partial(between_kernel, total_rows, step), "between",
                (vec, vec, edge, edge, vec, jax.ShapeDtypeStruct((2, tile), F32), square),
                [vmem()] * (8 + ITERS), [wide],
                (sums, basis, compact, weights, fresh, p_high, p_low, *images, previous),
            )
            previous = previous_next
        else:
            width = basis.shape[1] + 2
            made, listed = call(
                functools.partial(finish_kernel, total_rows), "finish",
                (
                    jax.ShapeDtypeStruct((steps, 2, tiles * tile), F32),
                    jax.ShapeDtypeStruct((steps, 2, width), F32),
                ),
                [vmem()] * (5 + ITERS), [],
                (sums, inner_sum, basis, *images, previous, coeffs),
            )
    return made, listed


def solution(mesh):
    placed = (
        P(None, None, AXES),
        P(),
        P(),
        P(),
        P(),
        P(AXES, None, None, None),
        P(AXES, None),
        P(AXES),
        P(AXES, None, None, None),
        P(AXES, None, None),
        P(AXES),
        P(AXES),
        P(AXES),
    )
    return jax.shard_map(
        functools.partial(local, mesh.shape["dom"], mesh.shape["sub"]),
        mesh=mesh,
        in_specs=placed,
        out_specs=(P(None, None, AXES), P()),
        check_vma=False,
    )
```

profile of v0, /device:TPU:0, one launch (start us, length us, event | category | flops | bytes accessed | tf_op | source)
XLA Modules:
  0.0 119.7 jit_solution(15203026415739007834)
XLA Ops:
  2.0 2.9 %start.1 = (f32[16,128]{1,0:T(8,128)}, f32[16,128]{1,0:T(8,128)}, f32[2,128]{1,0:T(2,128)}, f32[2,128]{1,0:T(2,128)}, bf16[128,2048]{1,0:T(8,128)(2,1)}, /*index=5*/bf16[128,2048]{1,0:T(8,128)(2,1)}) custom-call(f32[2,16,1024]{2,1,0:T(8,128)} %basis_ref.7, f32[2,32,16]{2,1,0:T(8,128)} %copy.15.compact_ref, f32[2,2,32]{2,1,0:T(2,128)} %weights_ref.3, ...), custom_call_target="tpu_custom_call" | custom-call | flops 10000000 | bytes 1000000 | tf_op jit(solution)/shard_map/start/pallas_call | solution.py:500
  4.9 2.4 %collective-permute-start.2 = (f32[16,128]{1,0:T(8,128)}, f32[16,128]{1,0:T(8,128)S(1)}, u32[]{:S(2)}, u32[]{:S(2)}) collective-permute-start(f32[16,128]{1,0:T(8,128)} %get-tuple-element.41.image_ref.refs_18_.refs_0_), channel_id=1, source_target_pairs={{0,3},{1,2},{2,1},{3,0},{4,7},{5,6},{6,5},{7,4},{8,11},{9,10},{10,... | collective-permute-start | bytes 24584 | tf_op jit(solution)/shard_map/ppermute | solution.py:553
  9.8 3.5 %collective-permute-start.4 = (f32[2,128]{1,0:T(2,128)}, f32[2,128]{1,0:T(2,128)S(1)}, u32[]{:S(2)}, u32[]{:S(2)}) collective-permute-start(f32[2,128]{1,0:T(2,128)} %get-tuple-element.44), channel_id=1, source_target_pairs={{0,28},{4,8},{8,4},{12,16},{16,12},{20,24},{24,20},{28,0},{1,29},{... | collective-permute-start | bytes 3080 | tf_op jit(solution)/shard_map/ppermute | solution.py:550
  15.3 3.6 %prepare.1 = (bf16[128,4096]{1,0:T(8,128)(2,1)}, bf16[128,4096]{1,0:T(8,128)(2,1)}, bf16[16,32]{1,0:T(8,128)(2,1)}, f32[8,8,128]{2,1,0:T(8,128)}, f32[8,8,128]{2,1,0:T(8,128)}, /*index=5*/f32[8,128]{1,0:T(8,128)}) custom-call(s32[8,2]{1,0:T(8,128)} %copy.16.pattern_ref, s32[8]{0:T(128)} %rows_ref.1, s32[8]{0:T(128)} %side_ref.1, s32[1]{0:T(128)S(6)} %copy.18.count_ref, ...), custom_call_target="tpu_custom_call" | custom-call | flops 10000000 | bytes 1000000 | tf_op jit(solution)/shard_map/prepare/pallas_call | solution.py:500
  19.7 4.4 %level.4 = (f32[16,128]{1,0:T(8,128)}, f32[16,128]{1,0:T(8,128)}, f32[16,128]{1,0:T(8,128)}, f32[2,128]{1,0:T(2,128)}, f32[2,128]{1,0:T(2,128)}) custom-call(f32[16,128]{1,0:T(8,128)} %get-tuple-element.41.image_ref.refs_18_.refs_0_, f32[16,128]{1,0:T(8,128)} %get-tuple-element.42.term_ref.refs_17_, f32[16,128]{1,0:T(8,128)} %copy-done.3, ...), custom_call_target="tpu_custom_call" | custom-call | flops 10000000 | bytes 1000000 | tf_op jit(solution)/shard_map/level/pallas_call | solution.py:500
  25.9 1.9 %collective-permute-start.9 = (f32[2,128]{1,0:T(2,128)}, f32[2,128]{1,0:T(2,128)S(1)}, u32[]{:S(2)}, u32[]{:S(2)}) collective-permute-start(f32[2,128]{1,0:T(2,128)} %get-tuple-element.55), channel_id=1, source_target_pairs={{0,28},{4,8},{8,4},{12,16},{16,12},{20,24},{24,20},{28,0},{1,29},{... | collective-permute-start | bytes 3080 | tf_op jit(solution)/shard_map/ppermute | solution.py:550
  27.9 1.9 %collective-permute-done.8.refs_3_ = f32[2,128]{1,0:T(2,128)S(1)} collective-permute-done((f32[2,128]{1,0:T(2,128)}, f32[2,128]{1,0:T(2,128)S(1)}, u32[]{:S(2)}, u32[]{:S(2)}) %collective-permute-start.8) | collective-permute-done | bytes 1056 | tf_op jit(solution)/shard_map/ppermute | solution.py:551
  29.7 2.7 %collective-permute-done.9.refs_4_ = f32[2,128]{1,0:T(2,128)S(1)} collective-permute-done((f32[2,128]{1,0:T(2,128)}, f32[2,128]{1,0:T(2,128)S(1)}, u32[]{:S(2)}, u32[]{:S(2)}) %collective-permute-start.9) | collective-permute-done | bytes 1056 | tf_op jit(solution)/shard_map/ppermute | solution.py:550
  33.1 4.4 %level.5 = (f32[16,128]{1,0:T(8,128)}, f32[16,128]{1,0:T(8,128)}, f32[16,128]{1,0:T(8,128)}, f32[2,128]{1,0:T(2,128)}, f32[2,128]{1,0:T(2,128)}) custom-call(f32[16,128]{1,0:T(8,128)} %get-tuple-element.52.image_ref.refs_19_.refs_1_, f32[16,128]{1,0:T(8,128)} %get-tuple-element.53.term_ref, f32[16,128]{1,0:T(8,128)} %copy-done.16, f32[16,128]{1,0:T(8,128)} %copy-done.12, ...), custom_call_target="tpu_custom_call" | custom-call | flops 10000000 | bytes 1000000 | tf_op jit(solution)/shard_map/level/pallas_call | solution.py:500
  43.1 2.9 %collective-permute-done.14.refs_4_ = f32[2,128]{1,0:T(2,128)S(1)} collective-permute-done((f32[2,128]{1,0:T(2,128)}, f32[2,128]{1,0:T(2,128)S(1)}, u32[]{:S(2)}, u32[]{:S(2)}) %collective-permute-start.14) | collective-permute-done | bytes 1056 | tf_op jit(solution)/shard_map/ppermute | solution.py:550
  46.7 4.4 %last.2 = f32[32,8,128]{2,1,0:T(8,128)} custom-call(f32[16,128]{1,0:T(8,128)} %get-tuple-element.56.image_ref.refs_2_, f32[16,128]{1,0:T(8,128)} %get-tuple-element.57.term_ref, f32[16,128]{1,0:T(8,128)} %copy-done.13, f32[16,128]{1,0:T(8,128)} %copy-done.8, f32[16,128]{1,0:T(8,128)} %copy-done.4, f32[2,128]{1,0:T(2,128)} %copy-done.21, ...), custom_call_target="tpu_custom_call" | custom-call | flops 10000000 | bytes 1000000 | tf_op jit(solution)/shard_map/last/pallas_call | solution.py:500
  51.1 11.5 %all_to_all.10.sums_ref = f32[32,8,128]{2,1,0:T(8,128)} all-to-all(f32[32,8,128]{2,1,0:T(8,128)} %last.2), channel_id=1, replica_groups=mesh['dom'=8,'sub'=4] {'dom','sub'}, dimensions={0} | all-to-all | bytes 262144 | tf_op jit(solution)/shard_map/all_to_all | solution.py:595
  62.6 2.7 %between.1 = (f32[16,128]{1,0:T(8,128)}, f32[16,128]{1,0:T(8,128)}, f32[2,128]{1,0:T(2,128)}, f32[2,128]{1,0:T(2,128)}, f32[16,128]{1,0:T(8,128)}, /*index=5*/f32[2,128]{1,0:T(2,128)}, f32[8,128]{1,0:T(8,128)}) custom-call(f32[32,8,128]{2,1,0:T(8,128)} %all_to_all.10.sums_ref, f32[2,16,1024]{2,1,0:T(8,128)} %basis_ref.7, f32[2,32,16]{2,1,0:T(8,128)} %copy.15.compact_ref, ...), custom_call_target="tpu_custom_call" | custom-call | flops 10000000 | bytes 1000000 | tf_op jit(solution)/shard_map/between/pallas_call | solution.py:500
  67.8 2.1 %collective-permute-start.19 = (f32[2,128]{1,0:T(2,128)}, f32[2,128]{1,0:T(2,128)S(1)}, u32[]{:S(2)}, u32[]{:S(2)}) collective-permute-start(f32[2,128]{1,0:T(2,128)} %get-tuple-element.66), channel_id=1, source_target_pairs={{0,28},{4,8},{8,4},{12,16},{16,12},{20,24},{24,20},{28,0},{1,29},{... | collective-permute-start | bytes 3080 | tf_op jit(solution)/shard_map/ppermute | solution.py:550
  71.0 3.4 %collective-permute-done.19.refs_4_ = f32[2,128]{1,0:T(2,128)S(1)} collective-permute-done((f32[2,128]{1,0:T(2,128)}, f32[2,128]{1,0:T(2,128)S(1)}, u32[]{:S(2)}, u32[]{:S(2)}) %collective-permute-start.19) | collective-permute-done | bytes 1056 | tf_op jit(solution)/shard_map/ppermute | solution.py:550
  75.0 4.4 %level.6 = (f32[16,128]{1,0:T(8,128)}, f32[16,128]{1,0:T(8,128)}, f32[16,128]{1,0:T(8,128)}, f32[2,128]{1,0:T(2,128)}, f32[2,128]{1,0:T(2,128)}) custom-call(f32[16,128]{1,0:T(8,128)} %get-tuple-element.63.image_ref.refs_18_.refs_0_, f32[16,128]{1,0:T(8,128)} %get-tuple-element.64.term_ref.refs_17_, f32[16,128]{1,0:T(8,128)} %copy-done.17, ...), custom_call_target="tpu_custom_call" | custom-call | flops 10000000 | bytes 1000000 | tf_op jit(solution)/shard_map/level/pallas_call | solution.py:500
  81.2 2.1 %collective-permute-start.24 = (f32[2,128]{1,0:T(2,128)}, f32[2,128]{1,0:T(2,128)S(1)}, u32[]{:S(2)}, u32[]{:S(2)}) collective-permute-start(f32[2,128]{1,0:T(2,128)} %get-tuple-element.70), channel_id=1, source_target_pairs={{0,28},{4,8},{8,4},{12,16},{16,12},{20,24},{24,20},{28,0},{1,29},{... | collective-permute-start | bytes 3080 | tf_op jit(solution)/shard_map/ppermute | solution.py:550
  85.0 2.7 %collective-permute-done.24.refs_4_ = f32[2,128]{1,0:T(2,128)S(1)} collective-permute-done((f32[2,128]{1,0:T(2,128)}, f32[2,128]{1,0:T(2,128)S(1)}, u32[]{:S(2)}, u32[]{:S(2)}) %collective-permute-start.24) | collective-permute-done | bytes 1056 | tf_op jit(solution)/shard_map/ppermute | solution.py:550
  88.4 4.4 %level.7 = (f32[16,128]{1,0:T(8,128)}, f32[16,128]{1,0:T(8,128)}, f32[16,128]{1,0:T(8,128)}, f32[2,128]{1,0:T(2,128)}, f32[2,128]{1,0:T(2,128)}) custom-call(f32[16,128]{1,0:T(8,128)} %get-tuple-element.67.image_ref.refs_19_.refs_1_, f32[16,128]{1,0:T(8,128)} %get-tuple-element.68.term_ref, f32[16,128]{1,0:T(8,128)} %copy-done.15, f32[16,128]{1,0:T(8,128)} %copy-done.11, ...), custom_call_target="tpu_custom_call" | custom-call | flops 10000000 | bytes 1000000 | tf_op jit(solution)/shard_map/level/pallas_call | solution.py:500
  94.9 2.1 %collective-permute-start.29 = (f32[2,128]{1,0:T(2,128)}, f32[2,128]{1,0:T(2,128)S(1)}, u32[]{:S(2)}, u32[]{:S(2)}) collective-permute-start(f32[2,128]{1,0:T(2,128)} %get-tuple-element.74), channel_id=1, source_target_pairs={{0,28},{4,8},{8,4},{12,16},{16,12},{20,24},{24,20},{28,0},{1,29},{... | collective-permute-start | bytes 3080 | tf_op jit(solution)/shard_map/ppermute | solution.py:550
  98.4 2.9 %collective-permute-done.29.refs_4_ = f32[2,128]{1,0:T(2,128)S(1)} collective-permute-done((f32[2,128]{1,0:T(2,128)}, f32[2,128]{1,0:T(2,128)S(1)}, u32[]{:S(2)}, u32[]{:S(2)}) %collective-permute-start.29) | collective-permute-done | bytes 1056 | tf_op jit(solution)/shard_map/ppermute | solution.py:550
  102.0 4.4 %last.3 = f32[32,8,128]{2,1,0:T(8,128)} custom-call(f32[16,128]{1,0:T(8,128)} %get-tuple-element.71.image_ref.refs_2_, f32[16,128]{1,0:T(8,128)} %get-tuple-element.72.term_ref, f32[16,128]{1,0:T(8,128)} %copy-done.9, f32[16,128]{1,0:T(8,128)} %copy-done.5, f32[16,128]{1,0:T(8,128)} %copy-done.2, f32[2,128]{1,0:T(2,128)} %copy-done.20, f32[2,128]{1,0:T(2,128)} %copy-done.22, ...), custom_call_target="tpu_custom_call" | custom-call | flops 10000000 | bytes 1000000 | tf_op jit(solution)/shard_map/last/pallas_call | solution.py:500
  106.4 11.5 %all_to_all.11.sums_ref = f32[32,8,128]{2,1,0:T(8,128)} all-to-all(f32[32,8,128]{2,1,0:T(8,128)} %last.3), channel_id=1, replica_groups=mesh['dom'=8,'sub'=4] {'dom','sub'}, dimensions={0} | all-to-all | bytes 262144 | tf_op jit(solution)/shard_map/all_to_all | solution.py:595
  117.8 1.9 %finish.1 = (f32[2,2,1024]{2,1,0:T(2,128)}, f32[2,2,18]{2,1,0:T(2,128)}) custom-call(f32[32,8,128]{2,1,0:T(8,128)} %all_to_all.11.sums_ref, f32[8,128]{1,0:T(8,128)} %get-tuple-element.78.inner_ref, f32[2,16,1024]{2,1,0:T(8,128)} %basis_ref.7, f32[16,128]{1,0:T(8,128)} %get-tuple-element.63.image_ref.refs_18_.refs_0_, ...), custom_call_target="tpu_custom_call" | custom-call | flops 10000000 | bytes 1000000 | tf_op jit(solution)/shard_map/finish/pallas_call | solution.py:500
  (111 shorter events, 27.0 us)
Async XLA Ops:
  4.9 14.1 %collective-permute-start.2 = (f32[16,128]{1,0:T(8,128)}, f32[16,128]{1,0:T(8,128)S(1)}, u32[]{:S(2)}, u32[]{:S(2)}) collective-permute-start(f32[16,128]{1,0:T(8,128)} %get-tuple-element.41.image_ref.refs_18_.refs_0_), channel_id=1, source_target_pairs={{0,3},{1,2},{2,1},{3,0},{4,7},{5,6},{6,5},{7,4},{8,11},{9,10},{10,... | collective-permute-start | bytes 24584 | tf_op jit(solution)/shard_map/ppermute | solution.py:553
  7.3 11.7 %collective-permute-start.1 = (f32[16,128]{1,0:T(8,128)}, f32[16,128]{1,0:T(8,128)S(1)}, u32[]{:S(2)}, u32[]{:S(2)}) collective-permute-start(f32[16,128]{1,0:T(8,128)} %get-tuple-element.41.image_ref.refs_18_.refs_0_), channel_id=1, source_target_pairs={{0,2},{1,3},{2,0},{3,1},{4,6},{5,7},{6,4},{7,5},{8,10},{9,11},{10,... | collective-permute-start | bytes 24584 | tf_op jit(solution)/shard_map/ppermute | solution.py:553
  7.9 11.1 %collective-permute-start = (f32[16,128]{1,0:T(8,128)}, f32[16,128]{1,0:T(8,128)S(1)}, u32[]{:S(2)}, u32[]{:S(2)}) collective-permute-start(f32[16,128]{1,0:T(8,128)} %get-tuple-element.41.image_ref.refs_18_.refs_0_), channel_id=1, source_target_pairs={{0,1},{1,0},{2,3},{3,2},{4,5},{5,4},{6,7},{7,6},{8,9},{9,8},{10,11... | collective-permute-start | bytes 24584 | tf_op jit(solution)/shard_map/ppermute | solution.py:553
  8.0 11.0 %collective-permute-start.3 = (f32[2,128]{1,0:T(2,128)}, f32[2,128]{1,0:T(2,128)S(1)}, u32[]{:S(2)}, u32[]{:S(2)}) collective-permute-start(f32[2,128]{1,0:T(2,128)} %get-tuple-element.43), channel_id=1, source_target_pairs={{0,4},{4,0},{8,12},{12,8},{16,20},{20,16},{24,28},{28,24},{1,5},{5... | collective-permute-start | bytes 3080 | tf_op jit(solution)/shard_map/ppermute | solution.py:551
  9.8 9.2 %collective-permute-start.4 = (f32[2,128]{1,0:T(2,128)}, f32[2,128]{1,0:T(2,128)S(1)}, u32[]{:S(2)}, u32[]{:S(2)}) collective-permute-start(f32[2,128]{1,0:T(2,128)} %get-tuple-element.44), channel_id=1, source_target_pairs={{0,28},{4,8},{8,4},{12,16},{16,12},{20,24},{24,20},{28,0},{1,29},{... | collective-permute-start | bytes 3080 | tf_op jit(solution)/shard_map/ppermute | solution.py:550
  24.1 8.4 %collective-permute-start.7 = (f32[16,128]{1,0:T(8,128)}, f32[16,128]{1,0:T(8,128)S(1)}, u32[]{:S(2)}, u32[]{:S(2)}) collective-permute-start(f32[16,128]{1,0:T(8,128)} %get-tuple-element.52.image_ref.refs_19_.refs_1_), channel_id=1, source_target_pairs={{0,3},{1,2},{2,1},{3,0},{4,7},{5,6},{6,5},{7,4},{8,11},{9,10},{10,... | collective-permute-start | bytes 24584 | tf_op jit(solution)/shard_map/ppermute | solution.py:553
  24.7 7.7 %collective-permute-start.6 = (f32[16,128]{1,0:T(8,128)}, f32[16,128]{1,0:T(8,128)S(1)}, u32[]{:S(2)}, u32[]{:S(2)}) collective-permute-start(f32[16,128]{1,0:T(8,128)} %get-tuple-element.52.image_ref.refs_19_.refs_1_), channel_id=1, source_target_pairs={{0,2},{1,3},{2,0},{3,1},{4,6},{5,7},{6,4},{7,5},{8,10},{9,11},{10,... | collective-permute-start | bytes 24584 | tf_op jit(solution)/shard_map/ppermute | solution.py:553
  25.7 6.8 %collective-permute-start.5 = (f32[16,128]{1,0:T(8,128)}, f32[16,128]{1,0:T(8,128)S(1)}, u32[]{:S(2)}, u32[]{:S(2)}) collective-permute-start(f32[16,128]{1,0:T(8,128)} %get-tuple-element.52.image_ref.refs_19_.refs_1_), channel_id=1, source_target_pairs={{0,1},{1,0},{2,3},{3,2},{4,5},{5,4},{6,7},{7,6},{8,9},{9,8},{10,11... | collective-permute-start | bytes 24584 | tf_op jit(solution)/shard_map/ppermute | solution.py:553
  25.9 6.5 %collective-permute-start.9 = (f32[2,128]{1,0:T(2,128)}, f32[2,128]{1,0:T(2,128)S(1)}, u32[]{:S(2)}, u32[]{:S(2)}) collective-permute-start(f32[2,128]{1,0:T(2,128)} %get-tuple-element.55), channel_id=1, source_target_pairs={{0,28},{4,8},{8,4},{12,16},{16,12},{20,24},{24,20},{28,0},{1,29},{... | collective-permute-start | bytes 3080 | tf_op jit(solution)/shard_map/ppermute | solution.py:550
  37.5 8.6 %collective-permute-start.12 = (f32[16,128]{1,0:T(8,128)}, f32[16,128]{1,0:T(8,128)S(1)}, u32[]{:S(2)}, u32[]{:S(2)}) collective-permute-start(f32[16,128]{1,0:T(8,128)} %get-tuple-element.56.image_ref.refs_2_), channel_id=1, source_target_pairs={{0,3},{1,2},{2,1},{3,0},{4,7},{5,6},{6,5},{7,4},{8,11},{9,10},{10,... | collective-permute-start | bytes 24584 | tf_op jit(solution)/shard_map/ppermute | solution.py:553
  37.5 8.6 %collective-permute-start.11 = (f32[16,128]{1,0:T(8,128)}, f32[16,128]{1,0:T(8,128)S(1)}, u32[]{:S(2)}, u32[]{:S(2)}) collective-permute-start(f32[16,128]{1,0:T(8,128)} %get-tuple-element.56.image_ref.refs_2_), channel_id=1, source_target_pairs={{0,2},{1,3},{2,0},{3,1},{4,6},{5,7},{6,4},{7,5},{8,10},{9,11},{10,... | collective-permute-start | bytes 24584 | tf_op jit(solution)/shard_map/ppermute | solution.py:553
  39.1 7.0 %collective-permute-start.10 = (f32[16,128]{1,0:T(8,128)}, f32[16,128]{1,0:T(8,128)S(1)}, u32[]{:S(2)}, u32[]{:S(2)}) collective-permute-start(f32[16,128]{1,0:T(8,128)} %get-tuple-element.56.image_ref.refs_2_), channel_id=1, source_target_pairs={{0,1},{1,0},{2,3},{3,2},{4,5},{5,4},{6,7},{7,6},{8,9},{9,8},{10,11... | collective-permute-start | bytes 24584 | tf_op jit(solution)/shard_map/ppermute | solution.py:553
  39.6 6.5 %collective-permute-start.14 = (f32[2,128]{1,0:T(2,128)}, f32[2,128]{1,0:T(2,128)S(1)}, u32[]{:S(2)}, u32[]{:S(2)}) collective-permute-start(f32[2,128]{1,0:T(2,128)} %get-tuple-element.59), channel_id=1, source_target_pairs={{0,28},{4,8},{8,4},{12,16},{16,12},{20,24},{24,20},{28,0},{1,29},{... | collective-permute-start | bytes 3080 | tf_op jit(solution)/shard_map/ppermute | solution.py:550
  65.3 9.0 %collective-permute-start.17 = (f32[16,128]{1,0:T(8,128)}, f32[16,128]{1,0:T(8,128)S(1)}, u32[]{:S(2)}, u32[]{:S(2)}) collective-permute-start(f32[16,128]{1,0:T(8,128)} %get-tuple-element.63.image_ref.refs_18_.refs_0_), channel_id=1, source_target_pairs={{0,3},{1,2},{2,1},{3,0},{4,7},{5,6},{6,5},{7,4},{8,11},{9,10},{10,... | collective-permute-start | bytes 24584 | tf_op jit(solution)/shard_map/ppermute | solution.py:553
  65.5 8.9 %collective-permute-start.16 = (f32[16,128]{1,0:T(8,128)}, f32[16,128]{1,0:T(8,128)S(1)}, u32[]{:S(2)}, u32[]{:S(2)}) collective-permute-start(f32[16,128]{1,0:T(8,128)} %get-tuple-element.63.image_ref.refs_18_.refs_0_), channel_id=1, source_target_pairs={{0,2},{1,3},{2,0},{3,1},{4,6},{5,7},{6,4},{7,5},{8,10},{9,11},{10,... | collective-permute-start | bytes 24584 | tf_op jit(solution)/shard_map/ppermute | solution.py:553
  67.2 7.2 %collective-permute-start.15 = (f32[16,128]{1,0:T(8,128)}, f32[16,128]{1,0:T(8,128)S(1)}, u32[]{:S(2)}, u32[]{:S(2)}) collective-permute-start(f32[16,128]{1,0:T(8,128)} %get-tuple-element.63.image_ref.refs_18_.refs_0_), channel_id=1, source_target_pairs={{0,1},{1,0},{2,3},{3,2},{4,5},{5,4},{6,7},{7,6},{8,9},{9,8},{10,11... | collective-permute-start | bytes 24584 | tf_op jit(solution)/shard_map/ppermute | solution.py:553
  67.8 6.5 %collective-permute-start.19 = (f32[2,128]{1,0:T(2,128)}, f32[2,128]{1,0:T(2,128)S(1)}, u32[]{:S(2)}, u32[]{:S(2)}) collective-permute-start(f32[2,128]{1,0:T(2,128)} %get-tuple-element.66), channel_id=1, source_target_pairs={{0,28},{4,8},{8,4},{12,16},{16,12},{20,24},{24,20},{28,0},{1,29},{... | collective-permute-start | bytes 3080 | tf_op jit(solution)/shard_map/ppermute | solution.py:550
  79.4 8.4 %collective-permute-start.22 = (f32[16,128]{1,0:T(8,128)}, f32[16,128]{1,0:T(8,128)S(1)}, u32[]{:S(2)}, u32[]{:S(2)}) collective-permute-start(f32[16,128]{1,0:T(8,128)} %get-tuple-element.67.image_ref.refs_19_.refs_1_), channel_id=1, source_target_pairs={{0,3},{1,2},{2,1},{3,0},{4,7},{5,6},{6,5},{7,4},{8,11},{9,10},{10,... | collective-permute-start | bytes 24584 | tf_op jit(solution)/shard_map/ppermute | solution.py:553
  79.4 8.3 %collective-permute-start.21 = (f32[16,128]{1,0:T(8,128)}, f32[16,128]{1,0:T(8,128)S(1)}, u32[]{:S(2)}, u32[]{:S(2)}) collective-permute-start(f32[16,128]{1,0:T(8,128)} %get-tuple-element.67.image_ref.refs_19_.refs_1_), channel_id=1, source_target_pairs={{0,2},{1,3},{2,0},{3,1},{4,6},{5,7},{6,4},{7,5},{8,10},{9,11},{10,... | collective-permute-start | bytes 24584 | tf_op jit(solution)/shard_map/ppermute | solution.py:553
  80.2 7.5 %collective-permute-start.20 = (f32[16,128]{1,0:T(8,128)}, f32[16,128]{1,0:T(8,128)S(1)}, u32[]{:S(2)}, u32[]{:S(2)}) collective-permute-start(f32[16,128]{1,0:T(8,128)} %get-tuple-element.67.image_ref.refs_19_.refs_1_), channel_id=1, source_target_pairs={{0,1},{1,0},{2,3},{3,2},{4,5},{5,4},{6,7},{7,6},{8,9},{9,8},{10,11... | collective-permute-start | bytes 24584 | tf_op jit(solution)/shard_map/ppermute | solution.py:553
  81.2 6.5 %collective-permute-start.24 = (f32[2,128]{1,0:T(2,128)}, f32[2,128]{1,0:T(2,128)S(1)}, u32[]{:S(2)}, u32[]{:S(2)}) collective-permute-start(f32[2,128]{1,0:T(2,128)} %get-tuple-element.70), channel_id=1, source_target_pairs={{0,28},{4,8},{8,4},{12,16},{16,12},{20,24},{24,20},{28,0},{1,29},{... | collective-permute-start | bytes 3080 | tf_op jit(solution)/shard_map/ppermute | solution.py:550
  92.8 8.6 %collective-permute-start.27 = (f32[16,128]{1,0:T(8,128)}, f32[16,128]{1,0:T(8,128)S(1)}, u32[]{:S(2)}, u32[]{:S(2)}) collective-permute-start(f32[16,128]{1,0:T(8,128)} %get-tuple-element.71.image_ref.refs_2_), channel_id=1, source_target_pairs={{0,3},{1,2},{2,1},{3,0},{4,7},{5,6},{6,5},{7,4},{8,11},{9,10},{10,... | collective-permute-start | bytes 24584 | tf_op jit(solution)/shard_map/ppermute | solution.py:553
  92.8 8.6 %collective-permute-start.26 = (f32[16,128]{1,0:T(8,128)}, f32[16,128]{1,0:T(8,128)S(1)}, u32[]{:S(2)}, u32[]{:S(2)}) collective-permute-start(f32[16,128]{1,0:T(8,128)} %get-tuple-element.71.image_ref.refs_2_), channel_id=1, source_target_pairs={{0,2},{1,3},{2,0},{3,1},{4,6},{5,7},{6,4},{7,5},{8,10},{9,11},{10,... | collective-permute-start | bytes 24584 | tf_op jit(solution)/shard_map/ppermute | solution.py:553
  93.6 7.7 %collective-permute-start.25 = (f32[16,128]{1,0:T(8,128)}, f32[16,128]{1,0:T(8,128)S(1)}, u32[]{:S(2)}, u32[]{:S(2)}) collective-permute-start(f32[16,128]{1,0:T(8,128)} %get-tuple-element.71.image_ref.refs_2_), channel_id=1, source_target_pairs={{0,1},{1,0},{2,3},{3,2},{4,5},{5,4},{6,7},{7,6},{8,9},{9,8},{10,11... | collective-permute-start | bytes 24584 | tf_op jit(solution)/shard_map/ppermute | solution.py:553
  (36 other events, 55.7 us)
where the time goes:
time: 120 us
  Pallas kernels  37.7 us (31%)
  starting transfers between devices  28.6 us (24%)
  blocking collectives  22.9 us (19%)
  waiting for transfers between devices  22.7 us (19%)
  local copies, waits for them, and re-layouts  6.29 us (5%)
  between operations  1.6 us (1%)
    pallas_call x10, Pallas kernels, call(): pl.pallas_call(kernel, name=name, out_shape=out_shape, in_specs=in_specs,...  37.7 us
    all_to_all x2, blocking collectives, local(): sums = lax.all_to_all(payload, AXES, 0, 0)  22.9 us
    ppermute x6, waiting for transfers between devices, exchange(): second = lax.ppermute(second, 'dom', odd_swap)  14.6 us
    ppermute x6, starting transfers between devices, exchange(): second = lax.ppermute(second, 'dom', odd_swap)  13.3 us
    ppermute x18, starting transfers between devices, exchange(): lax.ppermute(image, 'sub', [(i, i ^ k) for i in range(n_sub)])  12.4 us
    ppermute x6, waiting for transfers between devices, exchange(): first = lax.ppermute(first, 'dom', even_swap)  8.01 us
    unnamed x62, local copies, waits for them, and re-layouts  5.7 us
    ppermute x6, starting transfers between devices, exchange(): first = lax.ppermute(first, 'dom', even_swap)  2.9 us
  transfers between devices with their start and end apart: 30, of which 10 were waited for; matrix products, arithmetic and copies ran while one was open for 1% of the time, Pallas kernels for 3%

commit v1 on v0

--- a/solution.py
+++ b/solution.py
@@ -13,6 +13,7 @@
 BF16 = jnp.bfloat16
 NT_DIMS = (((1,), (1,)), ((), ()))
 LANES = 128
+VMEM_LIMIT = 12 * 1024 * 1024
 AXES = ("dom", "sub")
 
 
@@ -125,61 +126,103 @@
 
 def coefficients(step, compact_ref, weights_ref, fresh_ref):
     beta = weights_ref[step]
-    part_real = lax.dot_general(
-        beta, compact_ref[0], (((1,), (0,)), ((), ())), precision=HIGH, preferred_element_type=F32
-    )
-    part_imag = lax.dot_general(
-        beta, compact_ref[1], (((1,), (0,)), ((), ())), precision=HIGH, preferred_element_type=F32
-    )
-    row_real = part_real[0:1] - part_imag[1:2]
-    row_imag = part_imag[0:1] + part_real[1:2]
-    count = compact_ref.shape[2]
-    same = iota((count, count), 0) == iota((count, count), 1)
-    coef_real = jnp.sum(jnp.where(same, row_real, 0.0), axis=1, keepdims=True)
-    coef_imag = jnp.sum(jnp.where(same, row_imag, 0.0), axis=1, keepdims=True)
+    beta_real, beta_imag = beta[0:1], beta[1:2]
+    compact_real, compact_imag = compact_ref[0], compact_ref[1]
+    coef_real = jnp.sum(compact_real * beta_real - compact_imag * beta_imag, axis=1, keepdims=True)
+    coef_imag = jnp.sum(compact_imag * beta_real + compact_real * beta_imag, axis=1, keepdims=True)
     fresh = fresh_ref[...]
-    gamma_real = jnp.sum(beta[0:1] * fresh[0:1] - beta[1:2] * fresh[1:2], axis=1, keepdims=True)
-    gamma_imag = jnp.sum(beta[0:1] * fresh[1:2] + beta[1:2] * fresh[0:1], axis=1, keepdims=True)
+    gamma_real = jnp.sum(beta_real * fresh[0:1] - beta_imag * fresh[1:2], axis=1, keepdims=True)
+    gamma_imag = jnp.sum(beta_real * fresh[1:2] + beta_imag * fresh[0:1], axis=1, keepdims=True)
     return (coef_real, coef_imag), (gamma_real, gamma_imag)
 
 
 def start_kernel(
-    basis_ref, compact_ref, weights_ref, fresh_ref, precond_ref,
+    basis_in, compact_in, weights_in, fresh_in, precond_in,
     right_ref, image_ref, first_ref, second_ref, high_ref, low_ref,
-    wide_ref,
+    basis_ref, compact_ref, weights_ref, fresh_ref,
+    wide_ref, precond_ref, small_sem, tile_sem,
 ):
-    for tile in range(precond_ref.shape[0]):
-        for part in range(2):
-            store_parts(high_ref, low_ref, 2 * tile + part, precond_ref[tile, part])
+    moves = [
+        pltpu.make_async_copy(source, target, small_sem.at[index])
+        for index, (source, target) in enumerate(
+            (
+                (compact_in, compact_ref),
+                (weights_in, weights_ref),
+                (fresh_in, fresh_ref),
+                (basis_in, basis_ref),
+            )
+        )
+    ]
+    for move in moves:
+        move.start()
+    tiles = precond_in.shape[0]
+    tile_moves = [
+        pltpu.make_async_copy(precond_in.at[tile], precond_ref.at[tile], tile_sem.at[tile])
+        for tile in range(tiles)
+    ]
+    for move in tile_moves:
+        move.start()
+    for move in moves:
+        move.wait()
     coef, _ = coefficients(0, compact_ref, weights_ref, fresh_ref)
     right = mix_basis(coef, basis_ref)
     save(right_ref, right)
+    for tile in range(tiles):
+        tile_moves[tile].wait()
+        for part in range(2):
+            store_parts(high_ref, low_ref, 2 * tile + part, precond_ref[tile, part])
     image = precondition(right, high_ref, low_ref, wide_ref)
     save(image_ref, image)
     send(image, first_ref, second_ref)
 
 
 def prepare_kernel(
-    n_dom, pattern_ref, rows_ref, side_ref, count_ref, basis_ref, k_ref, c_ref,
-    high_ref, low_ref, pick_ref, below_ref, above_ref, inner_ref,
+    n_dom, pattern_in, rows_in, side_in, count_ref, shifts_in, mass_in, k_in, c_in, basis_ref,
+    high_ref, low_ref, c_high_ref, c_low_ref, pick_ref, below_ref, above_ref, inner_ref, drag_ref,
+    k_ref, c_ref, mass_ref, pattern_ref, rows_ref, side_ref, shifts_ref,
+    small_sem, k_sem,
 ):
-    tiles, slots_k = k_ref.shape[0], k_ref.shape[1]
-    for tile in range(tiles):
-        for slot in range(slots_k):
-            store_parts(high_ref, low_ref, tile * slots_k + slot, k_ref[tile, slot])
-    slots = c_ref.shape[0]
-    for slot in range(slots):
-        store_parts(high_ref, low_ref, tiles * slots_k + slot, c_ref[slot])
+    moves = [
+        pltpu.make_async_copy(source, target, small_sem.at[index])
+        for index, (source, target) in enumerate(
+            (
+                (pattern_in, pattern_ref),
+                (rows_in, rows_ref),
+                (side_in, side_ref),
+                (shifts_in, shifts_ref),
+                (mass_in, mass_ref),
+                (c_in, c_ref),
+            )
+        )
+    ]
+    for move in moves:
+        move.start()
+    tiles, slots_k = k_in.shape[0], k_in.shape[1]
+    k_moves = [
+        pltpu.make_async_copy(k_in.at[tile], k_ref.at[tile], k_sem.at[tile]) for tile in range(tiles)
+    ]
+    for move in k_moves:
+        move.start()
+    real, imag = basis_ref[0], basis_ref[1]
+    inner = nt_dot(real, jnp.concatenate([real, imag], axis=0), HIGH)
+    inner = inner + nt_dot(imag, jnp.concatenate([imag, -real], axis=0), HIGH)
+    inner_ref[...] = jnp.zeros(inner_ref.shape, F32)
+    half, wide = inner_ref.shape[0], inner.shape[1]
+    inner_ref[:, 6 * half : 6 * half + wide] = inner[:half]
+    inner_ref[:, 6 * half + wide : 6 * half + 2 * wide] = inner[half:]
+    for move in moves:
+        move.wait()
     mine = lax.axis_index("sub") * tiles
     row, lane = iota(pick_ref.shape, 0), iota(pick_ref.shape, 1)
     picked = jnp.zeros(pick_ref.shape, F32)
     for slot in range(slots_k - 1):
         for tile in range(tiles):
-            column = pattern_ref[tile, slot] ^ mine
+            column = pattern_ref[slot, tile] ^ mine
             picked = jnp.where((row == slot * tiles + tile) & (lane == column), 1.0, picked)
     pick_ref[...] = picked.astype(BF16)
     domain = lax.axis_index("dom")
     row = iota((tiles, LANES), 0)
+    slots = c_ref.shape[0]
     for slot in range(slots):
         live = slot < count_ref[0]
         side = side_ref[slot]
@@ -188,19 +231,20 @@
         high_on = live & (side != 0) & (domain < n_dom - 1)
         below_ref[slot] = jnp.where(here & low_on, 1.0, 0.0)
         above_ref[slot] = jnp.where(here & high_on, 1.0, 0.0)
-    real, imag = basis_ref[0], basis_ref[1]
-    inner = nt_dot(real, jnp.concatenate([real, imag], axis=0), HIGH)
-    inner = inner + nt_dot(imag, jnp.concatenate([imag, -real], axis=0), HIGH)
-    inner_ref[...] = jnp.zeros(inner_ref.shape, F32)
-    half, wide = inner_ref.shape[0], inner.shape[1]
-    inner_ref[:, 6 * half : 6 * half + wide] = inner[:half]
-    inner_ref[:, 6 * half + wide : 6 * half + 2 * wide] = inner[half:]
-
-
-def operate(
-    step, image_ref, blocks, first_ref, second_ref, shifts_ref, mass_ref,
-    high_ref, low_ref, pick_ref, below_ref, above_ref, wide_ref,
-):
+    mass = mass_ref[...]
+    for step in range(drag_ref.shape[0]):
+        for part in range(2):
+            drag_ref[step, part] = mass * shifts_ref[step, part]
+    for slot in range(slots):
+        store_parts(c_high_ref, c_low_ref, slot, c_ref[slot])
+    for tile in range(tiles):
+        k_moves[tile].wait()
+        for slot in range(slots_k):
+            store_parts(high_ref, low_ref, tile * slots_k + slot, k_ref[tile, slot])
+
+
+def stiff_kernel(step, image_ref, *refs):
+    blocks, (drag_ref, high_ref, low_ref, pick_ref, result_ref, wide_ref) = refs[:-6], refs[-6:]
     image = load(image_ref)
     tiles = image[0].shape[0]
     own = parts_of(image)
@@ -225,6 +269,12 @@
                     for part in range(4)
                 ],
             )
+    stiff = product(high_ref, low_ref, wide_ref, tiles * (others + 1))
+    drag = cmul((drag_ref[step, 0], drag_ref[step, 1]), image)
+    save(result_ref, csub(stiff, drag))
+
+
+def couple(partial_ref, first_ref, second_ref, high_ref, low_ref, below_ref, above_ref, wide_ref):
     even = lax.rem(lax.axis_index("dom"), 2) == 0
     first, second = first_ref[...], second_ref[...]
     below = jnp.where(even, second, first)
@@ -232,32 +282,18 @@
     below = parts_of((below[0:1], below[1:2]))
     above = parts_of((above[0:1], above[1:2]))
     slots = below_ref.shape[0]
-    base = tiles * (others + 1)
     for slot in range(slots):
         low_mask, high_mask = below_ref[slot], above_ref[slot]
-        put(
-            wide_ref,
-            base + slot,
-            [low_mask * below[part] + high_mask * above[part] for part in range(4)],
-        )
-    stiff = product(high_ref, low_ref, wide_ref, base + slots)
-    mass = mass_ref[...]
-    moved = (mass * image[0], mass * image[1])
-    shift_real, shift_imag = shifts_ref[step, 0], shifts_ref[step, 1]
-    real = stiff[0] - (shift_real * moved[0] - shift_imag * moved[1])
-    imag = stiff[1] - (shift_real * moved[1] + shift_imag * moved[0])
-    return real, imag
-
-
-def level_kernel(step, others, image_ref, term_ref, *refs):
-    blocks, refs = refs[:others], refs[others:]
-    (
-        first_in, second_in, shifts_ref, mass_ref, k_high, k_low, pick_ref, below_ref, above_ref,
-        p_high, p_low, result_ref, next_ref, out_ref, first_ref, second_ref, wide_ref,
-    ) = refs
-    result = operate(
-        step, image_ref, blocks, first_in, second_in, shifts_ref, mass_ref,
-        k_high, k_low, pick_ref, below_ref, above_ref, wide_ref,
+        put(wide_ref, slot, [low_mask * below[part] + high_mask * above[part] for part in range(4)])
+    return cadd(load(partial_ref), product(high_ref, low_ref, wide_ref, slots))
+
+
+def level_kernel(
+    partial_ref, first_in, second_in, c_high, c_low, below_ref, above_ref, term_ref, p_high, p_low,
+    result_ref, next_ref, out_ref, first_ref, second_ref, wide_ref,
+):
+    result = couple(
+        partial_ref, first_in, second_in, c_high, c_low, below_ref, above_ref, wide_ref
     )
     save(result_ref, result)
     term = csub(result, load(term_ref))
@@ -267,22 +303,13 @@
     send(image, first_ref, second_ref)
 
 
-def last_kernel(step, others, image_ref, term_ref, *refs):
-    blocks, refs = refs[:others], refs[others:]
-    (
-        first_in, second_in, shifts_ref, mass_ref, k_high, k_low, pick_ref, below_ref, above_ref,
-        basis_ref, previous_ref, inner_ref,
-    ) = refs[:12]
-    earlier, refs = refs[12 : 12 + 2 * ITERS - 1], refs[12 + 2 * ITERS - 1 :]
-    payload_ref, wide_ref, rows_ref = refs
-    result = operate(
-        step, image_ref, blocks, first_in, second_in, shifts_ref, mass_ref,
-        k_high, k_low, pick_ref, below_ref, above_ref, wide_ref,
-    )
-    results = [load(ref) for ref in earlier[: ITERS - 1]] + [result]
-    right = load(earlier[ITERS - 1])
-    images = [load(ref) for ref in earlier[ITERS:]] + [load(image_ref)]
-    vectors = results + [right] + images + [load(previous_ref)]
+def gram_kernel(basis_ref, previous_ref, inner_ref, *refs):
+    refs, (out_ref, rows_ref) = refs[:-2], refs[-2:]
+    results = [load(ref) for ref in refs[: ITERS - 1]]
+    right = load(refs[ITERS - 1])
+    images = [load(ref) for ref in refs[ITERS:]]
+    zero = jnp.zeros(right[0].shape, F32)
+    vectors = results + [(zero, zero), right] + images + [load(previous_ref)]
     count = len(vectors)
     for index, (real, imag) in enumerate(vectors):
         rows_ref[:, index, :] = real
@@ -304,11 +331,35 @@
     width = 2 * count
     lane = iota((count, 3 * width), 1)
     merged = jnp.where(
-        lane < width, table[:count], jnp.where(lane < 2 * width, table[count : 2 * count], table[2 * count :])
+        lane < width,
+        table[:count],
+        jnp.where(lane < 2 * width, table[count : 2 * count], table[2 * count :]),
     )
-    total = jnp.concatenate(
-        [merged, inner_ref[:, 3 * width :]], axis=1
+    out_ref[...] = jnp.concatenate([merged, inner_ref[:, 3 * width :]], axis=1)
+
+
+def last_kernel(
+    partial_ref, first_in, second_in, c_high, c_low, below_ref, above_ref, sums_ref, *refs
+):
+    earlier, (payload_ref, wide_ref) = refs[:-2], refs[-2:]
+    result = couple(
+        partial_ref, first_in, second_in, c_high, c_low, below_ref, above_ref, wide_ref
     )
+    vectors = [load(ref) for ref in earlier[: ITERS - 1]]
+    total = sums_ref[...]
+    count = total.shape[0]
+    row, lane = iota(total.shape, 0), iota(total.shape, 1)
+    base = 4 * count
+    last = ITERS - 1
+    pairs = [(index, last, vector, result) for index, vector in enumerate(vectors)]
+    pairs += [(last, last, result, result), (last, ITERS, result, load(earlier[last]))]
+    for at_row, at_col, left, right in pairs:
+        real = left[0] * right[0] + left[1] * right[1]
+        imag = left[0] * right[1] - left[1] * right[0]
+        for part, value in enumerate((real, imag)):
+            value = jnp.sum(jnp.sum(value, axis=0, keepdims=True), axis=1, keepdims=True)
+            spot = (row == at_row) & (lane == base + part * count + at_col)
+            total = jnp.where(spot, value, total)
 
     @pl.loop(0, payload_ref.shape[0])
     def _(device):
@@ -492,19 +543,31 @@
     return pl.BlockSpec(memory_space=pltpu.VMEM)
 
 
+def hbm():
+    return pl.BlockSpec(memory_space=pltpu.HBM)
+
+
 def smem():
     return pl.BlockSpec(memory_space=pltpu.SMEM)
 
 
-def call(kernel, name, out_shape, in_specs, scratch, args, flops=10**7):
+def in_hbm(*arrays):
+    return tuple(pltpu.with_memory_space_constraint(array, pltpu.HBM) for array in arrays)
+
+
+def shape_of(array):
+    return jax.ShapeDtypeStruct(array.shape, array.dtype)
+
+
+def call(kernel, out_shape, in_specs, scratch, args, flops=10**7):
     return pl.pallas_call(
         kernel,
-        name=name,
         out_shape=out_shape,
         in_specs=in_specs,
         out_specs=jax.tree.map(lambda _: vmem(), out_shape),
         scratch_shapes=scratch,
         cost_estimate=pl.CostEstimate(flops=flops, bytes_accessed=10**6, transcendentals=0),
+        compiler_params=pltpu.CompilerParams(vmem_limit_bytes=VMEM_LIMIT),
     )(*args)
 
 
@@ -533,15 +596,21 @@
     vec = jax.ShapeDtypeStruct((2 * tiles, tile), F32)
     edge = jax.ShapeDtypeStruct((2, tile), F32)
     square = jax.ShapeDtypeStruct((tiles, tile), F32)
-    k_blocks = tiles * slots_k + slots
+    k_blocks = tiles * slots_k
     p_blocks = 2 * tiles
     k_part = jax.ShapeDtypeStruct((tile, k_blocks * tile), BF16)
+    c_part = jax.ShapeDtypeStruct((tile, slots * tile), BF16)
     p_part = jax.ShapeDtypeStruct((tile, p_blocks * tile), BF16)
     mask = jax.ShapeDtypeStruct((slots, tiles, tile), F32)
     pick = jax.ShapeDtypeStruct(((slots_k - 1) * tiles, tiles * n_sub), BF16)
-    wide = pltpu.VMEM((4 * tiles, max(k_blocks, p_blocks) * tile), BF16)
+    drag = jax.ShapeDtypeStruct((steps, 2, tiles, tile), F32)
+    compact = jnp.swapaxes(compact, 1, 2)
+    pattern = pattern.T
     mass = mass.reshape(tiles, tile)
     zero = jnp.zeros((2 * tiles, tile), F32)
+
+    def wide(blocks):
+        return pltpu.VMEM((4 * tiles, blocks * tile), BF16)
 
     even_swap = [(i, i ^ 1) for i in range(n_dom)]
     odd_swap = [(i, (i + 1 if i % 2 else i - 1) % n_dom) for i in range(n_dom)]
@@ -549,62 +618,84 @@
     def exchange(image, first, second):
         second = lax.ppermute(second, "dom", odd_swap)
         first = lax.ppermute(first, "dom", even_swap)
-        blocks = [
-            lax.ppermute(image, "sub", [(i, i ^ k) for i in range(n_sub)]) for k in range(1, n_sub)
-        ]
+        blocks = []
+        for k in range(1, n_sub):
+            blocks.append(lax.ppermute(image, "sub", [(i, i ^ k) for i in range(n_sub)]))
         return blocks, first, second
 
-    right, image, first, second, p_high, p_low = call(
-        start_kernel, "start", (vec, vec, edge, edge, p_part, p_part), [vmem()] * 5, [wide],
-        (basis, compact, weights, fresh, precond),
+    right, image, first, second, p_high, p_low, basis, compact, weights, fresh = call(
+        start_kernel,
+        (vec, vec, edge, edge, p_part, p_part, shape_of(basis), shape_of(compact), shape_of(weights), shape_of(fresh)),
+        [hbm()] * 5,
+        [
+            wide(p_blocks),
+            pltpu.VMEM(precond.shape, F32),
+            pltpu.SemaphoreType.DMA((4,)),
+            pltpu.SemaphoreType.DMA((tiles,)),
+        ],
+        in_hbm(basis, compact, weights, fresh, precond),
     )
-    k_high, k_low, pick_table, below, above, inner = call(
-        functools.partial(prepare_kernel, n_dom), "prepare",
-        (k_part, k_part, pick, mask, mask, square), [smem()] * 4 + [vmem()] * 3, [],
-        (pattern, c_rows, c_side, c_count, basis, k_tiles, c_tiles),
+    k_high, k_low, c_high, c_low, pick_table, below, above, inner, drag = call(
+        functools.partial(prepare_kernel, n_dom),
+        (k_part, k_part, c_part, c_part, pick, mask, mask, square, drag),
+        [hbm()] * 3 + [smem()] + [hbm()] * 4 + [vmem()],
+        [
+            pltpu.VMEM(k_tiles.shape, F32),
+            pltpu.VMEM(c_tiles.shape, F32),
+            pltpu.VMEM(mass.shape, F32),
+            pltpu.SMEM(pattern.shape, jnp.int32),
+            pltpu.SMEM(c_rows.shape, jnp.int32),
+            pltpu.SMEM(c_side.shape, jnp.int32),
+            pltpu.SMEM(shifts.shape, F32),
+            pltpu.SemaphoreType.DMA((6,)),
+            pltpu.SemaphoreType.DMA((tiles,)),
+        ],
+        in_hbm(pattern, c_rows, c_side)
+        + (c_count,)
+        + in_hbm(shifts, mass, k_tiles, c_tiles)
+        + (basis,),
     )
-    others = n_sub - 1
     previous = zero
     for step in range(steps):
         term = right
         images, results = [image], []
         for index in range(ITERS):
-            blocks, first_in, second_in = exchange(images[-1], first, second)
-            common = (
-                images[-1], term, *blocks, first_in, second_in, shifts, mass, k_high, k_low,
-                pick_table, below, above,
+            blocks, first_in, second_in = exchange(image, first, second)
+            partial = call(
+                functools.partial(stiff_kernel, step), vec, [vmem()] * (n_sub + 4),
+                [wide(k_blocks)], (image, *blocks, drag, k_high, k_low, pick_table),
             )
-            specs = [vmem()] * (4 + others) + [smem()] + [vmem()] * 6
+            common = (partial, first_in, second_in, c_high, c_low, below, above)
             if index + 1 < ITERS:
                 result, term, image, first, second = call(
-                    functools.partial(level_kernel, step, others), "level",
-                    (vec, vec, vec, edge, edge), specs + [vmem()] * 2, [wide],
-                    common + (p_high, p_low),
+                    level_kernel, (vec, vec, vec, edge, edge), [vmem()] * 10,
+                    [wide(max(slots, p_blocks))], common + (term, p_high, p_low),
                 )
                 results.append(result)
                 images.append(image)
             else:
-                earlier = (*results, right, *images[:-1])
+                sums = call(
+                    gram_kernel, square, [vmem()] * (3 + 2 * ITERS),
+                    [pltpu.VMEM((tiles, 4 * tiles, tile), F32)],
+                    (basis, previous, inner, *results, right, *images),
+                )
                 payload = call(
-                    functools.partial(last_kernel, step, others), "last",
-                    jax.ShapeDtypeStruct((devices, tiles, tile), F32),
-                    specs + [vmem()] * (3 + len(earlier)),
-                    [wide, pltpu.VMEM((tiles, 4 * (2 * ITERS + 2), tile), F32)],
-                    common + (basis, previous, inner, *earlier),
+                    last_kernel, jax.ShapeDtypeStruct((devices, tiles, tile), F32),
+                    [vmem()] * (8 + ITERS), [wide(slots)], common + (sums, *results, right),
                 )
         sums = lax.all_to_all(payload, AXES, 0, 0)
         if step + 1 < steps:
-            right, image, first, second, previous_next, coeffs, inner_sum = call(
-                functools.partial(between_kernel, total_rows, step), "between",
+            right, image, first, second, latest, coeffs, inner_sum = call(
+                functools.partial(between_kernel, total_rows, step),
                 (vec, vec, edge, edge, vec, jax.ShapeDtypeStruct((2, tile), F32), square),
-                [vmem()] * (8 + ITERS), [wide],
+                [vmem()] * (8 + ITERS), [wide(p_blocks)],
                 (sums, basis, compact, weights, fresh, p_high, p_low, *images, previous),
             )
-            previous = previous_next
+            previous = latest
         else:
             width = basis.shape[1] + 2
             made, listed = call(
-                functools.partial(finish_kernel, total_rows), "finish",
+                functools.partial(finish_kernel, total_rows),
                 (
                     jax.ShapeDtypeStruct((steps, 2, tiles * tile), F32),
                     jax.ShapeDtypeStruct((steps, 2, width), F32),

time: 120 us -> 87.5 us (0.73)
  Pallas kernels: 37.7 us -> 17.7 us
  waiting for transfers between devices: 22.7 us -> 15.2 us
  local copies, waits for them, and re-layouts: 6.29 us -> 0.01 us
  starting transfers between devices: 28.6 us -> 30.6 us
    pallas_call x10 -> x18, Pallas kernels: 37.7 us -> 17.7 us  [call(): pl.pallas_call(kernel, out_shape=out_shape, in_specs=in_specs, out_specs=...]
    ppermute x6, waiting for transfers between devices: 8.01 us -> 1.01 us  [exchange(): first = lax.ppermute(first, 'dom', even_swap)]
    unnamed x62 -> x0, local copies, waits for them, and re-layouts: 5.7 us -> none
    ppermute x6, starting transfers between devices: 13.3 us -> 15.1 us  [exchange(): second = lax.ppermute(second, 'dom', odd_swap)]
  transfers between devices with their start and end apart: 30 -> 30, of which waited for: 10 -> 7; matrix products, arithmetic and copies ran while one was open for 1% -> 0% of each run, Pallas kernels for 3% -> 9%
where the time goes in v1:
time: 87.5 us; the launch traced here: 87.3 us
  starting transfers between devices  30.6 us (35%)
  blocking collectives  22.4 us (26%)
  Pallas kernels  17.7 us (20%)
  waiting for transfers between devices  15.2 us (17%)
  between operations  1.44 us (2%)
    all_to_all x2, blocking collectives, local(): sums = lax.all_to_all(payload, AXES, 0, 0)  22.4 us
    pallas_call x18, Pallas kernels, call(): pl.pallas_call(kernel, out_shape=out_shape, in_specs=in_specs, out_specs=...  17.7 us
    ppermute x6, starting transfers between devices, exchange(): second = lax.ppermute(second, 'dom', odd_swap)  15.1 us
    ppermute x6, waiting for transfers between devices, exchange(): second = lax.ppermute(second, 'dom', odd_swap)  14.1 us
    ppermute x18, starting transfers between devices, exchange(): lax.ppermute(image, 'sub', [(i, i ^ k) for i in range(n_sub)])  12.6 us
    ppermute x6, starting transfers between devices, exchange(): first = lax.ppermute(first, 'dom', even_swap)  2.89 us
  transfers between devices with their start and end apart: 30, of which 7 were waited for; matrix products, arithmetic and copies ran while one was open for 0% of the time, Pallas kernels for 9%

profile of v1, /device:TPU:0, one launch (start us, length us, event | category | flops | bytes accessed | tf_op | source)
XLA Modules:
  0.0 87.3 jit_solution(9232390978921845192)
XLA Ops:
  0.6 2.2 %shard_map.140 = (f32[16,128]{1,0:T(8,128)S(1)}, f32[16,128]{1,0:T(8,128)S(1)}, f32[2,128]{1,0:T(2,128)S(1)}, f32[2,128]{1,0:T(2,128)S(1)}, bf16[128,2048]{1,0:T...) custom-call(f32[2,16,1024]{2,1,0:T(8,128)} %basis_in.1, ...), custom_call_target="tpu_custom_call" | custom-call | flops 10000000 | bytes 1000000 | tf_op jit(solution)/shard_map/pallas_call | solution.py:563
  2.9 2.5 %collective-permute-start.2 = (f32[16,128]{1,0:T(8,128)S(1)}, f32[16,128]{1,0:T(8,128)S(1)}, u32[]{:S(2)}, u32[]{:S(2)}) collective-permute-start(f32[16,128]{1,0:T(8,128)S(1)} %get-tuple-element.46.image_ref.refs_3_.refs_0_), channel_id=1, source_target_pairs={{0,3},{1,2},{2,1},{3,0},{4,7},{5,6},{6,5},{7,4},{8,11},{9,10},{10,... | collective-permute-start | bytes 24584 | tf_op jit(solution)/shard_map/ppermute | solution.py:623
  6.0 1.8 %collective-permute-start.3 = (f32[2,128]{1,0:T(2,128)S(1)}, f32[2,128]{1,0:T(2,128)S(1)}, u32[]{:S(2)}, u32[]{:S(2)}) collective-permute-start(f32[2,128]{1,0:T(2,128)S(1)} %get-tuple-element.52), channel_id=1, source_target_pairs={{0,4},{4,0},{8,12},{12,8},{16,20},{20,16},{24,28},{28,24},{1,5},{5... | collective-permute-start | bytes 3080 | tf_op jit(solution)/shard_map/ppermute | solution.py:620
  7.8 3.5 %collective-permute-start.4 = (f32[2,128]{1,0:T(2,128)S(1)}, f32[2,128]{1,0:T(2,128)S(1)}, u32[]{:S(2)}, u32[]{:S(2)}) collective-permute-start(f32[2,128]{1,0:T(2,128)S(1)} %get-tuple-element.53), channel_id=1, source_target_pairs={{0,28},{4,8},{8,4},{12,16},{16,12},{20,24},{24,20},{28,0},{1,29},{... | collective-permute-start | bytes 3080 | tf_op jit(solution)/shard_map/ppermute | solution.py:619
  12.0 2.2 %shard_map.141 = (bf16[128,3072]{1,0:T(8,128)(2,1)S(1)}, bf16[128,3072]{1,0:T(8,128)(2,1)S(1)}, bf16[128,1024]{1,0:T(8,128)(2,1)S(1)}, bf16[128,1024]{1,0:T(8,12...) custom-call(s32[2,8]{1,0:T(2,128)} %bitcast.5, ...), custom_call_target="tpu_custom_call" | custom-call | flops 10000000 | bytes 1000000 | tf_op jit(solution)/shard_map/pallas_call | solution.py:563
  15.0 1.1 %shard_map.143 = (f32[16,128]{1,0:T(8,128)S(1)}, f32[16,128]{1,0:T(8,128)S(1)}, f32[16,128]{1,0:T(8,128)S(1)}, f32[2,128]{1,0:T(2,128)S(1)}, f32[2,128]{1,0:T(2,128)S(1)}) custom-call(f32[16,128]{1,0:T(8,128)S(1)} %shard_map.142.partial_ref, f32[2,128]{1,0:T(2,128)S(1)} %collective-permute-done.3.first_in, f32[2,128]{1,0:T(2,128)S(1)} %collective-permute-done.4.second_in, ...), custom_call_target="tpu_custom_call" | custom-call | flops 10000000 | bytes 1000000 | tf_op jit(solution)/shard_map/pallas_call | solution.py:563
  18.0 2.6 %collective-permute-start.9 = (f32[2,128]{1,0:T(2,128)S(1)}, f32[2,128]{1,0:T(2,128)S(1)}, u32[]{:S(2)}, u32[]{:S(2)}) collective-permute-start(f32[2,128]{1,0:T(2,128)S(1)} %get-tuple-element.63), channel_id=1, source_target_pairs={{0,28},{4,8},{8,4},{12,16},{16,12},{20,24},{24,20},{28,0},{1,29},{... | collective-permute-start | bytes 3080 | tf_op jit(solution)/shard_map/ppermute | solution.py:619
  21.6 2.7 %collective-permute-done.9.second_in = f32[2,128]{1,0:T(2,128)S(1)} collective-permute-done((f32[2,128]{1,0:T(2,128)S(1)}, f32[2,128]{1,0:T(2,128)S(1)}, u32[]{:S(2)}, u32[]{:S(2)}) %collective-permute-start.9) | collective-permute-done | bytes 1056 | tf_op jit(solution)/shard_map/ppermute | solution.py:619
  24.3 1.5 %shard_map.145 = (f32[16,128]{1,0:T(8,128)S(1)}, f32[16,128]{1,0:T(8,128)}, f32[16,128]{1,0:T(8,128)S(1)}, f32[2,128]{1,0:T(2,128)S(1)}, f32[2,128]{1,0:T(2,128)S(1)}) custom-call(f32[16,128]{1,0:T(8,128)S(1)} %shard_map.144.partial_ref, f32[2,128]{1,0:T(2,128)S(1)} %collective-permute-done.8.first_in, f32[2,128]{1,0:T(2,128)S(1)} %collective-permute-done.9.second_in, ...), custom_call_target="tpu_custom_call" | custom-call | flops 10000000 | bytes 1000000 | tf_op jit(solution)/shard_map/pallas_call | solution.py:563
  25.7 1.5 %collective-permute-start.11 = (f32[16,128]{1,0:T(8,128)S(1)}, f32[16,128]{1,0:T(8,128)S(1)}, u32[]{:S(2)}, u32[]{:S(2)}) collective-permute-start(f32[16,128]{1,0:T(8,128)S(1)} %get-tuple-element.65.image_ref.refs_5_.refs_2_), channel_id=1, source_target_pairs={{0,2},{1,3},{2,0},{3,1},{4,6},{5,7},{6,4},{7,5},{8,10},{9,11},{10,... | collective-permute-start | bytes 24584 | tf_op jit(solution)/shard_map/ppermute | solution.py:623
  27.8 2.6 %collective-permute-start.14 = (f32[2,128]{1,0:T(2,128)S(1)}, f32[2,128]{1,0:T(2,128)S(1)}, u32[]{:S(2)}, u32[]{:S(2)}) collective-permute-start(f32[2,128]{1,0:T(2,128)S(1)} %get-tuple-element.67), channel_id=1, source_target_pairs={{0,28},{4,8},{8,4},{12,16},{16,12},{20,24},{24,20},{28,0},{1,29},{... | collective-permute-start | bytes 3080 | tf_op jit(solution)/shard_map/ppermute | solution.py:619
  31.6 2.4 %collective-permute-done.14.second_in = f32[2,128]{1,0:T(2,128)S(1)} collective-permute-done((f32[2,128]{1,0:T(2,128)S(1)}, f32[2,128]{1,0:T(2,128)S(1)}, u32[]{:S(2)}, u32[]{:S(2)}) %collective-permute-start.14) | collective-permute-done | bytes 1056 | tf_op jit(solution)/shard_map/ppermute | solution.py:619
  34.7 11.9 %all_to_all.10.sums_ref = f32[32,8,128]{2,1,0:T(8,128)S(1)} all-to-all(f32[32,8,128]{2,1,0:T(8,128)S(1)} %shard_map.148), channel_id=1, replica_groups=mesh['dom'=8,'sub'=4] {'dom','sub'}, dimensions={0} | all-to-all | bytes 262144 | tf_op jit(solution)/shard_map/all_to_all | solution.py:686
  47.6 1.7 %collective-permute-start.16 = (f32[16,128]{1,0:T(8,128)S(1)}, f32[16,128]{1,0:T(8,128)S(1)}, u32[]{:S(2)}, u32[]{:S(2)}) collective-permute-start(f32[16,128]{1,0:T(8,128)S(1)} %get-tuple-element.74.image_ref.refs_3_.refs_0_), channel_id=1, source_target_pairs={{0,2},{1,3},{2,0},{3,1},{4,6},{5,7},{6,4},{7,5},{8,10},{9,11},{10,... | collective-permute-start | bytes 24584 | tf_op jit(solution)/shard_map/ppermute | solution.py:623
  49.9 2.1 %collective-permute-start.19 = (f32[2,128]{1,0:T(2,128)S(1)}, f32[2,128]{1,0:T(2,128)S(1)}, u32[]{:S(2)}, u32[]{:S(2)}) collective-permute-start(f32[2,128]{1,0:T(2,128)S(1)} %get-tuple-element.76), channel_id=1, source_target_pairs={{0,28},{4,8},{8,4},{12,16},{16,12},{20,24},{24,20},{28,0},{1,29},{... | collective-permute-start | bytes 3080 | tf_op jit(solution)/shard_map/ppermute | solution.py:619
  52.8 3.4 %collective-permute-done.19.second_in = f32[2,128]{1,0:T(2,128)S(1)} collective-permute-done((f32[2,128]{1,0:T(2,128)S(1)}, f32[2,128]{1,0:T(2,128)S(1)}, u32[]{:S(2)}, u32[]{:S(2)}) %collective-permute-start.19) | collective-permute-done | bytes 1056 | tf_op jit(solution)/shard_map/ppermute | solution.py:619
  56.2 1.1 %shard_map.151 = (f32[16,128]{1,0:T(8,128)S(1)}, f32[16,128]{1,0:T(8,128)S(1)}, f32[16,128]{1,0:T(8,128)S(1)}, f32[2,128]{1,0:T(2,128)S(1)}, f32[2,128]{1,0:T(2,128)S(1)}) custom-call(f32[16,128]{1,0:T(8,128)S(1)} %shard_map.150.partial_ref, f32[2,128]{1,0:T(2,128)S(1)} %collective-permute-done.18.first_in, f32[2,128]{1,0:T(2,128)S(1)} %collective-permute-done.19.second_in, ...), custom_call_target="tpu_custom_call" | custom-call | flops 10000000 | bytes 1000000 | tf_op jit(solution)/shard_map/pallas_call | solution.py:563
  59.2 2.1 %collective-permute-start.24 = (f32[2,128]{1,0:T(2,128)S(1)}, f32[2,128]{1,0:T(2,128)S(1)}, u32[]{:S(2)}, u32[]{:S(2)}) collective-permute-start(f32[2,128]{1,0:T(2,128)S(1)} %get-tuple-element.80), channel_id=1, source_target_pairs={{0,28},{4,8},{8,4},{12,16},{16,12},{20,24},{24,20},{28,0},{1,29},{... | collective-permute-start | bytes 3080 | tf_op jit(solution)/shard_map/ppermute | solution.py:619
  62.7 2.7 %collective-permute-done.24.second_in = f32[2,128]{1,0:T(2,128)S(1)} collective-permute-done((f32[2,128]{1,0:T(2,128)S(1)}, f32[2,128]{1,0:T(2,128)S(1)}, u32[]{:S(2)}, u32[]{:S(2)}) %collective-permute-start.24) | collective-permute-done | bytes 1056 | tf_op jit(solution)/shard_map/ppermute | solution.py:619
  65.4 1.5 %shard_map.153 = (f32[16,128]{1,0:T(8,128)S(1)}, f32[16,128]{1,0:T(8,128)}, f32[16,128]{1,0:T(8,128)S(1)}, f32[2,128]{1,0:T(2,128)S(1)}, f32[2,128]{1,0:T(2,128)S(1)}) custom-call(f32[16,128]{1,0:T(8,128)S(1)} %shard_map.152.partial_ref, f32[2,128]{1,0:T(2,128)S(1)} %collective-permute-done.23.first_in, f32[2,128]{1,0:T(2,128)S(1)} %collective-permute-done.24.second_in, ...), custom_call_target="tpu_custom_call" | custom-call | flops 10000000 | bytes 1000000 | tf_op jit(solution)/shard_map/pallas_call | solution.py:563
  67.7 1.1 %collective-permute-start.25 = (f32[16,128]{1,0:T(8,128)S(1)}, f32[16,128]{1,0:T(8,128)S(1)}, u32[]{:S(2)}, u32[]{:S(2)}) collective-permute-start(f32[16,128]{1,0:T(8,128)S(1)} %get-tuple-element.82.image_ref.refs_5_.refs_2_), channel_id=1, source_target_pairs={{0,1},{1,0},{2,3},{3,2},{4,5},{5,4},{6,7},{7,6},{8,9},{9,8},{10,11... | collective-permute-start | bytes 24584 | tf_op jit(solution)/shard_map/ppermute | solution.py:623
  69.0 2.1 %collective-permute-start.29 = (f32[2,128]{1,0:T(2,128)S(1)}, f32[2,128]{1,0:T(2,128)S(1)}, u32[]{:S(2)}, u32[]{:S(2)}) collective-permute-start(f32[2,128]{1,0:T(2,128)S(1)} %get-tuple-element.84), channel_id=1, source_target_pairs={{0,28},{4,8},{8,4},{12,16},{16,12},{20,24},{24,20},{28,0},{1,29},{... | collective-permute-start | bytes 3080 | tf_op jit(solution)/shard_map/ppermute | solution.py:619
  72.4 2.9 %collective-permute-done.29.second_in = f32[2,128]{1,0:T(2,128)S(1)} collective-permute-done((f32[2,128]{1,0:T(2,128)S(1)}, f32[2,128]{1,0:T(2,128)S(1)}, u32[]{:S(2)}, u32[]{:S(2)}) %collective-permute-start.29) | collective-permute-done | bytes 1056 | tf_op jit(solution)/shard_map/ppermute | solution.py:619
  75.9 10.5 %all_to_all.11.sums_ref = f32[32,8,128]{2,1,0:T(8,128)S(1)} all-to-all(f32[32,8,128]{2,1,0:T(8,128)S(1)} %shard_map.156), channel_id=1, replica_groups=mesh['dom'=8,'sub'=4] {'dom','sub'}, dimensions={0} | all-to-all | bytes 262144 | tf_op jit(solution)/shard_map/all_to_all | solution.py:686
  (57 shorter events, 16.2 us)
Async XLA Ops:
  2.9 11.4 %collective-permute-start.2 = (f32[16,128]{1,0:T(8,128)S(1)}, f32[16,128]{1,0:T(8,128)S(1)}, u32[]{:S(2)}, u32[]{:S(2)}) collective-permute-start(f32[16,128]{1,0:T(8,128)S(1)} %get-tuple-element.46.image_ref.refs_3_.refs_0_), channel_id=1, source_target_pairs={{0,3},{1,2},{2,1},{3,0},{4,7},{5,6},{6,5},{7,4},{8,11},{9,10},{10,... | collective-permute-start | bytes 24584 | tf_op jit(solution)/shard_map/ppermute | solution.py:623
  5.4 8.9 %collective-permute-start.1 = (f32[16,128]{1,0:T(8,128)S(1)}, f32[16,128]{1,0:T(8,128)S(1)}, u32[]{:S(2)}, u32[]{:S(2)}) collective-permute-start(f32[16,128]{1,0:T(8,128)S(1)} %get-tuple-element.46.image_ref.refs_3_.refs_0_), channel_id=1, source_target_pairs={{0,2},{1,3},{2,0},{3,1},{4,6},{5,7},{6,4},{7,5},{8,10},{9,11},{10,... | collective-permute-start | bytes 24584 | tf_op jit(solution)/shard_map/ppermute | solution.py:623
  6.0 8.3 %collective-permute-start = (f32[16,128]{1,0:T(8,128)S(1)}, f32[16,128]{1,0:T(8,128)S(1)}, u32[]{:S(2)}, u32[]{:S(2)}) collective-permute-start(f32[16,128]{1,0:T(8,128)S(1)} %get-tuple-element.46.image_ref.refs_3_.refs_0_), channel_id=1, source_target_pairs={{0,1},{1,0},{2,3},{3,2},{4,5},{5,4},{6,7},{7,6},{8,9},{9,8},{10,11... | collective-permute-start | bytes 24584 | tf_op jit(solution)/shard_map/ppermute | solution.py:623
  6.0 9.0 %collective-permute-start.3 = (f32[2,128]{1,0:T(2,128)S(1)}, f32[2,128]{1,0:T(2,128)S(1)}, u32[]{:S(2)}, u32[]{:S(2)}) collective-permute-start(f32[2,128]{1,0:T(2,128)S(1)} %get-tuple-element.52), channel_id=1, source_target_pairs={{0,4},{4,0},{8,12},{12,8},{16,20},{20,16},{24,28},{28,24},{1,5},{5... | collective-permute-start | bytes 3080 | tf_op jit(solution)/shard_map/ppermute | solution.py:620
  7.8 7.2 %collective-permute-start.4 = (f32[2,128]{1,0:T(2,128)S(1)}, f32[2,128]{1,0:T(2,128)S(1)}, u32[]{:S(2)}, u32[]{:S(2)}) collective-permute-start(f32[2,128]{1,0:T(2,128)S(1)} %get-tuple-element.53), channel_id=1, source_target_pairs={{0,28},{4,8},{8,4},{12,16},{16,12},{20,24},{24,20},{28,0},{1,29},{... | collective-permute-start | bytes 3080 | tf_op jit(solution)/shard_map/ppermute | solution.py:619
  16.1 4.5 %collective-permute-start.7 = (f32[16,128]{1,0:T(8,128)S(1)}, f32[16,128]{1,0:T(8,128)S(1)}, u32[]{:S(2)}, u32[]{:S(2)}) collective-permute-start(f32[16,128]{1,0:T(8,128)S(1)} %get-tuple-element.61.image_ref.refs_4_.refs_1_), channel_id=1, source_target_pairs={{0,3},{1,2},{2,1},{3,0},{4,7},{5,6},{6,5},{7,4},{8,11},{9,10},{10,... | collective-permute-start | bytes 24584 | tf_op jit(solution)/shard_map/ppermute | solution.py:623
  16.8 3.8 %collective-permute-start.6 = (f32[16,128]{1,0:T(8,128)S(1)}, f32[16,128]{1,0:T(8,128)S(1)}, u32[]{:S(2)}, u32[]{:S(2)}) collective-permute-start(f32[16,128]{1,0:T(8,128)S(1)} %get-tuple-element.61.image_ref.refs_4_.refs_1_), channel_id=1, source_target_pairs={{0,2},{1,3},{2,0},{3,1},{4,6},{5,7},{6,4},{7,5},{8,10},{9,11},{10,... | collective-permute-start | bytes 24584 | tf_op jit(solution)/shard_map/ppermute | solution.py:623
  18.0 6.3 %collective-permute-start.9 = (f32[2,128]{1,0:T(2,128)S(1)}, f32[2,128]{1,0:T(2,128)S(1)}, u32[]{:S(2)}, u32[]{:S(2)}) collective-permute-start(f32[2,128]{1,0:T(2,128)S(1)} %get-tuple-element.63), channel_id=1, source_target_pairs={{0,28},{4,8},{8,4},{12,16},{16,12},{20,24},{24,20},{28,0},{1,29},{... | collective-permute-start | bytes 3080 | tf_op jit(solution)/shard_map/ppermute | solution.py:619
  25.7 5.2 %collective-permute-start.12 = (f32[16,128]{1,0:T(8,128)S(1)}, f32[16,128]{1,0:T(8,128)S(1)}, u32[]{:S(2)}, u32[]{:S(2)}) collective-permute-start(f32[16,128]{1,0:T(8,128)S(1)} %get-tuple-element.65.image_ref.refs_5_.refs_2_), channel_id=1, source_target_pairs={{0,3},{1,2},{2,1},{3,0},{4,7},{5,6},{6,5},{7,4},{8,11},{9,10},{10,... | collective-permute-start | bytes 24584 | tf_op jit(solution)/shard_map/ppermute | solution.py:623
  25.7 5.2 %collective-permute-start.11 = (f32[16,128]{1,0:T(8,128)S(1)}, f32[16,128]{1,0:T(8,128)S(1)}, u32[]{:S(2)}, u32[]{:S(2)}) collective-permute-start(f32[16,128]{1,0:T(8,128)S(1)} %get-tuple-element.65.image_ref.refs_5_.refs_2_), channel_id=1, source_target_pairs={{0,2},{1,3},{2,0},{3,1},{4,6},{5,7},{6,4},{7,5},{8,10},{9,11},{10,... | collective-permute-start | bytes 24584 | tf_op jit(solution)/shard_map/ppermute | solution.py:623
  27.2 3.7 %collective-permute-start.10 = (f32[16,128]{1,0:T(8,128)S(1)}, f32[16,128]{1,0:T(8,128)S(1)}, u32[]{:S(2)}, u32[]{:S(2)}) collective-permute-start(f32[16,128]{1,0:T(8,128)S(1)} %get-tuple-element.65.image_ref.refs_5_.refs_2_), channel_id=1, source_target_pairs={{0,1},{1,0},{2,3},{3,2},{4,5},{5,4},{6,7},{7,6},{8,9},{9,8},{10,11... | collective-permute-start | bytes 24584 | tf_op jit(solution)/shard_map/ppermute | solution.py:623
  27.6 4.0 %collective-permute-start.13 = (f32[2,128]{1,0:T(2,128)S(1)}, f32[2,128]{1,0:T(2,128)S(1)}, u32[]{:S(2)}, u32[]{:S(2)}) collective-permute-start(f32[2,128]{1,0:T(2,128)S(1)} %get-tuple-element.66), channel_id=1, source_target_pairs={{0,4},{4,0},{8,12},{12,8},{16,20},{20,16},{24,28},{28,24},{1,5},{5... | collective-permute-start | bytes 3080 | tf_op jit(solution)/shard_map/ppermute | solution.py:620
  27.8 6.3 %collective-permute-start.14 = (f32[2,128]{1,0:T(2,128)S(1)}, f32[2,128]{1,0:T(2,128)S(1)}, u32[]{:S(2)}, u32[]{:S(2)}) collective-permute-start(f32[2,128]{1,0:T(2,128)S(1)} %get-tuple-element.67), channel_id=1, source_target_pairs={{0,28},{4,8},{8,4},{12,16},{16,12},{20,24},{24,20},{28,0},{1,29},{... | collective-permute-start | bytes 3080 | tf_op jit(solution)/shard_map/ppermute | solution.py:619
  47.4 4.7 %collective-permute-start.17 = (f32[16,128]{1,0:T(8,128)S(1)}, f32[16,128]{1,0:T(8,128)S(1)}, u32[]{:S(2)}, u32[]{:S(2)}) collective-permute-start(f32[16,128]{1,0:T(8,128)S(1)} %get-tuple-element.74.image_ref.refs_3_.refs_0_), channel_id=1, source_target_pairs={{0,3},{1,2},{2,1},{3,0},{4,7},{5,6},{6,5},{7,4},{8,11},{9,10},{10,... | collective-permute-start | bytes 24584 | tf_op jit(solution)/shard_map/ppermute | solution.py:623
  47.6 4.5 %collective-permute-start.16 = (f32[16,128]{1,0:T(8,128)S(1)}, f32[16,128]{1,0:T(8,128)S(1)}, u32[]{:S(2)}, u32[]{:S(2)}) collective-permute-start(f32[16,128]{1,0:T(8,128)S(1)} %get-tuple-element.74.image_ref.refs_3_.refs_0_), channel_id=1, source_target_pairs={{0,2},{1,3},{2,0},{3,1},{4,6},{5,7},{6,4},{7,5},{8,10},{9,11},{10,... | collective-permute-start | bytes 24584 | tf_op jit(solution)/shard_map/ppermute | solution.py:623
  49.9 6.3 %collective-permute-start.19 = (f32[2,128]{1,0:T(2,128)S(1)}, f32[2,128]{1,0:T(2,128)S(1)}, u32[]{:S(2)}, u32[]{:S(2)}) collective-permute-start(f32[2,128]{1,0:T(2,128)S(1)} %get-tuple-element.76), channel_id=1, source_target_pairs={{0,28},{4,8},{8,4},{12,16},{16,12},{20,24},{24,20},{28,0},{1,29},{... | collective-permute-start | bytes 3080 | tf_op jit(solution)/shard_map/ppermute | solution.py:619
  57.3 4.0 %collective-permute-start.22 = (f32[16,128]{1,0:T(8,128)S(1)}, f32[16,128]{1,0:T(8,128)S(1)}, u32[]{:S(2)}, u32[]{:S(2)}) collective-permute-start(f32[16,128]{1,0:T(8,128)S(1)} %get-tuple-element.78.image_ref.refs_4_.refs_1_), channel_id=1, source_target_pairs={{0,3},{1,2},{2,1},{3,0},{4,7},{5,6},{6,5},{7,4},{8,11},{9,10},{10,... | collective-permute-start | bytes 24584 | tf_op jit(solution)/shard_map/ppermute | solution.py:623
  57.3 4.0 %collective-permute-start.21 = (f32[16,128]{1,0:T(8,128)S(1)}, f32[16,128]{1,0:T(8,128)S(1)}, u32[]{:S(2)}, u32[]{:S(2)}) collective-permute-start(f32[16,128]{1,0:T(8,128)S(1)} %get-tuple-element.78.image_ref.refs_4_.refs_1_), channel_id=1, source_target_pairs={{0,2},{1,3},{2,0},{3,1},{4,6},{5,7},{6,4},{7,5},{8,10},{9,11},{10,... | collective-permute-start | bytes 24584 | tf_op jit(solution)/shard_map/ppermute | solution.py:623
  59.2 6.3 %collective-permute-start.24 = (f32[2,128]{1,0:T(2,128)S(1)}, f32[2,128]{1,0:T(2,128)S(1)}, u32[]{:S(2)}, u32[]{:S(2)}) collective-permute-start(f32[2,128]{1,0:T(2,128)S(1)} %get-tuple-element.80), channel_id=1, source_target_pairs={{0,28},{4,8},{8,4},{12,16},{16,12},{20,24},{24,20},{28,0},{1,29},{... | collective-permute-start | bytes 3080 | tf_op jit(solution)/shard_map/ppermute | solution.py:619
  66.9 4.7 %collective-permute-start.27 = (f32[16,128]{1,0:T(8,128)S(1)}, f32[16,128]{1,0:T(8,128)S(1)}, u32[]{:S(2)}, u32[]{:S(2)}) collective-permute-start(f32[16,128]{1,0:T(8,128)S(1)} %get-tuple-element.82.image_ref.refs_5_.refs_2_), channel_id=1, source_target_pairs={{0,3},{1,2},{2,1},{3,0},{4,7},{5,6},{6,5},{7,4},{8,11},{9,10},{10,... | collective-permute-start | bytes 24584 | tf_op jit(solution)/shard_map/ppermute | solution.py:623
  66.9 4.7 %collective-permute-start.26 = (f32[16,128]{1,0:T(8,128)S(1)}, f32[16,128]{1,0:T(8,128)S(1)}, u32[]{:S(2)}, u32[]{:S(2)}) collective-permute-start(f32[16,128]{1,0:T(8,128)S(1)} %get-tuple-element.82.image_ref.refs_5_.refs_2_), channel_id=1, source_target_pairs={{0,2},{1,3},{2,0},{3,1},{4,6},{5,7},{6,4},{7,5},{8,10},{9,11},{10,... | collective-permute-start | bytes 24584 | tf_op jit(solution)/shard_map/ppermute | solution.py:623
  67.7 4.0 %collective-permute-start.25 = (f32[16,128]{1,0:T(8,128)S(1)}, f32[16,128]{1,0:T(8,128)S(1)}, u32[]{:S(2)}, u32[]{:S(2)}) collective-permute-start(f32[16,128]{1,0:T(8,128)S(1)} %get-tuple-element.82.image_ref.refs_5_.refs_2_), channel_id=1, source_target_pairs={{0,1},{1,0},{2,3},{3,2},{4,5},{5,4},{6,7},{7,6},{8,9},{9,8},{10,11... | collective-permute-start | bytes 24584 | tf_op jit(solution)/shard_map/ppermute | solution.py:623
  68.7 3.6 %collective-permute-start.28 = (f32[2,128]{1,0:T(2,128)S(1)}, f32[2,128]{1,0:T(2,128)S(1)}, u32[]{:S(2)}, u32[]{:S(2)}) collective-permute-start(f32[2,128]{1,0:T(2,128)S(1)} %get-tuple-element.83), channel_id=1, source_target_pairs={{0,4},{4,0},{8,12},{12,8},{16,20},{20,16},{24,28},{28,24},{1,5},{5... | collective-permute-start | bytes 3080 | tf_op jit(solution)/shard_map/ppermute | solution.py:620
  69.0 6.3 %collective-permute-start.29 = (f32[2,128]{1,0:T(2,128)S(1)}, f32[2,128]{1,0:T(2,128)S(1)}, u32[]{:S(2)}, u32[]{:S(2)}) collective-permute-start(f32[2,128]{1,0:T(2,128)S(1)} %get-tuple-element.84), channel_id=1, source_target_pairs={{0,28},{4,8},{8,4},{12,16},{16,12},{20,24},{24,20},{28,0},{1,29},{... | collective-permute-start | bytes 3080 | tf_op jit(solution)/shard_map/ppermute | solution.py:619
  (6 other events, 19.6 us)

commit v2 on v1

--- a/solution.py
+++ b/solution.py
@@ -13,6 +13,8 @@
 BF16 = jnp.bfloat16
 NT_DIMS = (((1,), (1,)), ((), ()))
 LANES = 128
+COPIED = 11
+FOLD = 4
 VMEM_LIMIT = 12 * 1024 * 1024
 AXES = ("dom", "sub")
 
@@ -136,34 +138,27 @@
     return (coef_real, coef_imag), (gamma_real, gamma_imag)
 
 
-def start_kernel(
-    basis_in, compact_in, weights_in, fresh_in, precond_in,
-    right_ref, image_ref, first_ref, second_ref, high_ref, low_ref,
-    basis_ref, compact_ref, weights_ref, fresh_ref,
-    wide_ref, precond_ref, small_sem, tile_sem,
-):
+def start_kernel(*refs):
+    sources, refs = refs[:COPIED], refs[COPIED:]
+    precond_in, refs = refs[0], refs[1:]
+    right_ref, image_ref, first_ref, second_ref, high_ref, low_ref = refs[:6]
+    targets, refs = refs[6 : 6 + COPIED], refs[6 + COPIED :]
+    wide_ref, precond_ref, small_sem, tile_sem = refs
     moves = [
         pltpu.make_async_copy(source, target, small_sem.at[index])
-        for index, (source, target) in enumerate(
-            (
-                (compact_in, compact_ref),
-                (weights_in, weights_ref),
-                (fresh_in, fresh_ref),
-                (basis_in, basis_ref),
-            )
-        )
+        for index, (source, target) in enumerate(zip(sources, targets))
     ]
-    for move in moves:
-        move.start()
     tiles = precond_in.shape[0]
     tile_moves = [
         pltpu.make_async_copy(precond_in.at[tile], precond_ref.at[tile], tile_sem.at[tile])
         for tile in range(tiles)
     ]
-    for move in tile_moves:
+    early, late = moves[:4], moves[4:]
+    for move in early + tile_moves + late:
         move.start()
-    for move in moves:
+    for move in early:
         move.wait()
+    basis_ref, compact_ref, weights_ref, fresh_ref = targets[:4]
     coef, _ = coefficients(0, compact_ref, weights_ref, fresh_ref)
     right = mix_basis(coef, basis_ref)
     save(right_ref, right)
@@ -174,77 +169,65 @@
     image = precondition(right, high_ref, low_ref, wide_ref)
     save(image_ref, image)
     send(image, first_ref, second_ref)
+    for move in late:
+        move.wait()
+
+
+def as_column(row):
+    count = row.shape[1]
+    same = iota((count, count), 0) == iota((count, count), 1)
+    return jnp.sum(jnp.where(same, row, 0.0), axis=1, keepdims=True)
 
 
 def prepare_kernel(
-    n_dom, pattern_in, rows_in, side_in, count_ref, shifts_in, mass_in, k_in, c_in, basis_ref,
-    high_ref, low_ref, c_high_ref, c_low_ref, pick_ref, below_ref, above_ref, inner_ref, drag_ref,
-    k_ref, c_ref, mass_ref, pattern_ref, rows_ref, side_ref, shifts_ref,
-    small_sem, k_sem,
+    n_dom, count_ref, pattern_ref, rows_ref, side_ref, shifts_ref, mass_ref, k_ref, c_ref,
+    high_ref, low_ref, c_high_ref, c_low_ref, pick_ref, below_ref, above_ref, drag_ref,
 ):
-    moves = [
-        pltpu.make_async_copy(source, target, small_sem.at[index])
-        for index, (source, target) in enumerate(
-            (
-                (pattern_in, pattern_ref),
-                (rows_in, rows_ref),
-                (side_in, side_ref),
-                (shifts_in, shifts_ref),
-                (mass_in, mass_ref),
-                (c_in, c_ref),
-            )
-        )
+    tiles, slots_k, slots = k_ref.shape[0], k_ref.shape[1], c_ref.shape[0]
+    for tile in range(tiles):
+        for slot in range(slots_k):
+            store_parts(high_ref, low_ref, tile * slots_k + slot, k_ref[tile, slot])
+    for slot in range(slots):
+        store_parts(c_high_ref, c_low_ref, slot, c_ref[slot])
+    mine = lax.axis_index("sub") * tiles
+    lane = iota((tiles, pick_ref.shape[1]), 1) ^ mine
+    lane = lane.astype(F32)
+    picked = [
+        jnp.where(as_column(pattern_ref[slot : slot + 1].astype(F32)) == lane, 1.0, 0.0)
+        for slot in range(slots_k - 1)
     ]
-    for move in moves:
-        move.start()
-    tiles, slots_k = k_in.shape[0], k_in.shape[1]
-    k_moves = [
-        pltpu.make_async_copy(k_in.at[tile], k_ref.at[tile], k_sem.at[tile]) for tile in range(tiles)
-    ]
-    for move in k_moves:
-        move.start()
+    pick_ref[...] = jnp.concatenate(picked, axis=0).astype(BF16)
+    domain = lax.axis_index("dom")
+    shape = (tiles, LANES)
+    row = iota(shape, 0)
+    for slot in range(slots):
+        live = slot < count_ref[0]
+        side = jnp.broadcast_to(side_ref[:, slot : slot + 1], shape)
+        here = row == jnp.broadcast_to(rows_ref[:, slot : slot + 1], shape)
+        low_on = jnp.where(live & (domain > 0), 1.0, 0.0)
+        high_on = jnp.where(live & (domain < n_dom - 1), 1.0, 0.0)
+        below_ref[slot] = jnp.where(here & (side == 0), low_on, 0.0)
+        above_ref[slot] = jnp.where(here & (side != 0), high_on, 0.0)
+    mass = mass_ref[...]
+    for step in range(drag_ref.shape[0]):
+        for part in range(2):
+            shift = jnp.broadcast_to(shifts_ref[step : step + 1, part : part + 1], shape)
+            drag_ref[step, part] = mass * shift
+
+
+def inner_kernel(basis_ref, after_ref, inner_ref):
     real, imag = basis_ref[0], basis_ref[1]
     inner = nt_dot(real, jnp.concatenate([real, imag], axis=0), HIGH)
     inner = inner + nt_dot(imag, jnp.concatenate([imag, -real], axis=0), HIGH)
     inner_ref[...] = jnp.zeros(inner_ref.shape, F32)
     half, wide = inner_ref.shape[0], inner.shape[1]
-    inner_ref[:, 6 * half : 6 * half + wide] = inner[:half]
-    inner_ref[:, 6 * half + wide : 6 * half + 2 * wide] = inner[half:]
-    for move in moves:
-        move.wait()
-    mine = lax.axis_index("sub") * tiles
-    row, lane = iota(pick_ref.shape, 0), iota(pick_ref.shape, 1)
-    picked = jnp.zeros(pick_ref.shape, F32)
-    for slot in range(slots_k - 1):
-        for tile in range(tiles):
-            column = pattern_ref[slot, tile] ^ mine
-            picked = jnp.where((row == slot * tiles + tile) & (lane == column), 1.0, picked)
-    pick_ref[...] = picked.astype(BF16)
-    domain = lax.axis_index("dom")
-    row = iota((tiles, LANES), 0)
-    slots = c_ref.shape[0]
-    for slot in range(slots):
-        live = slot < count_ref[0]
-        side = side_ref[slot]
-        here = row == rows_ref[slot]
-        low_on = live & (side == 0) & (domain > 0)
-        high_on = live & (side != 0) & (domain < n_dom - 1)
-        below_ref[slot] = jnp.where(here & low_on, 1.0, 0.0)
-        above_ref[slot] = jnp.where(here & high_on, 1.0, 0.0)
-    mass = mass_ref[...]
-    for step in range(drag_ref.shape[0]):
-        for part in range(2):
-            drag_ref[step, part] = mass * shifts_ref[step, part]
-    for slot in range(slots):
-        store_parts(c_high_ref, c_low_ref, slot, c_ref[slot])
-    for tile in range(tiles):
-        k_moves[tile].wait()
-        for slot in range(slots_k):
-            store_parts(high_ref, low_ref, tile * slots_k + slot, k_ref[tile, slot])
-
-
-def stiff_kernel(step, image_ref, *refs):
-    blocks, (drag_ref, high_ref, low_ref, pick_ref, result_ref, wide_ref) = refs[:-6], refs[-6:]
+    inner_ref[:, 4 * half : 4 * half + wide] = inner[:half]
+    inner_ref[:, 4 * half + wide : 4 * half + 2 * wide] = inner[half:]
+
+
+def stiff_kernel(step, others, image_ref, *refs):
+    blocks, (drag_ref, high_ref, low_ref, pick_ref) = refs[:others], refs[others : others + 4]
+    result_ref, wide_ref = refs[-2:]
     image = load(image_ref)
     tiles = image[0].shape[0]
     own = parts_of(image)
@@ -290,14 +273,16 @@
 
 def level_kernel(
     partial_ref, first_in, second_in, c_high, c_low, below_ref, above_ref, term_ref, p_high, p_low,
-    result_ref, next_ref, out_ref, first_ref, second_ref, wide_ref,
+    result_ref, out_ref, first_ref, second_ref, *refs,
 ):
+    next_refs, wide_ref = refs[:-1], refs[-1]
     result = couple(
         partial_ref, first_in, second_in, c_high, c_low, below_ref, above_ref, wide_ref
     )
     save(result_ref, result)
     term = csub(result, load(term_ref))
-    save(next_ref, term)
+    for next_ref in next_refs:
+        save(next_ref, term)
     image = precondition(term, p_high, p_low, wide_ref)
     save(out_ref, image)
     send(image, first_ref, second_ref)
@@ -317,29 +302,69 @@
         rows_ref[:, 2 * count + index, :] = imag
         rows_ref[:, 3 * count + index, :] = -real
     tiles = rows_ref.shape[0]
-    lefts, rights = [], []
+    lefts, rights, chosen = [], [], []
+    half = count // 2
     for tile in range(tiles):
         lanes = slice(tile * LANES, (tile + 1) * LANES)
         for part in range(2):
             left = rows_ref[tile, part * count : (part + 1) * count]
             lefts.append(jnp.concatenate([basis_ref[part, :, lanes], left], axis=0))
-            rights.append(rows_ref[tile, 2 * part * count : 2 * (part + 1) * count])
+            base = 2 * part * count
+            rights.append(rows_ref[tile, base : base + 2 * count])
+            chosen.append(
+                jnp.concatenate(
+                    [
+                        rows_ref[tile, base + half : base + count],
+                        rows_ref[tile, base + count + half : base + 2 * count],
+                    ],
+                    axis=0,
+                )
+            )
     left = jnp.concatenate(lefts, axis=1)
-    right_rows = jnp.concatenate(rights, axis=1)
-    right_rows = jnp.concatenate([right_rows] * 3, axis=0)
+    chosen = jnp.concatenate(chosen, axis=1)
+    right_rows = jnp.concatenate([chosen, chosen, jnp.concatenate(rights, axis=1)], axis=0)
     table = nt_dot(left, right_rows, HIGH)
-    width = 2 * count
-    lane = iota((count, 3 * width), 1)
+    width = table.shape[1]
+    lane = iota((count, width), 1)
     merged = jnp.where(
-        lane < width,
+        lane < count,
         table[:count],
-        jnp.where(lane < 2 * width, table[count : 2 * count], table[2 * count :]),
-    )
-    out_ref[...] = jnp.concatenate([merged, inner_ref[:, 3 * width :]], axis=1)
+        jnp.where(lane < 2 * count, table[count : 2 * count], table[2 * count :]),
+    )
+    out_ref[...] = jnp.concatenate([merged, inner_ref[:, width:]], axis=1)
+
+
+def pack(total, fold):
+    width = LANES // fold
+    row, lane = iota(total.shape, 0), iota(total.shape, 1)
+    kept = jnp.where(lane < width, total, 0.0)
+    moved = kept
+    for k in range(1, fold):
+        moved = jnp.where(row % fold == k, pltpu.roll(kept, k * width, 1), moved)
+    return jnp.concatenate(
+        [
+            jnp.sum(moved[k : k + fold], axis=0, keepdims=True)
+            for k in range(0, total.shape[0], fold)
+        ],
+        axis=0,
+    )
+
+
+def unpack(packed, fold):
+    width = LANES // fold
+    rows = packed.shape[0]
+    spread = jnp.concatenate(
+        [jnp.broadcast_to(packed[k : k + 1], (fold, LANES)) for k in range(rows)], axis=0
+    )
+    row, lane = iota(spread.shape, 0), iota(spread.shape, 1)
+    moved = spread
+    for k in range(1, fold):
+        moved = jnp.where(row % fold == k, pltpu.roll(spread, LANES - k * width, 1), moved)
+    return jnp.where(lane < width, moved, 0.0)
 
 
 def last_kernel(
-    partial_ref, first_in, second_in, c_high, c_low, below_ref, above_ref, sums_ref, *refs
+    fold, partial_ref, first_in, second_in, c_high, c_low, below_ref, above_ref, sums_ref, *refs
 ):
     earlier, (payload_ref, wide_ref) = refs[:-2], refs[-2:]
     result = couple(
@@ -349,7 +374,7 @@
     total = sums_ref[...]
     count = total.shape[0]
     row, lane = iota(total.shape, 0), iota(total.shape, 1)
-    base = 4 * count
+    base = 2 * count
     last = ITERS - 1
     pairs = [(index, last, vector, result) for index, vector in enumerate(vectors)]
     pairs += [(last, last, result, result), (last, ITERS, result, load(earlier[last]))]
@@ -360,6 +385,8 @@
             value = jnp.sum(jnp.sum(value, axis=0, keepdims=True), axis=1, keepdims=True)
             spot = (row == at_row) & (lane == base + part * count + at_col)
             total = jnp.where(spot, value, total)
+    if fold > 1:
+        total = pack(total, fold)
 
     @pl.loop(0, payload_ref.shape[0])
     def _(device):
@@ -370,7 +397,7 @@
     total_rows, sums, inner, basis_ref, images, previous,
 ):
     count = sums.shape[0]
-    width = 2 * count
+    half = count // 2
     shape = sums.shape
 
     def column(lane, table=sums):
@@ -380,7 +407,7 @@
         return jnp.broadcast_to(column(lane)[row : row + 1], shape)
 
     def entry(row, col):
-        base = 2 * width
+        base = 2 * count
         return cell(row, base + col), cell(row, base + count + col)
 
     gram = {(a, b): entry(a, b) for a in range(ITERS) for b in range(a, ITERS)}
@@ -420,10 +447,10 @@
 
     projections = []
     for block in range(2):
-        base = block * width
+        base = block * count
         value = None
         for a in range(ITERS):
-            term = cmul(solved[a], (column(base + offset + a), column(base + count + offset + a)))
+            term = cmul(solved[a], (column(base + a), column(base + half + a)))
             value = term if value is None else cadd(value, term)
         projections.append(scale(value, 1.0 / total_rows))
     value = None
@@ -433,7 +460,7 @@
     extra = scale(value, 1.0 / total_rows)
 
     row, lane = iota(shape, 0), iota(shape, 1)
-    first = 3 * width
+    first = 4 * count
     span = 4 * count
     first_row = jnp.zeros(shape, F32)
     second_row = jnp.zeros(shape, F32)
@@ -453,10 +480,10 @@
     quad = jnp.sum(inner * (real_col * first_row + imag_col * second_row), axis=1, keepdims=True)
     quad = jnp.broadcast_to(quad, shape)
     for block in range(2):
-        base = block * width
+        base = block * count
         real, imag = projections[block]
         cross = cmul(
-            cmul((real, -imag), extra), (column(base + count - 1), column(base + width - 1))
+            cmul((real, -imag), extra), (column(base + half - 1), column(base + count - 1))
         )[0]
         quad = quad + 2.0 * cross - 2.0 * total_rows * (real * real + imag * imag)
     quad = jnp.broadcast_to(jnp.sum(quad, axis=0, keepdims=True), shape)
@@ -525,7 +552,7 @@
 def finish_kernel(total_rows, sums_ref, inner_ref, basis_ref, *refs):
     images = [load(ref) for ref in refs[:ITERS]]
     previous_ref, before_ref, made_ref, listed_ref = refs[ITERS:]
-    sums = reduce_sums(sums_ref)
+    sums = unpack(reduce_sums(sums_ref), FOLD)
     previous = load(previous_ref)
     latest, coeffs = settle(total_rows, sums, inner_ref[...], basis_ref, images, previous)
     for step, vector in enumerate((previous, latest)):
@@ -553,10 +580,6 @@
 
 def in_hbm(*arrays):
     return tuple(pltpu.with_memory_space_constraint(array, pltpu.HBM) for array in arrays)
-
-
-def shape_of(array):
-    return jax.ShapeDtypeStruct(array.shape, array.dtype)
 
 
 def call(kernel, out_shape, in_specs, scratch, args, flops=10**7):
@@ -613,47 +636,44 @@
         return pltpu.VMEM((4 * tiles, blocks * tile), BF16)
 
     even_swap = [(i, i ^ 1) for i in range(n_dom)]
-    odd_swap = [(i, (i + 1 if i % 2 else i - 1) % n_dom) for i in range(n_dom)]
+    odd_swap = []
+    for i in range(n_dom):
+        other = i + 1 if i % 2 else i - 1
+        for j in range(n_sub):
+            inside = 0 <= other < n_dom
+            target = other * n_sub + j if inside else i * n_sub + (j ^ 1)
+            odd_swap.append((i * n_sub + j, target))
 
     def exchange(image, first, second):
-        second = lax.ppermute(second, "dom", odd_swap)
+        second = lax.ppermute(second, AXES, odd_swap)
         first = lax.ppermute(first, "dom", even_swap)
         blocks = []
         for k in range(1, n_sub):
             blocks.append(lax.ppermute(image, "sub", [(i, i ^ k) for i in range(n_sub)]))
         return blocks, first, second
 
-    right, image, first, second, p_high, p_low, basis, compact, weights, fresh = call(
+    copied = (
+        basis, compact, weights, fresh, pattern, c_rows.reshape(1, slots), c_side.reshape(1, slots),
+        shifts, mass, k_tiles, c_tiles,
+    )
+    (right, image, first, second, p_high, p_low, *copied) = call(
         start_kernel,
-        (vec, vec, edge, edge, p_part, p_part, shape_of(basis), shape_of(compact), shape_of(weights), shape_of(fresh)),
-        [hbm()] * 5,
+        (vec, vec, edge, edge, p_part, p_part)
+        + tuple(pltpu.VMEM(array.shape, array.dtype) for array in copied),
+        [hbm()] * (len(copied) + 1),
         [
             wide(p_blocks),
             pltpu.VMEM(precond.shape, F32),
-            pltpu.SemaphoreType.DMA((4,)),
+            pltpu.SemaphoreType.DMA((len(copied),)),
             pltpu.SemaphoreType.DMA((tiles,)),
         ],
-        in_hbm(basis, compact, weights, fresh, precond),
-    )
-    k_high, k_low, c_high, c_low, pick_table, below, above, inner, drag = call(
+        in_hbm(*copied, precond),
+    )
+    basis, compact, weights, fresh = copied[:4]
+    k_high, k_low, c_high, c_low, pick_table, below, above, drag = call(
         functools.partial(prepare_kernel, n_dom),
-        (k_part, k_part, c_part, c_part, pick, mask, mask, square, drag),
-        [hbm()] * 3 + [smem()] + [hbm()] * 4 + [vmem()],
-        [
-            pltpu.VMEM(k_tiles.shape, F32),
-            pltpu.VMEM(c_tiles.shape, F32),
-            pltpu.VMEM(mass.shape, F32),
-            pltpu.SMEM(pattern.shape, jnp.int32),
-            pltpu.SMEM(c_rows.shape, jnp.int32),
-            pltpu.SMEM(c_side.shape, jnp.int32),
-            pltpu.SMEM(shifts.shape, F32),
-            pltpu.SemaphoreType.DMA((6,)),
-            pltpu.SemaphoreType.DMA((tiles,)),
-        ],
-        in_hbm(pattern, c_rows, c_side)
-        + (c_count,)
-        + in_hbm(shifts, mass, k_tiles, c_tiles)
-        + (basis,),
+        (k_part, k_part, c_part, c_part, pick, mask, mask, drag),
+        [smem()] + [vmem()] * 7, [], (c_count, *copied[4:]),
     )
     previous = zero
     for step in range(steps):
@@ -661,16 +681,23 @@
         images, results = [image], []
         for index in range(ITERS):
             blocks, first_in, second_in = exchange(image, first, second)
+            ahead = ()
+            if step == 0 and index == ITERS - 2:
+                inner = call(inner_kernel, square, [vmem()] * 2, [], (basis, image))
+                ahead = (inner,)
             partial = call(
-                functools.partial(stiff_kernel, step), vec, [vmem()] * (n_sub + 4),
-                [wide(k_blocks)], (image, *blocks, drag, k_high, k_low, pick_table),
+                functools.partial(stiff_kernel, step, n_sub - 1), vec,
+                [vmem()] * (n_sub + 4 + len(ahead)), [wide(k_blocks)],
+                (image, *blocks, drag, k_high, k_low, pick_table, *ahead),
             )
             common = (partial, first_in, second_in, c_high, c_low, below, above)
             if index + 1 < ITERS:
-                result, term, image, first, second = call(
-                    level_kernel, (vec, vec, vec, edge, edge), [vmem()] * 10,
+                later = [vec] if index + 2 < ITERS else []
+                result, image, first, second, *later = call(
+                    level_kernel, (vec, vec, edge, edge, *later), [vmem()] * 10,
                     [wide(max(slots, p_blocks))], common + (term, p_high, p_low),
                 )
+                term = later[0] if later else None
                 results.append(result)
                 images.append(image)
             else:
@@ -679,8 +706,10 @@
                     [pltpu.VMEM((tiles, 4 * tiles, tile), F32)],
                     (basis, previous, inner, *results, right, *images),
                 )
+                fold = FOLD if step + 1 == steps else 1
                 payload = call(
-                    last_kernel, jax.ShapeDtypeStruct((devices, tiles, tile), F32),
+                    functools.partial(last_kernel, fold),
+                    jax.ShapeDtypeStruct((devices, tiles // fold, tile), F32),
                     [vmem()] * (8 + ITERS), [wide(slots)], common + (sums, *results, right),
                 )
         sums = lax.all_to_all(payload, AXES, 0, 0)

time: 87.5 us -> 77.6 us (0.89)
  waiting for transfers between devices: 15.2 us -> 3.89 us
  blocking collectives: 22.4 us -> 28.7 us
  starting transfers between devices: 30.6 us -> 27.4 us
  Pallas kernels: 17.7 us -> 15.9 us
    ppermute x6, starting transfers between devices: 15.1 us -> 0.47 us  [exchange(): second = lax.ppermute(second, AXES, odd_swap)]
    ppermute x6, waiting for transfers between devices: 14.1 us -> 0.02 us  [exchange(): second = lax.ppermute(second, AXES, odd_swap)]
    ppermute x6, starting transfers between devices: 2.89 us -> 14.2 us  [exchange(): first = lax.ppermute(first, 'dom', even_swap)]
    all_to_all x2, blocking collectives: 22.4 us -> 28.7 us  [local(): sums = lax.all_to_all(payload, AXES, 0, 0)]
    pallas_call x18 -> x19, Pallas kernels: 17.7 us -> 15.9 us  [call(): pl.pallas_call(kernel, out_shape=out_shape, in_specs=in_specs, out_specs=...]
    ppermute x6, waiting for transfers between devices: 1.01 us -> 2.55 us  [exchange(): first = lax.ppermute(first, 'dom', even_swap)]
    ppermute x18, waiting for transfers between devices: 0.06 us -> 1.32 us  [exchange(): lax.ppermute(image, 'sub', [(i, i ^ k) for i in range(n_sub)])]
  transfers between devices with their start and end apart: 30 -> 30, of which waited for: 7 -> 6; matrix products, arithmetic and copies ran while one was open for 0% -> 0% of each run, Pallas kernels for 9% -> 8%
where the time goes in v2:
time: 77.6 us; the launch traced here: 77.4 us
  blocking collectives  28.7 us (37%)
  starting transfers between devices  27.4 us (35%)
  Pallas kernels  15.9 us (20%)
  waiting for transfers between devices  3.89 us (5%)
  between operations  1.45 us (2%)
    all_to_all x2, blocking collectives, local(): sums = lax.all_to_all(payload, AXES, 0, 0)  28.7 us
    pallas_call x19, Pallas kernels, call(): pl.pallas_call(kernel, out_shape=out_shape, in_specs=in_specs, out_specs=...  15.9 us
    ppermute x6, starting transfers between devices, exchange(): first = lax.ppermute(first, 'dom', even_swap)  14.2 us
    ppermute x18, starting transfers between devices, exchange(): lax.ppermute(image, 'sub', [(i, i ^ k) for i in range(n_sub)])  12.7 us
    ppermute x6, waiting for transfers between devices, exchange(): first = lax.ppermute(first, 'dom', even_swap)  2.55 us
  transfers between devices with their start and end apart: 30, of which 6 were waited for; matrix products, arithmetic and copies ran while one was open for 0% of the time, Pallas kernels for 8%

profile of v2, /device:TPU:0, one launch (start us, length us, event | category | flops | bytes accessed | tf_op | source)
XLA Modules:
  0.0 77.4 jit_solution(11960839592723563194)
XLA Ops:
  0.6 2.5 %shard_map.140 = (f32[16,128]{1,0:T(8,128)S(1)}, f32[16,128]{1,0:T(8,128)S(1)}, f32[2,128]{1,0:T(2,128)S(1)}, f32[2,128]{1,0:T(2,128)S(1)}, bf16[128,2048]{1,0:T...) custom-call(f32[2,16,1024]{2,1,0:T(8,128)} %refs_0_.1, ...), custom_call_target="tpu_custom_call" | custom-call | flops 10000000 | bytes 1000000 | tf_op jit(solution)/shard_map/pallas_call | solution.py:586
  3.7 2.5 %collective-permute-start.1 = (f32[16,128]{1,0:T(8,128)S(1)}, f32[16,128]{1,0:T(8,128)S(1)}, u32[]{:S(2)}, u32[]{:S(2)}) collective-permute-start(f32[16,128]{1,0:T(8,128)S(1)} %get-tuple-element.52.image_ref.refs_3_.refs_0_), channel_id=1, source_target_pairs={{0,2},{1,3},{2,0},{3,1},{4,6},{5,7},{6,4},{7,5},{8,10},{9,11},{10,... | collective-permute-start | bytes 24584 | tf_op jit(solution)/shard_map/ppermute | solution.py:652
  6.3 1.8 %collective-permute-start.3 = (f32[2,128]{1,0:T(2,128)S(1)}, f32[2,128]{1,0:T(2,128)S(1)}, u32[]{:S(2)}, u32[]{:S(2)}) collective-permute-start(f32[2,128]{1,0:T(2,128)S(1)} %get-tuple-element.64), channel_id=1, source_target_pairs={{0,4},{4,0},{8,12},{12,8},{16,20},{20,16},{24,28},{28,24},{1,5},{5... | collective-permute-start | bytes 3080 | tf_op jit(solution)/shard_map/ppermute | solution.py:649
  10.2 1.1 %shard_map.143 = (f32[16,128]{1,0:T(8,128)S(1)}, f32[16,128]{1,0:T(8,128)S(1)}, f32[2,128]{1,0:T(2,128)S(1)}, f32[2,128]{1,0:T(2,128)S(1)}, f32[16,128]{1,0:T(8,128)S(1)}) custom-call(f32[16,128]{1,0:T(8,128)S(1)} %shard_map.142.partial_ref, f32[2,128]{1,0:T(2,128)S(1)} %collective-permute-done.3.first_in, f32[2,128]{1,0:T(2,128)S(1)} %collective-permute-done.4.second_in, ...), custom_call_target="tpu_custom_call" | custom-call | flops 10000000 | bytes 1000000 | tf_op jit(solution)/shard_map/pallas_call | solution.py:586
  11.8 1.5 %collective-permute-start.6 = (f32[16,128]{1,0:T(8,128)S(1)}, f32[16,128]{1,0:T(8,128)S(1)}, u32[]{:S(2)}, u32[]{:S(2)}) collective-permute-start(f32[16,128]{1,0:T(8,128)S(1)} %get-tuple-element.73.after_ref.image_ref.refs_4_.refs_1_), channel_id=1, source_target_pairs={{0,2},{1,3},{2,0},{3,1},{4,6},{5,7},{6,4},{7,5},{8,10},{9,11},{10,... | collective-permute-start | bytes 24584 | tf_op jit(solution)/shard_map/ppermute | solution.py:652
  13.3 2.9 %collective-permute-start.8 = (f32[2,128]{1,0:T(2,128)S(1)}, f32[2,128]{1,0:T(2,128)S(1)}, u32[]{:S(2)}, u32[]{:S(2)}) collective-permute-start(f32[2,128]{1,0:T(2,128)S(1)} %get-tuple-element.75), channel_id=1, source_target_pairs={{0,4},{4,0},{8,12},{12,8},{16,20},{20,16},{24,28},{28,24},{1,5},{5... | collective-permute-start | bytes 3080 | tf_op jit(solution)/shard_map/ppermute | solution.py:649
  17.7 1.1 %shard_map.146 = (f32[16,128]{1,0:T(8,128)S(1)}, f32[16,128]{1,0:T(8,128)S(1)}, f32[2,128]{1,0:T(2,128)S(1)}, f32[2,128]{1,0:T(2,128)S(1)}) custom-call(f32[16,128]{1,0:T(8,128)S(1)} %shard_map.145.partial_ref, f32[2,128]{1,0:T(2,128)S(1)} %collective-permute-done.8.first_in, f32[2,128]{1,0:T(2,128)S(1)} %collective-permute-done.9.second_in, ...), custom_call_target="tpu_custom_call" | custom-call | flops 10000000 | bytes 1000000 | tf_op jit(solution)/shard_map/pallas_call | solution.py:586
  18.9 1.5 %collective-permute-start.11 = (f32[16,128]{1,0:T(8,128)S(1)}, f32[16,128]{1,0:T(8,128)S(1)}, u32[]{:S(2)}, u32[]{:S(2)}) collective-permute-start(f32[16,128]{1,0:T(8,128)S(1)} %get-tuple-element.78.image_ref.refs_5_.refs_2_), channel_id=1, source_target_pairs={{0,2},{1,3},{2,0},{3,1},{4,6},{5,7},{6,4},{7,5},{8,10},{9,11},{10,... | collective-permute-start | bytes 24584 | tf_op jit(solution)/shard_map/ppermute | solution.py:652
  20.7 3.0 %collective-permute-start.13 = (f32[2,128]{1,0:T(2,128)S(1)}, f32[2,128]{1,0:T(2,128)S(1)}, u32[]{:S(2)}, u32[]{:S(2)}) collective-permute-start(f32[2,128]{1,0:T(2,128)S(1)} %get-tuple-element.79), channel_id=1, source_target_pairs={{0,4},{4,0},{8,12},{12,8},{16,20},{20,16},{24,28},{28,24},{1,5},{5... | collective-permute-start | bytes 3080 | tf_op jit(solution)/shard_map/ppermute | solution.py:649
  25.9 16.1 %all_to_all.10.sums_ref = f32[32,8,128]{2,1,0:T(8,128)S(1)} all-to-all(f32[32,8,128]{2,1,0:T(8,128)S(1)} %shard_map.149), channel_id=1, replica_groups=mesh['dom'=8,'sub'=4] {'dom','sub'}, dimensions={0} | all-to-all | bytes 262144 | tf_op jit(solution)/shard_map/all_to_all | solution.py:715
  42.0 0.8 shard_map.150
  43.4 1.3 %collective-permute-start.17 = (f32[16,128]{1,0:T(8,128)S(1)}, f32[16,128]{1,0:T(8,128)S(1)}, u32[]{:S(2)}, u32[]{:S(2)}) collective-permute-start(f32[16,128]{1,0:T(8,128)S(1)} %get-tuple-element.86.image_ref.refs_3_.refs_0_), channel_id=1, source_target_pairs={{0,3},{1,2},{2,1},{3,0},{4,7},{5,6},{6,5},{7,4},{8,11},{9,10},{10,... | collective-permute-start | bytes 24584 | tf_op jit(solution)/shard_map/ppermute | solution.py:652
  45.4 1.3 %collective-permute-done.16.refs_1_ = f32[16,128]{1,0:T(8,128)S(1)} collective-permute-done((f32[16,128]{1,0:T(8,128)S(1)}, f32[16,128]{1,0:T(8,128)S(1)}, u32[]{:S(2)}, u32[]{:S(2)}) %collective-permute-start.16) | collective-permute-done | bytes 8224 | tf_op jit(solution)/shard_map/ppermute | solution.py:652
  47.4 0.8 %collective-permute-done.18.first_in = f32[2,128]{1,0:T(2,128)S(1)} collective-permute-done((f32[2,128]{1,0:T(2,128)S(1)}, f32[2,128]{1,0:T(2,128)S(1)}, u32[]{:S(2)}, u32[]{:S(2)}) %collective-permute-start.18) | collective-permute-done | bytes 1056 | tf_op jit(solution)/shard_map/ppermute | solution.py:649
  48.3 1.1 %shard_map.152 = (f32[16,128]{1,0:T(8,128)S(1)}, f32[16,128]{1,0:T(8,128)S(1)}, f32[2,128]{1,0:T(2,128)S(1)}, f32[2,128]{1,0:T(2,128)S(1)}, f32[16,128]{1,0:T(8,128)S(1)}) custom-call(f32[16,128]{1,0:T(8,128)S(1)} %shard_map.151.partial_ref, f32[2,128]{1,0:T(2,128)S(1)} %collective-permute-done.18.first_in, f32[2,128]{1,0:T(2,128)S(1)} %collective-permute-done.19.second_in, ...), custom_call_target="tpu_custom_call" | custom-call | flops 10000000 | bytes 1000000 | tf_op jit(solution)/shard_map/pallas_call | solution.py:586
  49.4 0.7 collective-permute-start.21
  50.1 1.1 %collective-permute-start.22 = (f32[16,128]{1,0:T(8,128)S(1)}, f32[16,128]{1,0:T(8,128)S(1)}, u32[]{:S(2)}, u32[]{:S(2)}) collective-permute-start(f32[16,128]{1,0:T(8,128)S(1)} %get-tuple-element.90.image_ref.refs_4_.refs_1_), channel_id=1, source_target_pairs={{0,3},{1,2},{2,1},{3,0},{4,7},{5,6},{6,5},{7,4},{8,11},{9,10},{10,... | collective-permute-start | bytes 24584 | tf_op jit(solution)/shard_map/ppermute | solution.py:652
  51.2 2.9 %collective-permute-start.23 = (f32[2,128]{1,0:T(2,128)S(1)}, f32[2,128]{1,0:T(2,128)S(1)}, u32[]{:S(2)}, u32[]{:S(2)}) collective-permute-start(f32[2,128]{1,0:T(2,128)S(1)} %get-tuple-element.91), channel_id=1, source_target_pairs={{0,4},{4,0},{8,12},{12,8},{16,20},{20,16},{24,28},{28,24},{1,5},{5... | collective-permute-start | bytes 3080 | tf_op jit(solution)/shard_map/ppermute | solution.py:649
  55.0 0.7 collective-permute-done.23.first_in
  55.7 1.1 %shard_map.154 = (f32[16,128]{1,0:T(8,128)S(1)}, f32[16,128]{1,0:T(8,128)S(1)}, f32[2,128]{1,0:T(2,128)S(1)}, f32[2,128]{1,0:T(2,128)S(1)}) custom-call(f32[16,128]{1,0:T(8,128)S(1)} %shard_map.153.partial_ref, f32[2,128]{1,0:T(2,128)S(1)} %collective-permute-done.23.first_in, f32[2,128]{1,0:T(2,128)S(1)} %collective-permute-done.24.second_in, ...), custom_call_target="tpu_custom_call" | custom-call | flops 10000000 | bytes 1000000 | tf_op jit(solution)/shard_map/pallas_call | solution.py:586
  57.3 1.4 %collective-permute-start.27 = (f32[16,128]{1,0:T(8,128)S(1)}, f32[16,128]{1,0:T(8,128)S(1)}, u32[]{:S(2)}, u32[]{:S(2)}) collective-permute-start(f32[16,128]{1,0:T(8,128)S(1)} %get-tuple-element.94.image_ref.refs_5_.refs_2_), channel_id=1, source_target_pairs={{0,3},{1,2},{2,1},{3,0},{4,7},{5,6},{6,5},{7,4},{8,11},{9,10},{10,... | collective-permute-start | bytes 24584 | tf_op jit(solution)/shard_map/ppermute | solution.py:652
  58.7 2.9 %collective-permute-start.28 = (f32[2,128]{1,0:T(2,128)S(1)}, f32[2,128]{1,0:T(2,128)S(1)}, u32[]{:S(2)}, u32[]{:S(2)}) collective-permute-start(f32[2,128]{1,0:T(2,128)S(1)} %get-tuple-element.95), channel_id=1, source_target_pairs={{0,4},{4,0},{8,12},{12,8},{16,20},{20,16},{24,28},{28,24},{1,5},{5... | collective-permute-start | bytes 3080 | tf_op jit(solution)/shard_map/ppermute | solution.py:649
  63.8 12.6 %all_to_all.11.sums_ref = f32[32,2,128]{2,1,0:T(2,128)S(1)} all-to-all(f32[32,2,128]{2,1,0:T(2,128)S(1)} %shard_map.157), channel_id=1, replica_groups=mesh['dom'=8,'sub'=4] {'dom','sub'}, dimensions={0} | all-to-all | bytes 65536 | tf_op jit(solution)/shard_map/all_to_all | solution.py:715
  76.4 1.0 %shard_map.158 = (f32[2,2,1024]{2,1,0:T(2,128)}, f32[2,2,18]{2,1,0:T(2,128)}) custom-call(f32[32,2,128]{2,1,0:T(2,128)S(1)} %all_to_all.11.sums_ref, f32[8,128]{1,0:T(8,128)S(1)} %get-tuple-element.100.inner_ref, f32[2,16,1024]{2,1,0:T(8,128)S(1)} %get-tuple-element.74.basis_ref, f32[16,128]{1,0:T(8,128)S(1)} %get-tuple-element.86.image_ref.refs_3_.refs_0_, ...), custom_call_target="tpu_custom_call" | custom-call | flops 10000000 | bytes 1000000 | tf_op jit(solution)/shard_map/pallas_call | solution.py:586
  (58 shorter events, 12.2 us)
Async XLA Ops:
  3.2 6.2 %collective-permute-start = (f32[16,128]{1,0:T(8,128)S(1)}, f32[16,128]{1,0:T(8,128)S(1)}, u32[]{:S(2)}, u32[]{:S(2)}) collective-permute-start(f32[16,128]{1,0:T(8,128)S(1)} %get-tuple-element.52.image_ref.refs_3_.refs_0_), channel_id=1, source_target_pairs={{0,1},{1,0},{2,3},{3,2},{4,5},{5,4},{6,7},{7,6},{8,9},{9,8},{10,11... | collective-permute-start | bytes 24584 | tf_op jit(solution)/shard_map/ppermute | solution.py:652
  3.7 5.7 %collective-permute-start.1 = (f32[16,128]{1,0:T(8,128)S(1)}, f32[16,128]{1,0:T(8,128)S(1)}, u32[]{:S(2)}, u32[]{:S(2)}) collective-permute-start(f32[16,128]{1,0:T(8,128)S(1)} %get-tuple-element.52.image_ref.refs_3_.refs_0_), channel_id=1, source_target_pairs={{0,2},{1,3},{2,0},{3,1},{4,6},{5,7},{6,4},{7,5},{8,10},{9,11},{10,... | collective-permute-start | bytes 24584 | tf_op jit(solution)/shard_map/ppermute | solution.py:652
  6.3 3.2 %collective-permute-start.2 = (f32[16,128]{1,0:T(8,128)S(1)}, f32[16,128]{1,0:T(8,128)S(1)}, u32[]{:S(2)}, u32[]{:S(2)}) collective-permute-start(f32[16,128]{1,0:T(8,128)S(1)} %get-tuple-element.52.image_ref.refs_3_.refs_0_), channel_id=1, source_target_pairs={{0,3},{1,2},{2,1},{3,0},{4,7},{5,6},{6,5},{7,4},{8,11},{9,10},{10,... | collective-permute-start | bytes 24584 | tf_op jit(solution)/shard_map/ppermute | solution.py:652
  6.3 3.9 %collective-permute-start.3 = (f32[2,128]{1,0:T(2,128)S(1)}, f32[2,128]{1,0:T(2,128)S(1)}, u32[]{:S(2)}, u32[]{:S(2)}) collective-permute-start(f32[2,128]{1,0:T(2,128)S(1)} %get-tuple-element.64), channel_id=1, source_target_pairs={{0,4},{4,0},{8,12},{12,8},{16,20},{20,16},{24,28},{28,24},{1,5},{5... | collective-permute-start | bytes 3080 | tf_op jit(solution)/shard_map/ppermute | solution.py:649
  11.3 5.3 %collective-permute-start.5 = (f32[16,128]{1,0:T(8,128)S(1)}, f32[16,128]{1,0:T(8,128)S(1)}, u32[]{:S(2)}, u32[]{:S(2)}) collective-permute-start(f32[16,128]{1,0:T(8,128)S(1)} %get-tuple-element.73.after_ref.image_ref.refs_4_.refs_1_), channel_id=1, source_target_pairs={{0,1},{1,0},{2,3},{3,2},{4,5},{5,4},{6,7},{7,6},{8,9},{9,8},{10,11... | collective-permute-start | bytes 24584 | tf_op jit(solution)/shard_map/ppermute | solution.py:652
  11.8 4.9 %collective-permute-start.6 = (f32[16,128]{1,0:T(8,128)S(1)}, f32[16,128]{1,0:T(8,128)S(1)}, u32[]{:S(2)}, u32[]{:S(2)}) collective-permute-start(f32[16,128]{1,0:T(8,128)S(1)} %get-tuple-element.73.after_ref.image_ref.refs_4_.refs_1_), channel_id=1, source_target_pairs={{0,2},{1,3},{2,0},{3,1},{4,6},{5,7},{6,4},{7,5},{8,10},{9,11},{10,... | collective-permute-start | bytes 24584 | tf_op jit(solution)/shard_map/ppermute | solution.py:652
  13.3 3.4 %collective-permute-start.7 = (f32[16,128]{1,0:T(8,128)S(1)}, f32[16,128]{1,0:T(8,128)S(1)}, u32[]{:S(2)}, u32[]{:S(2)}) collective-permute-start(f32[16,128]{1,0:T(8,128)S(1)} %get-tuple-element.73.after_ref.image_ref.refs_4_.refs_1_), channel_id=1, source_target_pairs={{0,3},{1,2},{2,1},{3,0},{4,7},{5,6},{6,5},{7,4},{8,11},{9,10},{10,... | collective-permute-start | bytes 24584 | tf_op jit(solution)/shard_map/ppermute | solution.py:652
  13.3 4.4 %collective-permute-start.8 = (f32[2,128]{1,0:T(2,128)S(1)}, f32[2,128]{1,0:T(2,128)S(1)}, u32[]{:S(2)}, u32[]{:S(2)}) collective-permute-start(f32[2,128]{1,0:T(2,128)S(1)} %get-tuple-element.75), channel_id=1, source_target_pairs={{0,4},{4,0},{8,12},{12,8},{16,20},{20,16},{24,28},{28,24},{1,5},{5... | collective-permute-start | bytes 3080 | tf_op jit(solution)/shard_map/ppermute | solution.py:649
  18.8 5.4 %collective-permute-start.10 = (f32[16,128]{1,0:T(8,128)S(1)}, f32[16,128]{1,0:T(8,128)S(1)}, u32[]{:S(2)}, u32[]{:S(2)}) collective-permute-start(f32[16,128]{1,0:T(8,128)S(1)} %get-tuple-element.78.image_ref.refs_5_.refs_2_), channel_id=1, source_target_pairs={{0,1},{1,0},{2,3},{3,2},{4,5},{5,4},{6,7},{7,6},{8,9},{9,8},{10,11... | collective-permute-start | bytes 24584 | tf_op jit(solution)/shard_map/ppermute | solution.py:652
  18.9 5.3 %collective-permute-start.11 = (f32[16,128]{1,0:T(8,128)S(1)}, f32[16,128]{1,0:T(8,128)S(1)}, u32[]{:S(2)}, u32[]{:S(2)}) collective-permute-start(f32[16,128]{1,0:T(8,128)S(1)} %get-tuple-element.78.image_ref.refs_5_.refs_2_), channel_id=1, source_target_pairs={{0,2},{1,3},{2,0},{3,1},{4,6},{5,7},{6,4},{7,5},{8,10},{9,11},{10,... | collective-permute-start | bytes 24584 | tf_op jit(solution)/shard_map/ppermute | solution.py:652
  20.4 3.8 %collective-permute-start.12 = (f32[16,128]{1,0:T(8,128)S(1)}, f32[16,128]{1,0:T(8,128)S(1)}, u32[]{:S(2)}, u32[]{:S(2)}) collective-permute-start(f32[16,128]{1,0:T(8,128)S(1)} %get-tuple-element.78.image_ref.refs_5_.refs_2_), channel_id=1, source_target_pairs={{0,3},{1,2},{2,1},{3,0},{4,7},{5,6},{6,5},{7,4},{8,11},{9,10},{10,... | collective-permute-start | bytes 24584 | tf_op jit(solution)/shard_map/ppermute | solution.py:652
  20.7 4.6 %collective-permute-start.13 = (f32[2,128]{1,0:T(2,128)S(1)}, f32[2,128]{1,0:T(2,128)S(1)}, u32[]{:S(2)}, u32[]{:S(2)}) collective-permute-start(f32[2,128]{1,0:T(2,128)S(1)} %get-tuple-element.79), channel_id=1, source_target_pairs={{0,4},{4,0},{8,12},{12,8},{16,20},{20,16},{24,28},{28,24},{1,5},{5... | collective-permute-start | bytes 3080 | tf_op jit(solution)/shard_map/ppermute | solution.py:649
  43.0 3.7 %collective-permute-start.16 = (f32[16,128]{1,0:T(8,128)S(1)}, f32[16,128]{1,0:T(8,128)S(1)}, u32[]{:S(2)}, u32[]{:S(2)}) collective-permute-start(f32[16,128]{1,0:T(8,128)S(1)} %get-tuple-element.86.image_ref.refs_3_.refs_0_), channel_id=1, source_target_pairs={{0,2},{1,3},{2,0},{3,1},{4,6},{5,7},{6,4},{7,5},{8,10},{9,11},{10,... | collective-permute-start | bytes 24584 | tf_op jit(solution)/shard_map/ppermute | solution.py:652
  43.4 3.3 %collective-permute-start.17 = (f32[16,128]{1,0:T(8,128)S(1)}, f32[16,128]{1,0:T(8,128)S(1)}, u32[]{:S(2)}, u32[]{:S(2)}) collective-permute-start(f32[16,128]{1,0:T(8,128)S(1)} %get-tuple-element.86.image_ref.refs_3_.refs_0_), channel_id=1, source_target_pairs={{0,3},{1,2},{2,1},{3,0},{4,7},{5,6},{6,5},{7,4},{8,11},{9,10},{10,... | collective-permute-start | bytes 24584 | tf_op jit(solution)/shard_map/ppermute | solution.py:652
  44.7 3.6 %collective-permute-start.18 = (f32[2,128]{1,0:T(2,128)S(1)}, f32[2,128]{1,0:T(2,128)S(1)}, u32[]{:S(2)}, u32[]{:S(2)}) collective-permute-start(f32[2,128]{1,0:T(2,128)S(1)} %get-tuple-element.87), channel_id=1, source_target_pairs={{0,4},{4,0},{8,12},{12,8},{16,20},{20,16},{24,28},{28,24},{1,5},{5... | collective-permute-start | bytes 3080 | tf_op jit(solution)/shard_map/ppermute | solution.py:649
  45.3 2.9 %collective-permute-start.19 = (f32[2,128]{1,0:T(2,128)S(1)}, f32[2,128]{1,0:T(2,128)S(1)}, u32[]{:S(2)}, u32[]{:S(2)}) collective-permute-start(f32[2,128]{1,0:T(2,128)S(1)} %get-tuple-element.88), channel_id=1, source_target_pairs={{0,1},{1,0},{2,3},{3,2},{4,8},{5,9},{6,10},{7,11},{8,4},{9,5},{10,... | collective-permute-start | bytes 3080 | tf_op jit(solution)/shard_map/ppermute | solution.py:648
  49.3 4.9 %collective-permute-start.20 = (f32[16,128]{1,0:T(8,128)S(1)}, f32[16,128]{1,0:T(8,128)S(1)}, u32[]{:S(2)}, u32[]{:S(2)}) collective-permute-start(f32[16,128]{1,0:T(8,128)S(1)} %get-tuple-element.90.image_ref.refs_4_.refs_1_), channel_id=1, source_target_pairs={{0,1},{1,0},{2,3},{3,2},{4,5},{5,4},{6,7},{7,6},{8,9},{9,8},{10,11... | collective-permute-start | bytes 24584 | tf_op jit(solution)/shard_map/ppermute | solution.py:652
  49.4 4.9 %collective-permute-start.21 = (f32[16,128]{1,0:T(8,128)S(1)}, f32[16,128]{1,0:T(8,128)S(1)}, u32[]{:S(2)}, u32[]{:S(2)}) collective-permute-start(f32[16,128]{1,0:T(8,128)S(1)} %get-tuple-element.90.image_ref.refs_4_.refs_1_), channel_id=1, source_target_pairs={{0,2},{1,3},{2,0},{3,1},{4,6},{5,7},{6,4},{7,5},{8,10},{9,11},{10,... | collective-permute-start | bytes 24584 | tf_op jit(solution)/shard_map/ppermute | solution.py:652
  50.1 4.1 %collective-permute-start.22 = (f32[16,128]{1,0:T(8,128)S(1)}, f32[16,128]{1,0:T(8,128)S(1)}, u32[]{:S(2)}, u32[]{:S(2)}) collective-permute-start(f32[16,128]{1,0:T(8,128)S(1)} %get-tuple-element.90.image_ref.refs_4_.refs_1_), channel_id=1, source_target_pairs={{0,3},{1,2},{2,1},{3,0},{4,7},{5,6},{6,5},{7,4},{8,11},{9,10},{10,... | collective-permute-start | bytes 24584 | tf_op jit(solution)/shard_map/ppermute | solution.py:652
  51.2 4.5 %collective-permute-start.23 = (f32[2,128]{1,0:T(2,128)S(1)}, f32[2,128]{1,0:T(2,128)S(1)}, u32[]{:S(2)}, u32[]{:S(2)}) collective-permute-start(f32[2,128]{1,0:T(2,128)S(1)} %get-tuple-element.91), channel_id=1, source_target_pairs={{0,4},{4,0},{8,12},{12,8},{16,20},{20,16},{24,28},{28,24},{1,5},{5... | collective-permute-start | bytes 3080 | tf_op jit(solution)/shard_map/ppermute | solution.py:649
  56.8 5.3 %collective-permute-start.25 = (f32[16,128]{1,0:T(8,128)S(1)}, f32[16,128]{1,0:T(8,128)S(1)}, u32[]{:S(2)}, u32[]{:S(2)}) collective-permute-start(f32[16,128]{1,0:T(8,128)S(1)} %get-tuple-element.94.image_ref.refs_5_.refs_2_), channel_id=1, source_target_pairs={{0,1},{1,0},{2,3},{3,2},{4,5},{5,4},{6,7},{7,6},{8,9},{9,8},{10,11... | collective-permute-start | bytes 24584 | tf_op jit(solution)/shard_map/ppermute | solution.py:652
  56.8 5.2 %collective-permute-start.26 = (f32[16,128]{1,0:T(8,128)S(1)}, f32[16,128]{1,0:T(8,128)S(1)}, u32[]{:S(2)}, u32[]{:S(2)}) collective-permute-start(f32[16,128]{1,0:T(8,128)S(1)} %get-tuple-element.94.image_ref.refs_5_.refs_2_), channel_id=1, source_target_pairs={{0,2},{1,3},{2,0},{3,1},{4,6},{5,7},{6,4},{7,5},{8,10},{9,11},{10,... | collective-permute-start | bytes 24584 | tf_op jit(solution)/shard_map/ppermute | solution.py:652
  57.3 4.8 %collective-permute-start.27 = (f32[16,128]{1,0:T(8,128)S(1)}, f32[16,128]{1,0:T(8,128)S(1)}, u32[]{:S(2)}, u32[]{:S(2)}) collective-permute-start(f32[16,128]{1,0:T(8,128)S(1)} %get-tuple-element.94.image_ref.refs_5_.refs_2_), channel_id=1, source_target_pairs={{0,3},{1,2},{2,1},{3,0},{4,7},{5,6},{6,5},{7,4},{8,11},{9,10},{10,... | collective-permute-start | bytes 24584 | tf_op jit(solution)/shard_map/ppermute | solution.py:652
  58.7 4.5 %collective-permute-start.28 = (f32[2,128]{1,0:T(2,128)S(1)}, f32[2,128]{1,0:T(2,128)S(1)}, u32[]{:S(2)}, u32[]{:S(2)}) collective-permute-start(f32[2,128]{1,0:T(2,128)S(1)} %get-tuple-element.95), channel_id=1, source_target_pairs={{0,4},{4,0},{8,12},{12,8},{16,20},{20,16},{24,28},{28,24},{1,5},{5... | collective-permute-start | bytes 3080 | tf_op jit(solution)/shard_map/ppermute | solution.py:649
  (6 other events, 11.0 us)

commit v3 on v2

--- a/solution.py
+++ b/solution.py
@@ -14,7 +14,7 @@
 NT_DIMS = (((1,), (1,)), ((), ()))
 LANES = 128
 COPIED = 11
-FOLD = 4
+FOLDS = (2, 4)
 VMEM_LIMIT = 12 * 1024 * 1024
 AXES = ("dom", "sub")
 
@@ -219,10 +219,23 @@
     real, imag = basis_ref[0], basis_ref[1]
     inner = nt_dot(real, jnp.concatenate([real, imag], axis=0), HIGH)
     inner = inner + nt_dot(imag, jnp.concatenate([imag, -real], axis=0), HIGH)
+    half = inner_ref.shape[0]
+    row, lane = iota((half, half), 0), iota((half, half), 1)
+
+    def block(left, right, part):
+        lanes = (2 * part + right) * half
+        return inner[left * half : (left + 1) * half, lanes : lanes + half]
+
+    low_real = block(1, 1, 0)
+    pieces = [
+        jnp.where(lane >= row, block(0, 0, 0), low_real),
+        jnp.where(lane > row, block(0, 0, 1), jnp.where(lane < row, block(1, 1, 1), low_real)),
+        block(0, 1, 0),
+        block(0, 1, 1),
+    ]
     inner_ref[...] = jnp.zeros(inner_ref.shape, F32)
-    half, wide = inner_ref.shape[0], inner.shape[1]
-    inner_ref[:, 4 * half : 4 * half + wide] = inner[:half]
-    inner_ref[:, 4 * half + wide : 4 * half + 2 * wide] = inner[half:]
+    for index, piece in enumerate(pieces):
+        inner_ref[:, (4 + index) * half : (5 + index) * half] = piece
 
 
 def stiff_kernel(step, others, image_ref, *refs):
@@ -385,8 +398,7 @@
             value = jnp.sum(jnp.sum(value, axis=0, keepdims=True), axis=1, keepdims=True)
             spot = (row == at_row) & (lane == base + part * count + at_col)
             total = jnp.where(spot, value, total)
-    if fold > 1:
-        total = pack(total, fold)
+    total = pack(total, fold)
 
     @pl.loop(0, payload_ref.shape[0])
     def _(device):
@@ -460,24 +472,44 @@
     extra = scale(value, 1.0 / total_rows)
 
     row, lane = iota(shape, 0), iota(shape, 1)
-    first = 4 * count
-    span = 4 * count
-    first_row = jnp.zeros(shape, F32)
-    second_row = jnp.zeros(shape, F32)
-    for block in range(2):
-        real, imag = projections[block]
-        at_real = (lane == first + block * count + row) | (lane == first + span + block * count + row)
-        at_imag = (lane == first + 2 * count + block * count + row) | (
-            lane == first + span + 2 * count + block * count + row
-        )
-        first_row = first_row + jnp.where(at_real, real, jnp.where(at_imag, -imag, 0.0))
-        second_row = second_row + jnp.where(at_real, imag, jnp.where(at_imag, real, 0.0))
-    first_row = jnp.sum(first_row, axis=0, keepdims=True)
-    second_row = jnp.sum(second_row, axis=0, keepdims=True)
-    upper = lane < first + span
-    real_col = jnp.where(upper, projections[0][0], projections[1][0])
-    imag_col = jnp.where(upper, projections[0][1], projections[1][1])
-    quad = jnp.sum(inner * (real_col * first_row + imag_col * second_row), axis=1, keepdims=True)
+    spot = lane - 4 * count
+    column_of = spot % count
+    zone = jnp.where((spot >= 0) & (spot < 4 * count), spot // count, 4)
+    spread = [
+        [
+            jnp.sum(jnp.where(column_of == row, part, 0.0), axis=0, keepdims=True)
+            for part in projections[block]
+        ]
+        for block in range(2)
+    ]
+
+    def real_weight(left, right):
+        return left[0] * right[0] + left[1] * right[1]
+
+    def imag_weight(left, right):
+        return left[1] * right[0] - left[0] * right[1]
+
+    first, second = projections
+    same = real_weight(second, spread[1])
+    upper, lower = column_of > row, column_of < row
+    zones = [
+        jnp.where(
+            lower,
+            2.0 * same,
+            jnp.where(upper, 2.0, 1.0) * real_weight(first, spread[0]),
+        ),
+        jnp.where(
+            upper,
+            2.0 * imag_weight(first, spread[0]),
+            jnp.where(lower, 2.0 * imag_weight(second, spread[1]), same),
+        ),
+        2.0 * real_weight(first, spread[1]),
+        2.0 * imag_weight(first, spread[1]),
+    ]
+    weight = jnp.zeros(shape, F32)
+    for index, value in enumerate(zones):
+        weight = jnp.where(zone == index, value, weight)
+    quad = jnp.sum(inner * weight, axis=1, keepdims=True)
     quad = jnp.broadcast_to(quad, shape)
     for block in range(2):
         base = block * count
@@ -536,7 +568,7 @@
     (right_ref, image_ref, first_ref, second_ref, latest_ref, coeffs_ref, inner_ref, wide_ref) = refs[
         ITERS + 1 :
     ]
-    sums = reduce_sums(sums_ref)
+    sums = unpack(reduce_sums(sums_ref), FOLDS[step])
     inner_ref[...] = sums
     latest, coeffs = settle(total_rows, sums, sums, basis_ref, images, load(previous_ref))
     save(latest_ref, latest)
@@ -552,7 +584,7 @@
 def finish_kernel(total_rows, sums_ref, inner_ref, basis_ref, *refs):
     images = [load(ref) for ref in refs[:ITERS]]
     previous_ref, before_ref, made_ref, listed_ref = refs[ITERS:]
-    sums = unpack(reduce_sums(sums_ref), FOLD)
+    sums = unpack(reduce_sums(sums_ref), FOLDS[-1])
     previous = load(previous_ref)
     latest, coeffs = settle(total_rows, sums, inner_ref[...], basis_ref, images, previous)
     for step, vector in enumerate((previous, latest)):
@@ -706,7 +738,7 @@
                     [pltpu.VMEM((tiles, 4 * tiles, tile), F32)],
                     (basis, previous, inner, *results, right, *images),
                 )
-                fold = FOLD if step + 1 == steps else 1
+                fold = FOLDS[step]
                 payload = call(
                     functools.partial(last_kernel, fold),
                     jax.ShapeDtypeStruct((devices, tiles // fold, tile), F32),

time: 77.6 us -> 76.8 us (0.990)
  blocking collectives: 28.7 us -> 27.8 us
    all_to_all x2, blocking collectives: 28.7 us -> 27.8 us  [local(): sums = lax.all_to_all(payload, AXES, 0, 0)]
where the time goes in v3:
time: 76.8 us; the launch traced here: 76.6 us
  blocking collectives  27.8 us (36%)
  starting transfers between devices  27.3 us (36%)
  Pallas kernels  16.1 us (21%)
  waiting for transfers between devices  3.89 us (5%)
  between operations  1.46 us (2%)
    all_to_all x2, blocking collectives, local(): sums = lax.all_to_all(payload, AXES, 0, 0)  27.8 us
    pallas_call x19, Pallas kernels, call(): pl.pallas_call(kernel, out_shape=out_shape, in_specs=in_specs, out_specs=...  16.1 us
    ppermute x6, starting transfers between devices, exchange(): first = lax.ppermute(first, 'dom', even_swap)  14.1 us
    ppermute x18, starting transfers between devices, exchange(): lax.ppermute(image, 'sub', [(i, i ^ k) for i in range(n_sub)])  12.7 us
    ppermute x6, waiting for transfers between devices, exchange(): first = lax.ppermute(first, 'dom', even_swap)  2.58 us
  transfers between devices with their start and end apart: 30, of which 6 were waited for; matrix products, arithmetic and copies ran while one was open for 0% of the time, Pallas kernels for 8%

profile of v3, /device:TPU:0, one launch (start us, length us, event | category | flops | bytes accessed | tf_op | source)
XLA Modules:
  0.0 76.6 jit_solution(10709401974337097660)
XLA Ops:
  0.6 2.5 %shard_map.140 = (f32[16,128]{1,0:T(8,128)S(1)}, f32[16,128]{1,0:T(8,128)S(1)}, f32[2,128]{1,0:T(2,128)S(1)}, f32[2,128]{1,0:T(2,128)S(1)}, bf16[128,2048]{1,0:T...) custom-call(f32[2,16,1024]{2,1,0:T(8,128)} %refs_0_.1, ...), custom_call_target="tpu_custom_call" | custom-call | flops 10000000 | bytes 1000000 | tf_op jit(solution)/shard_map/pallas_call | solution.py:618
  3.7 2.5 %collective-permute-start.1 = (f32[16,128]{1,0:T(8,128)S(1)}, f32[16,128]{1,0:T(8,128)S(1)}, u32[]{:S(2)}, u32[]{:S(2)}) collective-permute-start(f32[16,128]{1,0:T(8,128)S(1)} %get-tuple-element.52.image_ref.refs_3_.refs_0_), channel_id=1, source_target_pairs={{0,2},{1,3},{2,0},{3,1},{4,6},{5,7},{6,4},{7,5},{8,10},{9,11},{10,... | collective-permute-start | bytes 24584 | tf_op jit(solution)/shard_map/ppermute | solution.py:684
  6.3 1.8 %collective-permute-start.3 = (f32[2,128]{1,0:T(2,128)S(1)}, f32[2,128]{1,0:T(2,128)S(1)}, u32[]{:S(2)}, u32[]{:S(2)}) collective-permute-start(f32[2,128]{1,0:T(2,128)S(1)} %get-tuple-element.64), channel_id=1, source_target_pairs={{0,4},{4,0},{8,12},{12,8},{16,20},{20,16},{24,28},{28,24},{1,5},{5... | collective-permute-start | bytes 3080 | tf_op jit(solution)/shard_map/ppermute | solution.py:681
  9.5 0.7 shard_map.142.partial_ref
  10.2 1.1 %shard_map.143 = (f32[16,128]{1,0:T(8,128)S(1)}, f32[16,128]{1,0:T(8,128)S(1)}, f32[2,128]{1,0:T(2,128)S(1)}, f32[2,128]{1,0:T(2,128)S(1)}, f32[16,128]{1,0:T(8,128)S(1)}) custom-call(f32[16,128]{1,0:T(8,128)S(1)} %shard_map.142.partial_ref, f32[2,128]{1,0:T(2,128)S(1)} %collective-permute-done.3.first_in, f32[2,128]{1,0:T(2,128)S(1)} %collective-permute-done.4.second_in, ...), custom_call_target="tpu_custom_call" | custom-call | flops 10000000 | bytes 1000000 | tf_op jit(solution)/shard_map/pallas_call | solution.py:618
  11.8 1.5 %collective-permute-start.6 = (f32[16,128]{1,0:T(8,128)S(1)}, f32[16,128]{1,0:T(8,128)S(1)}, u32[]{:S(2)}, u32[]{:S(2)}) collective-permute-start(f32[16,128]{1,0:T(8,128)S(1)} %get-tuple-element.73.after_ref.image_ref.refs_4_.refs_1_), channel_id=1, source_target_pairs={{0,2},{1,3},{2,0},{3,1},{4,6},{5,7},{6,4},{7,5},{8,10},{9,11},{10,... | collective-permute-start | bytes 24584 | tf_op jit(solution)/shard_map/ppermute | solution.py:684
  13.3 2.9 %collective-permute-start.8 = (f32[2,128]{1,0:T(2,128)S(1)}, f32[2,128]{1,0:T(2,128)S(1)}, u32[]{:S(2)}, u32[]{:S(2)}) collective-permute-start(f32[2,128]{1,0:T(2,128)S(1)} %get-tuple-element.75), channel_id=1, source_target_pairs={{0,4},{4,0},{8,12},{12,8},{16,20},{20,16},{24,28},{28,24},{1,5},{5... | collective-permute-start | bytes 3080 | tf_op jit(solution)/shard_map/ppermute | solution.py:681
  17.7 1.1 %shard_map.146 = (f32[16,128]{1,0:T(8,128)S(1)}, f32[16,128]{1,0:T(8,128)S(1)}, f32[2,128]{1,0:T(2,128)S(1)}, f32[2,128]{1,0:T(2,128)S(1)}) custom-call(f32[16,128]{1,0:T(8,128)S(1)} %shard_map.145.partial_ref, f32[2,128]{1,0:T(2,128)S(1)} %collective-permute-done.8.first_in, f32[2,128]{1,0:T(2,128)S(1)} %collective-permute-done.9.second_in, ...), custom_call_target="tpu_custom_call" | custom-call | flops 10000000 | bytes 1000000 | tf_op jit(solution)/shard_map/pallas_call | solution.py:618
  19.0 1.5 %collective-permute-start.11 = (f32[16,128]{1,0:T(8,128)S(1)}, f32[16,128]{1,0:T(8,128)S(1)}, u32[]{:S(2)}, u32[]{:S(2)}) collective-permute-start(f32[16,128]{1,0:T(8,128)S(1)} %get-tuple-element.78.image_ref.refs_5_.refs_2_), channel_id=1, source_target_pairs={{0,2},{1,3},{2,0},{3,1},{4,6},{5,7},{6,4},{7,5},{8,10},{9,11},{10,... | collective-permute-start | bytes 24584 | tf_op jit(solution)/shard_map/ppermute | solution.py:684
  20.7 3.0 %collective-permute-start.13 = (f32[2,128]{1,0:T(2,128)S(1)}, f32[2,128]{1,0:T(2,128)S(1)}, u32[]{:S(2)}, u32[]{:S(2)}) collective-permute-start(f32[2,128]{1,0:T(2,128)S(1)} %get-tuple-element.79), channel_id=1, source_target_pairs={{0,4},{4,0},{8,12},{12,8},{16,20},{20,16},{24,28},{28,24},{1,5},{5... | collective-permute-start | bytes 3080 | tf_op jit(solution)/shard_map/ppermute | solution.py:681
  25.9 15.4 %all_to_all.10.sums_ref = f32[32,4,128]{2,1,0:T(4,128)S(1)} all-to-all(f32[32,4,128]{2,1,0:T(4,128)S(1)} %shard_map.149), channel_id=1, replica_groups=mesh['dom'=8,'sub'=4] {'dom','sub'}, dimensions={0} | all-to-all | bytes 131072 | tf_op jit(solution)/shard_map/all_to_all | solution.py:747
  41.3 0.8 %shard_map.150 = (f32[16,128]{1,0:T(8,128)S(1)}, f32[16,128]{1,0:T(8,128)S(1)}, f32[2,128]{1,0:T(2,128)S(1)}, f32[2,128]{1,0:T(2,128)S(1)}, f32[16,128]{1,0:T(8,...) custom-call(f32[32,4,128]{2,1,0:T(4,128)S(1)} %all_to_all.10.sums_ref, ...), custom_call_target="tpu_custom_call" | custom-call | flops 10000000 | bytes 1000000 | tf_op jit(solution)/shard_map/pallas_call | solution.py:618
  42.7 1.3 %collective-permute-start.17 = (f32[16,128]{1,0:T(8,128)S(1)}, f32[16,128]{1,0:T(8,128)S(1)}, u32[]{:S(2)}, u32[]{:S(2)}) collective-permute-start(f32[16,128]{1,0:T(8,128)S(1)} %get-tuple-element.86.image_ref.refs_3_.refs_0_), channel_id=1, source_target_pairs={{0,3},{1,2},{2,1},{3,0},{4,7},{5,6},{6,5},{7,4},{8,11},{9,10},{10,... | collective-permute-start | bytes 24584 | tf_op jit(solution)/shard_map/ppermute | solution.py:684
  44.7 1.2 %collective-permute-done.16.refs_1_ = f32[16,128]{1,0:T(8,128)S(1)} collective-permute-done((f32[16,128]{1,0:T(8,128)S(1)}, f32[16,128]{1,0:T(8,128)S(1)}, u32[]{:S(2)}, u32[]{:S(2)}) %collective-permute-start.16) | collective-permute-done | bytes 8224 | tf_op jit(solution)/shard_map/ppermute | solution.py:684
  46.6 0.9 %collective-permute-done.18.first_in = f32[2,128]{1,0:T(2,128)S(1)} collective-permute-done((f32[2,128]{1,0:T(2,128)S(1)}, f32[2,128]{1,0:T(2,128)S(1)}, u32[]{:S(2)}, u32[]{:S(2)}) %collective-permute-start.18) | collective-permute-done | bytes 1056 | tf_op jit(solution)/shard_map/ppermute | solution.py:681
  47.6 1.1 %shard_map.152 = (f32[16,128]{1,0:T(8,128)S(1)}, f32[16,128]{1,0:T(8,128)S(1)}, f32[2,128]{1,0:T(2,128)S(1)}, f32[2,128]{1,0:T(2,128)S(1)}, f32[16,128]{1,0:T(8,128)S(1)}) custom-call(f32[16,128]{1,0:T(8,128)S(1)} %shard_map.151.partial_ref, f32[2,128]{1,0:T(2,128)S(1)} %collective-permute-done.18.first_in, f32[2,128]{1,0:T(2,128)S(1)} %collective-permute-done.19.second_in, ...), custom_call_target="tpu_custom_call" | custom-call | flops 10000000 | bytes 1000000 | tf_op jit(solution)/shard_map/pallas_call | solution.py:618
  49.3 1.2 %collective-permute-start.22 = (f32[16,128]{1,0:T(8,128)S(1)}, f32[16,128]{1,0:T(8,128)S(1)}, u32[]{:S(2)}, u32[]{:S(2)}) collective-permute-start(f32[16,128]{1,0:T(8,128)S(1)} %get-tuple-element.90.image_ref.refs_4_.refs_1_), channel_id=1, source_target_pairs={{0,3},{1,2},{2,1},{3,0},{4,7},{5,6},{6,5},{7,4},{8,11},{9,10},{10,... | collective-permute-start | bytes 24584 | tf_op jit(solution)/shard_map/ppermute | solution.py:684
  50.5 2.9 %collective-permute-start.23 = (f32[2,128]{1,0:T(2,128)S(1)}, f32[2,128]{1,0:T(2,128)S(1)}, u32[]{:S(2)}, u32[]{:S(2)}) collective-permute-start(f32[2,128]{1,0:T(2,128)S(1)} %get-tuple-element.91), channel_id=1, source_target_pairs={{0,4},{4,0},{8,12},{12,8},{16,20},{20,16},{24,28},{28,24},{1,5},{5... | collective-permute-start | bytes 3080 | tf_op jit(solution)/shard_map/ppermute | solution.py:681
  54.3 0.7 collective-permute-done.23.first_in
  55.0 1.1 %shard_map.154 = (f32[16,128]{1,0:T(8,128)S(1)}, f32[16,128]{1,0:T(8,128)S(1)}, f32[2,128]{1,0:T(2,128)S(1)}, f32[2,128]{1,0:T(2,128)S(1)}) custom-call(f32[16,128]{1,0:T(8,128)S(1)} %shard_map.153.partial_ref, f32[2,128]{1,0:T(2,128)S(1)} %collective-permute-done.23.first_in, f32[2,128]{1,0:T(2,128)S(1)} %collective-permute-done.24.second_in, ...), custom_call_target="tpu_custom_call" | custom-call | flops 10000000 | bytes 1000000 | tf_op jit(solution)/shard_map/pallas_call | solution.py:618
  56.6 1.3 %collective-permute-start.27 = (f32[16,128]{1,0:T(8,128)S(1)}, f32[16,128]{1,0:T(8,128)S(1)}, u32[]{:S(2)}, u32[]{:S(2)}) collective-permute-start(f32[16,128]{1,0:T(8,128)S(1)} %get-tuple-element.94.image_ref.refs_5_.refs_2_), channel_id=1, source_target_pairs={{0,3},{1,2},{2,1},{3,0},{4,7},{5,6},{6,5},{7,4},{8,11},{9,10},{10,... | collective-permute-start | bytes 24584 | tf_op jit(solution)/shard_map/ppermute | solution.py:684
  58.0 2.9 %collective-permute-start.28 = (f32[2,128]{1,0:T(2,128)S(1)}, f32[2,128]{1,0:T(2,128)S(1)}, u32[]{:S(2)}, u32[]{:S(2)}) collective-permute-start(f32[2,128]{1,0:T(2,128)S(1)} %get-tuple-element.95), channel_id=1, source_target_pairs={{0,4},{4,0},{8,12},{12,8},{16,20},{20,16},{24,28},{28,24},{1,5},{5... | collective-permute-start | bytes 3080 | tf_op jit(solution)/shard_map/ppermute | solution.py:681
  63.1 12.5 %all_to_all.11.sums_ref = f32[32,2,128]{2,1,0:T(2,128)S(1)} all-to-all(f32[32,2,128]{2,1,0:T(2,128)S(1)} %shard_map.157), channel_id=1, replica_groups=mesh['dom'=8,'sub'=4] {'dom','sub'}, dimensions={0} | all-to-all | bytes 65536 | tf_op jit(solution)/shard_map/all_to_all | solution.py:747
  75.6 1.0 %shard_map.158 = (f32[2,2,1024]{2,1,0:T(2,128)}, f32[2,2,18]{2,1,0:T(2,128)}) custom-call(f32[32,2,128]{2,1,0:T(2,128)S(1)} %all_to_all.11.sums_ref, f32[8,128]{1,0:T(8,128)S(1)} %get-tuple-element.100.inner_ref, f32[2,16,1024]{2,1,0:T(8,128)S(1)} %get-tuple-element.74.basis_ref, f32[16,128]{1,0:T(8,128)S(1)} %get-tuple-element.86.image_ref.refs_3_.refs_0_, ...), custom_call_target="tpu_custom_call" | custom-call | flops 10000000 | bytes 1000000 | tf_op jit(solution)/shard_map/pallas_call | solution.py:618
  (58 shorter events, 12.2 us)
Async XLA Ops:
  3.2 6.2 %collective-permute-start = (f32[16,128]{1,0:T(8,128)S(1)}, f32[16,128]{1,0:T(8,128)S(1)}, u32[]{:S(2)}, u32[]{:S(2)}) collective-permute-start(f32[16,128]{1,0:T(8,128)S(1)} %get-tuple-element.52.image_ref.refs_3_.refs_0_), channel_id=1, source_target_pairs={{0,1},{1,0},{2,3},{3,2},{4,5},{5,4},{6,7},{7,6},{8,9},{9,8},{10,11... | collective-permute-start | bytes 24584 | tf_op jit(solution)/shard_map/ppermute | solution.py:684
  3.7 5.7 %collective-permute-start.1 = (f32[16,128]{1,0:T(8,128)S(1)}, f32[16,128]{1,0:T(8,128)S(1)}, u32[]{:S(2)}, u32[]{:S(2)}) collective-permute-start(f32[16,128]{1,0:T(8,128)S(1)} %get-tuple-element.52.image_ref.refs_3_.refs_0_), channel_id=1, source_target_pairs={{0,2},{1,3},{2,0},{3,1},{4,6},{5,7},{6,4},{7,5},{8,10},{9,11},{10,... | collective-permute-start | bytes 24584 | tf_op jit(solution)/shard_map/ppermute | solution.py:684
  6.3 3.2 %collective-permute-start.2 = (f32[16,128]{1,0:T(8,128)S(1)}, f32[16,128]{1,0:T(8,128)S(1)}, u32[]{:S(2)}, u32[]{:S(2)}) collective-permute-start(f32[16,128]{1,0:T(8,128)S(1)} %get-tuple-element.52.image_ref.refs_3_.refs_0_), channel_id=1, source_target_pairs={{0,3},{1,2},{2,1},{3,0},{4,7},{5,6},{6,5},{7,4},{8,11},{9,10},{10,... | collective-permute-start | bytes 24584 | tf_op jit(solution)/shard_map/ppermute | solution.py:684
  6.3 3.9 %collective-permute-start.3 = (f32[2,128]{1,0:T(2,128)S(1)}, f32[2,128]{1,0:T(2,128)S(1)}, u32[]{:S(2)}, u32[]{:S(2)}) collective-permute-start(f32[2,128]{1,0:T(2,128)S(1)} %get-tuple-element.64), channel_id=1, source_target_pairs={{0,4},{4,0},{8,12},{12,8},{16,20},{20,16},{24,28},{28,24},{1,5},{5... | collective-permute-start | bytes 3080 | tf_op jit(solution)/shard_map/ppermute | solution.py:681
  11.3 5.4 %collective-permute-start.5 = (f32[16,128]{1,0:T(8,128)S(1)}, f32[16,128]{1,0:T(8,128)S(1)}, u32[]{:S(2)}, u32[]{:S(2)}) collective-permute-start(f32[16,128]{1,0:T(8,128)S(1)} %get-tuple-element.73.after_ref.image_ref.refs_4_.refs_1_), channel_id=1, source_target_pairs={{0,1},{1,0},{2,3},{3,2},{4,5},{5,4},{6,7},{7,6},{8,9},{9,8},{10,11... | collective-permute-start | bytes 24584 | tf_op jit(solution)/shard_map/ppermute | solution.py:684
  11.8 4.9 %collective-permute-start.6 = (f32[16,128]{1,0:T(8,128)S(1)}, f32[16,128]{1,0:T(8,128)S(1)}, u32[]{:S(2)}, u32[]{:S(2)}) collective-permute-start(f32[16,128]{1,0:T(8,128)S(1)} %get-tuple-element.73.after_ref.image_ref.refs_4_.refs_1_), channel_id=1, source_target_pairs={{0,2},{1,3},{2,0},{3,1},{4,6},{5,7},{6,4},{7,5},{8,10},{9,11},{10,... | collective-permute-start | bytes 24584 | tf_op jit(solution)/shard_map/ppermute | solution.py:684
  13.3 3.4 %collective-permute-start.7 = (f32[16,128]{1,0:T(8,128)S(1)}, f32[16,128]{1,0:T(8,128)S(1)}, u32[]{:S(2)}, u32[]{:S(2)}) collective-permute-start(f32[16,128]{1,0:T(8,128)S(1)} %get-tuple-element.73.after_ref.image_ref.refs_4_.refs_1_), channel_id=1, source_target_pairs={{0,3},{1,2},{2,1},{3,0},{4,7},{5,6},{6,5},{7,4},{8,11},{9,10},{10,... | collective-permute-start | bytes 24584 | tf_op jit(solution)/shard_map/ppermute | solution.py:684
  13.3 4.4 %collective-permute-start.8 = (f32[2,128]{1,0:T(2,128)S(1)}, f32[2,128]{1,0:T(2,128)S(1)}, u32[]{:S(2)}, u32[]{:S(2)}) collective-permute-start(f32[2,128]{1,0:T(2,128)S(1)} %get-tuple-element.75), channel_id=1, source_target_pairs={{0,4},{4,0},{8,12},{12,8},{16,20},{20,16},{24,28},{28,24},{1,5},{5... | collective-permute-start | bytes 3080 | tf_op jit(solution)/shard_map/ppermute | solution.py:681
  18.8 5.4 %collective-permute-start.10 = (f32[16,128]{1,0:T(8,128)S(1)}, f32[16,128]{1,0:T(8,128)S(1)}, u32[]{:S(2)}, u32[]{:S(2)}) collective-permute-start(f32[16,128]{1,0:T(8,128)S(1)} %get-tuple-element.78.image_ref.refs_5_.refs_2_), channel_id=1, source_target_pairs={{0,1},{1,0},{2,3},{3,2},{4,5},{5,4},{6,7},{7,6},{8,9},{9,8},{10,11... | collective-permute-start | bytes 24584 | tf_op jit(solution)/shard_map/ppermute | solution.py:684
  19.0 5.2 %collective-permute-start.11 = (f32[16,128]{1,0:T(8,128)S(1)}, f32[16,128]{1,0:T(8,128)S(1)}, u32[]{:S(2)}, u32[]{:S(2)}) collective-permute-start(f32[16,128]{1,0:T(8,128)S(1)} %get-tuple-element.78.image_ref.refs_5_.refs_2_), channel_id=1, source_target_pairs={{0,2},{1,3},{2,0},{3,1},{4,6},{5,7},{6,4},{7,5},{8,10},{9,11},{10,... | collective-permute-start | bytes 24584 | tf_op jit(solution)/shard_map/ppermute | solution.py:684
  20.5 3.7 %collective-permute-start.12 = (f32[16,128]{1,0:T(8,128)S(1)}, f32[16,128]{1,0:T(8,128)S(1)}, u32[]{:S(2)}, u32[]{:S(2)}) collective-permute-start(f32[16,128]{1,0:T(8,128)S(1)} %get-tuple-element.78.image_ref.refs_5_.refs_2_), channel_id=1, source_target_pairs={{0,3},{1,2},{2,1},{3,0},{4,7},{5,6},{6,5},{7,4},{8,11},{9,10},{10,... | collective-permute-start | bytes 24584 | tf_op jit(solution)/shard_map/ppermute | solution.py:684
  20.7 4.6 %collective-permute-start.13 = (f32[2,128]{1,0:T(2,128)S(1)}, f32[2,128]{1,0:T(2,128)S(1)}, u32[]{:S(2)}, u32[]{:S(2)}) collective-permute-start(f32[2,128]{1,0:T(2,128)S(1)} %get-tuple-element.79), channel_id=1, source_target_pairs={{0,4},{4,0},{8,12},{12,8},{16,20},{20,16},{24,28},{28,24},{1,5},{5... | collective-permute-start | bytes 3080 | tf_op jit(solution)/shard_map/ppermute | solution.py:681
  42.3 3.7 %collective-permute-start.16 = (f32[16,128]{1,0:T(8,128)S(1)}, f32[16,128]{1,0:T(8,128)S(1)}, u32[]{:S(2)}, u32[]{:S(2)}) collective-permute-start(f32[16,128]{1,0:T(8,128)S(1)} %get-tuple-element.86.image_ref.refs_3_.refs_0_), channel_id=1, source_target_pairs={{0,2},{1,3},{2,0},{3,1},{4,6},{5,7},{6,4},{7,5},{8,10},{9,11},{10,... | collective-permute-start | bytes 24584 | tf_op jit(solution)/shard_map/ppermute | solution.py:684
  42.7 3.2 %collective-permute-start.17 = (f32[16,128]{1,0:T(8,128)S(1)}, f32[16,128]{1,0:T(8,128)S(1)}, u32[]{:S(2)}, u32[]{:S(2)}) collective-permute-start(f32[16,128]{1,0:T(8,128)S(1)} %get-tuple-element.86.image_ref.refs_3_.refs_0_), channel_id=1, source_target_pairs={{0,3},{1,2},{2,1},{3,0},{4,7},{5,6},{6,5},{7,4},{8,11},{9,10},{10,... | collective-permute-start | bytes 24584 | tf_op jit(solution)/shard_map/ppermute | solution.py:684
  44.0 3.6 %collective-permute-start.18 = (f32[2,128]{1,0:T(2,128)S(1)}, f32[2,128]{1,0:T(2,128)S(1)}, u32[]{:S(2)}, u32[]{:S(2)}) collective-permute-start(f32[2,128]{1,0:T(2,128)S(1)} %get-tuple-element.87), channel_id=1, source_target_pairs={{0,4},{4,0},{8,12},{12,8},{16,20},{20,16},{24,28},{28,24},{1,5},{5... | collective-permute-start | bytes 3080 | tf_op jit(solution)/shard_map/ppermute | solution.py:681
  44.6 3.0 %collective-permute-start.19 = (f32[2,128]{1,0:T(2,128)S(1)}, f32[2,128]{1,0:T(2,128)S(1)}, u32[]{:S(2)}, u32[]{:S(2)}) collective-permute-start(f32[2,128]{1,0:T(2,128)S(1)} %get-tuple-element.88), channel_id=1, source_target_pairs={{0,1},{1,0},{2,3},{3,2},{4,8},{5,9},{6,10},{7,11},{8,4},{9,5},{10,... | collective-permute-start | bytes 3080 | tf_op jit(solution)/shard_map/ppermute | solution.py:680
  48.6 4.9 %collective-permute-start.20 = (f32[16,128]{1,0:T(8,128)S(1)}, f32[16,128]{1,0:T(8,128)S(1)}, u32[]{:S(2)}, u32[]{:S(2)}) collective-permute-start(f32[16,128]{1,0:T(8,128)S(1)} %get-tuple-element.90.image_ref.refs_4_.refs_1_), channel_id=1, source_target_pairs={{0,1},{1,0},{2,3},{3,2},{4,5},{5,4},{6,7},{7,6},{8,9},{9,8},{10,11... | collective-permute-start | bytes 24584 | tf_op jit(solution)/shard_map/ppermute | solution.py:684
  48.7 4.9 %collective-permute-start.21 = (f32[16,128]{1,0:T(8,128)S(1)}, f32[16,128]{1,0:T(8,128)S(1)}, u32[]{:S(2)}, u32[]{:S(2)}) collective-permute-start(f32[16,128]{1,0:T(8,128)S(1)} %get-tuple-element.90.image_ref.refs_4_.refs_1_), channel_id=1, source_target_pairs={{0,2},{1,3},{2,0},{3,1},{4,6},{5,7},{6,4},{7,5},{8,10},{9,11},{10,... | collective-permute-start | bytes 24584 | tf_op jit(solution)/shard_map/ppermute | solution.py:684
  49.3 4.2 %collective-permute-start.22 = (f32[16,128]{1,0:T(8,128)S(1)}, f32[16,128]{1,0:T(8,128)S(1)}, u32[]{:S(2)}, u32[]{:S(2)}) collective-permute-start(f32[16,128]{1,0:T(8,128)S(1)} %get-tuple-element.90.image_ref.refs_4_.refs_1_), channel_id=1, source_target_pairs={{0,3},{1,2},{2,1},{3,0},{4,7},{5,6},{6,5},{7,4},{8,11},{9,10},{10,... | collective-permute-start | bytes 24584 | tf_op jit(solution)/shard_map/ppermute | solution.py:684
  50.5 4.5 %collective-permute-start.23 = (f32[2,128]{1,0:T(2,128)S(1)}, f32[2,128]{1,0:T(2,128)S(1)}, u32[]{:S(2)}, u32[]{:S(2)}) collective-permute-start(f32[2,128]{1,0:T(2,128)S(1)} %get-tuple-element.91), channel_id=1, source_target_pairs={{0,4},{4,0},{8,12},{12,8},{16,20},{20,16},{24,28},{28,24},{1,5},{5... | collective-permute-start | bytes 3080 | tf_op jit(solution)/shard_map/ppermute | solution.py:681
  56.1 5.3 %collective-permute-start.25 = (f32[16,128]{1,0:T(8,128)S(1)}, f32[16,128]{1,0:T(8,128)S(1)}, u32[]{:S(2)}, u32[]{:S(2)}) collective-permute-start(f32[16,128]{1,0:T(8,128)S(1)} %get-tuple-element.94.image_ref.refs_5_.refs_2_), channel_id=1, source_target_pairs={{0,1},{1,0},{2,3},{3,2},{4,5},{5,4},{6,7},{7,6},{8,9},{9,8},{10,11... | collective-permute-start | bytes 24584 | tf_op jit(solution)/shard_map/ppermute | solution.py:684
  56.1 5.2 %collective-permute-start.26 = (f32[16,128]{1,0:T(8,128)S(1)}, f32[16,128]{1,0:T(8,128)S(1)}, u32[]{:S(2)}, u32[]{:S(2)}) collective-permute-start(f32[16,128]{1,0:T(8,128)S(1)} %get-tuple-element.94.image_ref.refs_5_.refs_2_), channel_id=1, source_target_pairs={{0,2},{1,3},{2,0},{3,1},{4,6},{5,7},{6,4},{7,5},{8,10},{9,11},{10,... | collective-permute-start | bytes 24584 | tf_op jit(solution)/shard_map/ppermute | solution.py:684
  56.6 4.8 %collective-permute-start.27 = (f32[16,128]{1,0:T(8,128)S(1)}, f32[16,128]{1,0:T(8,128)S(1)}, u32[]{:S(2)}, u32[]{:S(2)}) collective-permute-start(f32[16,128]{1,0:T(8,128)S(1)} %get-tuple-element.94.image_ref.refs_5_.refs_2_), channel_id=1, source_target_pairs={{0,3},{1,2},{2,1},{3,0},{4,7},{5,6},{6,5},{7,4},{8,11},{9,10},{10,... | collective-permute-start | bytes 24584 | tf_op jit(solution)/shard_map/ppermute | solution.py:684
  58.0 4.5 %collective-permute-start.28 = (f32[2,128]{1,0:T(2,128)S(1)}, f32[2,128]{1,0:T(2,128)S(1)}, u32[]{:S(2)}, u32[]{:S(2)}) collective-permute-start(f32[2,128]{1,0:T(2,128)S(1)} %get-tuple-element.95), channel_id=1, source_target_pairs={{0,4},{4,0},{8,12},{12,8},{16,20},{20,16},{24,28},{28,24},{1,5},{5... | collective-permute-start | bytes 3080 | tf_op jit(solution)/shard_map/ppermute | solution.py:681
  (6 other events, 10.9 us)

commit v4 on v3

--- a/solution.py
+++ b/solution.py
@@ -13,7 +13,7 @@
 BF16 = jnp.bfloat16
 NT_DIMS = (((1,), (1,)), ((), ()))
 LANES = 128
-COPIED = 11
+COPIED = 10
 FOLDS = (2, 4)
 VMEM_LIMIT = 12 * 1024 * 1024
 AXES = ("dom", "sub")
@@ -686,7 +686,7 @@
 
     copied = (
         basis, compact, weights, fresh, pattern, c_rows.reshape(1, slots), c_side.reshape(1, slots),
-        shifts, mass, k_tiles, c_tiles,
+        shifts, mass, c_tiles,
     )
     (right, image, first, second, p_high, p_low, *copied) = call(
         start_kernel,
@@ -705,7 +705,7 @@
     k_high, k_low, c_high, c_low, pick_table, below, above, drag = call(
         functools.partial(prepare_kernel, n_dom),
         (k_part, k_part, c_part, c_part, pick, mask, mask, drag),
-        [smem()] + [vmem()] * 7, [], (c_count, *copied[4:]),
+        [smem()] + [vmem()] * 7, [], (c_count, *copied[4:9], k_tiles, copied[9]),
     )
     previous = zero
     for step in range(steps):

time: 76.8 us -> 76.4 us (level)
  no operation moved by 1% of the time
where the time goes in v4:
time: 76.4 us; the launch traced here: 76.2 us
  blocking collectives  27.8 us (36%)
  starting transfers between devices  27.3 us (36%)
  Pallas kernels  15.7 us (21%)
  waiting for transfers between devices  3.89 us (5%)
  between operations  1.47 us (2%)
    all_to_all x2, blocking collectives, local(): sums = lax.all_to_all(payload, AXES, 0, 0)  27.8 us
    pallas_call x19, Pallas kernels, call(): pl.pallas_call(kernel, out_shape=out_shape, in_specs=in_specs, out_specs=...  15.7 us
    ppermute x6, starting transfers between devices, exchange(): first = lax.ppermute(first, 'dom', even_swap)  14.1 us
    ppermute x18, starting transfers between devices, exchange(): lax.ppermute(image, 'sub', [(i, i ^ k) for i in range(n_sub)])  12.7 us
    ppermute x6, waiting for transfers between devices, exchange(): first = lax.ppermute(first, 'dom', even_swap)  2.58 us
  transfers between devices with their start and end apart: 30, of which 6 were waited for; matrix products, arithmetic and copies ran while one was open for 0% of the time, Pallas kernels for 8%

profile of v4, /device:TPU:0, one launch (start us, length us, event | category | flops | bytes accessed | tf_op | source)
XLA Modules:
  0.0 76.2 jit_solution(14239402637446883338)
XLA Ops:
  0.6 2.2 %shard_map.140 = (f32[16,128]{1,0:T(8,128)S(1)}, f32[16,128]{1,0:T(8,128)S(1)}, f32[2,128]{1,0:T(2,128)S(1)}, f32[2,128]{1,0:T(2,128)S(1)}, bf16[128,2048]{1,0:T...) custom-call(f32[2,16,1024]{2,1,0:T(8,128)} %refs_0_.1, ...), custom_call_target="tpu_custom_call" | custom-call | flops 10000000 | bytes 1000000 | tf_op jit(solution)/shard_map/pallas_call | solution.py:618
  3.4 2.5 %collective-permute-start.1 = (f32[16,128]{1,0:T(8,128)S(1)}, f32[16,128]{1,0:T(8,128)S(1)}, u32[]{:S(2)}, u32[]{:S(2)}) collective-permute-start(f32[16,128]{1,0:T(8,128)S(1)} %get-tuple-element.51.image_ref.refs_3_.refs_0_), channel_id=1, source_target_pairs={{0,2},{1,3},{2,0},{3,1},{4,6},{5,7},{6,4},{7,5},{8,10},{9,11},{10,... | collective-permute-start | bytes 24584 | tf_op jit(solution)/shard_map/ppermute | solution.py:684
  5.9 1.8 %collective-permute-start.3 = (f32[2,128]{1,0:T(2,128)S(1)}, f32[2,128]{1,0:T(2,128)S(1)}, u32[]{:S(2)}, u32[]{:S(2)}) collective-permute-start(f32[2,128]{1,0:T(2,128)S(1)} %get-tuple-element.62), channel_id=1, source_target_pairs={{0,4},{4,0},{8,12},{12,8},{16,20},{20,16},{24,28},{28,24},{1,5},{5... | collective-permute-start | bytes 3080 | tf_op jit(solution)/shard_map/ppermute | solution.py:681
  9.1 0.7 shard_map.142.partial_ref
  9.8 1.1 %shard_map.143 = (f32[16,128]{1,0:T(8,128)S(1)}, f32[16,128]{1,0:T(8,128)S(1)}, f32[2,128]{1,0:T(2,128)S(1)}, f32[2,128]{1,0:T(2,128)S(1)}, f32[16,128]{1,0:T(8,128)S(1)}) custom-call(f32[16,128]{1,0:T(8,128)S(1)} %shard_map.142.partial_ref, f32[2,128]{1,0:T(2,128)S(1)} %collective-permute-done.3.first_in, f32[2,128]{1,0:T(2,128)S(1)} %collective-permute-done.4.second_in, ...), custom_call_target="tpu_custom_call" | custom-call | flops 10000000 | bytes 1000000 | tf_op jit(solution)/shard_map/pallas_call | solution.py:618
  11.4 1.5 %collective-permute-start.6 = (f32[16,128]{1,0:T(8,128)S(1)}, f32[16,128]{1,0:T(8,128)S(1)}, u32[]{:S(2)}, u32[]{:S(2)}) collective-permute-start(f32[16,128]{1,0:T(8,128)S(1)} %get-tuple-element.71.after_ref.image_ref.refs_4_.refs_1_), channel_id=1, source_target_pairs={{0,2},{1,3},{2,0},{3,1},{4,6},{5,7},{6,4},{7,5},{8,10},{9,11},{10,... | collective-permute-start | bytes 24584 | tf_op jit(solution)/shard_map/ppermute | solution.py:684
  12.9 2.9 %collective-permute-start.8 = (f32[2,128]{1,0:T(2,128)S(1)}, f32[2,128]{1,0:T(2,128)S(1)}, u32[]{:S(2)}, u32[]{:S(2)}) collective-permute-start(f32[2,128]{1,0:T(2,128)S(1)} %get-tuple-element.73), channel_id=1, source_target_pairs={{0,4},{4,0},{8,12},{12,8},{16,20},{20,16},{24,28},{28,24},{1,5},{5... | collective-permute-start | bytes 3080 | tf_op jit(solution)/shard_map/ppermute | solution.py:681
  17.3 1.1 %shard_map.146 = (f32[16,128]{1,0:T(8,128)S(1)}, f32[16,128]{1,0:T(8,128)S(1)}, f32[2,128]{1,0:T(2,128)S(1)}, f32[2,128]{1,0:T(2,128)S(1)}) custom-call(f32[16,128]{1,0:T(8,128)S(1)} %shard_map.145.partial_ref, f32[2,128]{1,0:T(2,128)S(1)} %collective-permute-done.8.first_in, f32[2,128]{1,0:T(2,128)S(1)} %collective-permute-done.9.second_in, ...), custom_call_target="tpu_custom_call" | custom-call | flops 10000000 | bytes 1000000 | tf_op jit(solution)/shard_map/pallas_call | solution.py:618
  18.6 1.5 %collective-permute-start.11 = (f32[16,128]{1,0:T(8,128)S(1)}, f32[16,128]{1,0:T(8,128)S(1)}, u32[]{:S(2)}, u32[]{:S(2)}) collective-permute-start(f32[16,128]{1,0:T(8,128)S(1)} %get-tuple-element.76.image_ref.refs_5_.refs_2_), channel_id=1, source_target_pairs={{0,2},{1,3},{2,0},{3,1},{4,6},{5,7},{6,4},{7,5},{8,10},{9,11},{10,... | collective-permute-start | bytes 24584 | tf_op jit(solution)/shard_map/ppermute | solution.py:684
  20.3 3.0 %collective-permute-start.13 = (f32[2,128]{1,0:T(2,128)S(1)}, f32[2,128]{1,0:T(2,128)S(1)}, u32[]{:S(2)}, u32[]{:S(2)}) collective-permute-start(f32[2,128]{1,0:T(2,128)S(1)} %get-tuple-element.77), channel_id=1, source_target_pairs={{0,4},{4,0},{8,12},{12,8},{16,20},{20,16},{24,28},{28,24},{1,5},{5... | collective-permute-start | bytes 3080 | tf_op jit(solution)/shard_map/ppermute | solution.py:681
  25.6 15.4 %all_to_all.10.sums_ref = f32[32,4,128]{2,1,0:T(4,128)S(1)} all-to-all(f32[32,4,128]{2,1,0:T(4,128)S(1)} %shard_map.149), channel_id=1, replica_groups=mesh['dom'=8,'sub'=4] {'dom','sub'}, dimensions={0} | all-to-all | bytes 131072 | tf_op jit(solution)/shard_map/all_to_all | solution.py:747
  40.9 0.8 %shard_map.150 = (f32[16,128]{1,0:T(8,128)S(1)}, f32[16,128]{1,0:T(8,128)S(1)}, f32[2,128]{1,0:T(2,128)S(1)}, f32[2,128]{1,0:T(2,128)S(1)}, f32[16,128]{1,0:T(8,...) custom-call(f32[32,4,128]{2,1,0:T(4,128)S(1)} %all_to_all.10.sums_ref, ...), custom_call_target="tpu_custom_call" | custom-call | flops 10000000 | bytes 1000000 | tf_op jit(solution)/shard_map/pallas_call | solution.py:618
  42.3 1.3 %collective-permute-start.17 = (f32[16,128]{1,0:T(8,128)S(1)}, f32[16,128]{1,0:T(8,128)S(1)}, u32[]{:S(2)}, u32[]{:S(2)}) collective-permute-start(f32[16,128]{1,0:T(8,128)S(1)} %get-tuple-element.84.image_ref.refs_3_.refs_0_), channel_id=1, source_target_pairs={{0,3},{1,2},{2,1},{3,0},{4,7},{5,6},{6,5},{7,4},{8,11},{9,10},{10,... | collective-permute-start | bytes 24584 | tf_op jit(solution)/shard_map/ppermute | solution.py:684
  44.3 1.2 %collective-permute-done.16.refs_1_ = f32[16,128]{1,0:T(8,128)S(1)} collective-permute-done((f32[16,128]{1,0:T(8,128)S(1)}, f32[16,128]{1,0:T(8,128)S(1)}, u32[]{:S(2)}, u32[]{:S(2)}) %collective-permute-start.16) | collective-permute-done | bytes 8224 | tf_op jit(solution)/shard_map/ppermute | solution.py:684
  46.3 0.9 %collective-permute-done.18.first_in = f32[2,128]{1,0:T(2,128)S(1)} collective-permute-done((f32[2,128]{1,0:T(2,128)S(1)}, f32[2,128]{1,0:T(2,128)S(1)}, u32[]{:S(2)}, u32[]{:S(2)}) %collective-permute-start.18) | collective-permute-done | bytes 1056 | tf_op jit(solution)/shard_map/ppermute | solution.py:681
  47.2 1.1 %shard_map.152 = (f32[16,128]{1,0:T(8,128)S(1)}, f32[16,128]{1,0:T(8,128)S(1)}, f32[2,128]{1,0:T(2,128)S(1)}, f32[2,128]{1,0:T(2,128)S(1)}, f32[16,128]{1,0:T(8,128)S(1)}) custom-call(f32[16,128]{1,0:T(8,128)S(1)} %shard_map.151.partial_ref, f32[2,128]{1,0:T(2,128)S(1)} %collective-permute-done.18.first_in, f32[2,128]{1,0:T(2,128)S(1)} %collective-permute-done.19.second_in, ...), custom_call_target="tpu_custom_call" | custom-call | flops 10000000 | bytes 1000000 | tf_op jit(solution)/shard_map/pallas_call | solution.py:618
  49.0 1.2 %collective-permute-start.22 = (f32[16,128]{1,0:T(8,128)S(1)}, f32[16,128]{1,0:T(8,128)S(1)}, u32[]{:S(2)}, u32[]{:S(2)}) collective-permute-start(f32[16,128]{1,0:T(8,128)S(1)} %get-tuple-element.88.image_ref.refs_4_.refs_1_), channel_id=1, source_target_pairs={{0,3},{1,2},{2,1},{3,0},{4,7},{5,6},{6,5},{7,4},{8,11},{9,10},{10,... | collective-permute-start | bytes 24584 | tf_op jit(solution)/shard_map/ppermute | solution.py:684
  50.2 2.9 %collective-permute-start.23 = (f32[2,128]{1,0:T(2,128)S(1)}, f32[2,128]{1,0:T(2,128)S(1)}, u32[]{:S(2)}, u32[]{:S(2)}) collective-permute-start(f32[2,128]{1,0:T(2,128)S(1)} %get-tuple-element.89), channel_id=1, source_target_pairs={{0,4},{4,0},{8,12},{12,8},{16,20},{20,16},{24,28},{28,24},{1,5},{5... | collective-permute-start | bytes 3080 | tf_op jit(solution)/shard_map/ppermute | solution.py:681
  53.9 0.7 collective-permute-done.23.first_in
  54.7 1.1 %shard_map.154 = (f32[16,128]{1,0:T(8,128)S(1)}, f32[16,128]{1,0:T(8,128)S(1)}, f32[2,128]{1,0:T(2,128)S(1)}, f32[2,128]{1,0:T(2,128)S(1)}) custom-call(f32[16,128]{1,0:T(8,128)S(1)} %shard_map.153.partial_ref, f32[2,128]{1,0:T(2,128)S(1)} %collective-permute-done.23.first_in, f32[2,128]{1,0:T(2,128)S(1)} %collective-permute-done.24.second_in, ...), custom_call_target="tpu_custom_call" | custom-call | flops 10000000 | bytes 1000000 | tf_op jit(solution)/shard_map/pallas_call | solution.py:618
  56.3 1.3 %collective-permute-start.27 = (f32[16,128]{1,0:T(8,128)S(1)}, f32[16,128]{1,0:T(8,128)S(1)}, u32[]{:S(2)}, u32[]{:S(2)}) collective-permute-start(f32[16,128]{1,0:T(8,128)S(1)} %get-tuple-element.92.image_ref.refs_5_.refs_2_), channel_id=1, source_target_pairs={{0,3},{1,2},{2,1},{3,0},{4,7},{5,6},{6,5},{7,4},{8,11},{9,10},{10,... | collective-permute-start | bytes 24584 | tf_op jit(solution)/shard_map/ppermute | solution.py:684
  57.6 2.9 %collective-permute-start.28 = (f32[2,128]{1,0:T(2,128)S(1)}, f32[2,128]{1,0:T(2,128)S(1)}, u32[]{:S(2)}, u32[]{:S(2)}) collective-permute-start(f32[2,128]{1,0:T(2,128)S(1)} %get-tuple-element.93), channel_id=1, source_target_pairs={{0,4},{4,0},{8,12},{12,8},{16,20},{20,16},{24,28},{28,24},{1,5},{5... | collective-permute-start | bytes 3080 | tf_op jit(solution)/shard_map/ppermute | solution.py:681
  62.8 12.5 %all_to_all.11.sums_ref = f32[32,2,128]{2,1,0:T(2,128)S(1)} all-to-all(f32[32,2,128]{2,1,0:T(2,128)S(1)} %shard_map.157), channel_id=1, replica_groups=mesh['dom'=8,'sub'=4] {'dom','sub'}, dimensions={0} | all-to-all | bytes 65536 | tf_op jit(solution)/shard_map/all_to_all | solution.py:747
  75.3 1.0 %shard_map.158 = (f32[2,2,1024]{2,1,0:T(2,128)}, f32[2,2,18]{2,1,0:T(2,128)}) custom-call(f32[32,2,128]{2,1,0:T(2,128)S(1)} %all_to_all.11.sums_ref, f32[8,128]{1,0:T(8,128)S(1)} %get-tuple-element.98.inner_ref, f32[2,16,1024]{2,1,0:T(8,128)S(1)} %get-tuple-element.72.basis_ref, f32[16,128]{1,0:T(8,128)S(1)} %get-tuple-element.84.image_ref.refs_3_.refs_0_, ...), custom_call_target="tpu_custom_call" | custom-call | flops 10000000 | bytes 1000000 | tf_op jit(solution)/shard_map/pallas_call | solution.py:618
  (60 shorter events, 12.2 us)
Async XLA Ops:
  2.8 6.3 %collective-permute-start = (f32[16,128]{1,0:T(8,128)S(1)}, f32[16,128]{1,0:T(8,128)S(1)}, u32[]{:S(2)}, u32[]{:S(2)}) collective-permute-start(f32[16,128]{1,0:T(8,128)S(1)} %get-tuple-element.51.image_ref.refs_3_.refs_0_), channel_id=1, source_target_pairs={{0,1},{1,0},{2,3},{3,2},{4,5},{5,4},{6,7},{7,6},{8,9},{9,8},{10,11... | collective-permute-start | bytes 24584 | tf_op jit(solution)/shard_map/ppermute | solution.py:684
  3.4 5.7 %collective-permute-start.1 = (f32[16,128]{1,0:T(8,128)S(1)}, f32[16,128]{1,0:T(8,128)S(1)}, u32[]{:S(2)}, u32[]{:S(2)}) collective-permute-start(f32[16,128]{1,0:T(8,128)S(1)} %get-tuple-element.51.image_ref.refs_3_.refs_0_), channel_id=1, source_target_pairs={{0,2},{1,3},{2,0},{3,1},{4,6},{5,7},{6,4},{7,5},{8,10},{9,11},{10,... | collective-permute-start | bytes 24584 | tf_op jit(solution)/shard_map/ppermute | solution.py:684
  5.9 3.2 %collective-permute-start.2 = (f32[16,128]{1,0:T(8,128)S(1)}, f32[16,128]{1,0:T(8,128)S(1)}, u32[]{:S(2)}, u32[]{:S(2)}) collective-permute-start(f32[16,128]{1,0:T(8,128)S(1)} %get-tuple-element.51.image_ref.refs_3_.refs_0_), channel_id=1, source_target_pairs={{0,3},{1,2},{2,1},{3,0},{4,7},{5,6},{6,5},{7,4},{8,11},{9,10},{10,... | collective-permute-start | bytes 24584 | tf_op jit(solution)/shard_map/ppermute | solution.py:684
  5.9 3.9 %collective-permute-start.3 = (f32[2,128]{1,0:T(2,128)S(1)}, f32[2,128]{1,0:T(2,128)S(1)}, u32[]{:S(2)}, u32[]{:S(2)}) collective-permute-start(f32[2,128]{1,0:T(2,128)S(1)} %get-tuple-element.62), channel_id=1, source_target_pairs={{0,4},{4,0},{8,12},{12,8},{16,20},{20,16},{24,28},{28,24},{1,5},{5... | collective-permute-start | bytes 3080 | tf_op jit(solution)/shard_map/ppermute | solution.py:681
  10.9 5.4 %collective-permute-start.5 = (f32[16,128]{1,0:T(8,128)S(1)}, f32[16,128]{1,0:T(8,128)S(1)}, u32[]{:S(2)}, u32[]{:S(2)}) collective-permute-start(f32[16,128]{1,0:T(8,128)S(1)} %get-tuple-element.71.after_ref.image_ref.refs_4_.refs_1_), channel_id=1, source_target_pairs={{0,1},{1,0},{2,3},{3,2},{4,5},{5,4},{6,7},{7,6},{8,9},{9,8},{10,11... | collective-permute-start | bytes 24584 | tf_op jit(solution)/shard_map/ppermute | solution.py:684
  11.4 4.9 %collective-permute-start.6 = (f32[16,128]{1,0:T(8,128)S(1)}, f32[16,128]{1,0:T(8,128)S(1)}, u32[]{:S(2)}, u32[]{:S(2)}) collective-permute-start(f32[16,128]{1,0:T(8,128)S(1)} %get-tuple-element.71.after_ref.image_ref.refs_4_.refs_1_), channel_id=1, source_target_pairs={{0,2},{1,3},{2,0},{3,1},{4,6},{5,7},{6,4},{7,5},{8,10},{9,11},{10,... | collective-permute-start | bytes 24584 | tf_op jit(solution)/shard_map/ppermute | solution.py:684
  12.9 3.5 %collective-permute-start.7 = (f32[16,128]{1,0:T(8,128)S(1)}, f32[16,128]{1,0:T(8,128)S(1)}, u32[]{:S(2)}, u32[]{:S(2)}) collective-permute-start(f32[16,128]{1,0:T(8,128)S(1)} %get-tuple-element.71.after_ref.image_ref.refs_4_.refs_1_), channel_id=1, source_target_pairs={{0,3},{1,2},{2,1},{3,0},{4,7},{5,6},{6,5},{7,4},{8,11},{9,10},{10,... | collective-permute-start | bytes 24584 | tf_op jit(solution)/shard_map/ppermute | solution.py:684
  12.9 4.5 %collective-permute-start.8 = (f32[2,128]{1,0:T(2,128)S(1)}, f32[2,128]{1,0:T(2,128)S(1)}, u32[]{:S(2)}, u32[]{:S(2)}) collective-permute-start(f32[2,128]{1,0:T(2,128)S(1)} %get-tuple-element.73), channel_id=1, source_target_pairs={{0,4},{4,0},{8,12},{12,8},{16,20},{20,16},{24,28},{28,24},{1,5},{5... | collective-permute-start | bytes 3080 | tf_op jit(solution)/shard_map/ppermute | solution.py:681
  18.4 5.4 %collective-permute-start.10 = (f32[16,128]{1,0:T(8,128)S(1)}, f32[16,128]{1,0:T(8,128)S(1)}, u32[]{:S(2)}, u32[]{:S(2)}) collective-permute-start(f32[16,128]{1,0:T(8,128)S(1)} %get-tuple-element.76.image_ref.refs_5_.refs_2_), channel_id=1, source_target_pairs={{0,1},{1,0},{2,3},{3,2},{4,5},{5,4},{6,7},{7,6},{8,9},{9,8},{10,11... | collective-permute-start | bytes 24584 | tf_op jit(solution)/shard_map/ppermute | solution.py:684
  18.6 5.2 %collective-permute-start.11 = (f32[16,128]{1,0:T(8,128)S(1)}, f32[16,128]{1,0:T(8,128)S(1)}, u32[]{:S(2)}, u32[]{:S(2)}) collective-permute-start(f32[16,128]{1,0:T(8,128)S(1)} %get-tuple-element.76.image_ref.refs_5_.refs_2_), channel_id=1, source_target_pairs={{0,2},{1,3},{2,0},{3,1},{4,6},{5,7},{6,4},{7,5},{8,10},{9,11},{10,... | collective-permute-start | bytes 24584 | tf_op jit(solution)/shard_map/ppermute | solution.py:684
  20.1 3.7 %collective-permute-start.12 = (f32[16,128]{1,0:T(8,128)S(1)}, f32[16,128]{1,0:T(8,128)S(1)}, u32[]{:S(2)}, u32[]{:S(2)}) collective-permute-start(f32[16,128]{1,0:T(8,128)S(1)} %get-tuple-element.76.image_ref.refs_5_.refs_2_), channel_id=1, source_target_pairs={{0,3},{1,2},{2,1},{3,0},{4,7},{5,6},{6,5},{7,4},{8,11},{9,10},{10,... | collective-permute-start | bytes 24584 | tf_op jit(solution)/shard_map/ppermute | solution.py:684
  20.3 4.6 %collective-permute-start.13 = (f32[2,128]{1,0:T(2,128)S(1)}, f32[2,128]{1,0:T(2,128)S(1)}, u32[]{:S(2)}, u32[]{:S(2)}) collective-permute-start(f32[2,128]{1,0:T(2,128)S(1)} %get-tuple-element.77), channel_id=1, source_target_pairs={{0,4},{4,0},{8,12},{12,8},{16,20},{20,16},{24,28},{28,24},{1,5},{5... | collective-permute-start | bytes 3080 | tf_op jit(solution)/shard_map/ppermute | solution.py:681
  41.9 3.7 %collective-permute-start.16 = (f32[16,128]{1,0:T(8,128)S(1)}, f32[16,128]{1,0:T(8,128)S(1)}, u32[]{:S(2)}, u32[]{:S(2)}) collective-permute-start(f32[16,128]{1,0:T(8,128)S(1)} %get-tuple-element.84.image_ref.refs_3_.refs_0_), channel_id=1, source_target_pairs={{0,2},{1,3},{2,0},{3,1},{4,6},{5,7},{6,4},{7,5},{8,10},{9,11},{10,... | collective-permute-start | bytes 24584 | tf_op jit(solution)/shard_map/ppermute | solution.py:684
  42.3 3.2 %collective-permute-start.17 = (f32[16,128]{1,0:T(8,128)S(1)}, f32[16,128]{1,0:T(8,128)S(1)}, u32[]{:S(2)}, u32[]{:S(2)}) collective-permute-start(f32[16,128]{1,0:T(8,128)S(1)} %get-tuple-element.84.image_ref.refs_3_.refs_0_), channel_id=1, source_target_pairs={{0,3},{1,2},{2,1},{3,0},{4,7},{5,6},{6,5},{7,4},{8,11},{9,10},{10,... | collective-permute-start | bytes 24584 | tf_op jit(solution)/shard_map/ppermute | solution.py:684
  43.6 3.6 %collective-permute-start.18 = (f32[2,128]{1,0:T(2,128)S(1)}, f32[2,128]{1,0:T(2,128)S(1)}, u32[]{:S(2)}, u32[]{:S(2)}) collective-permute-start(f32[2,128]{1,0:T(2,128)S(1)} %get-tuple-element.85), channel_id=1, source_target_pairs={{0,4},{4,0},{8,12},{12,8},{16,20},{20,16},{24,28},{28,24},{1,5},{5... | collective-permute-start | bytes 3080 | tf_op jit(solution)/shard_map/ppermute | solution.py:681
  44.2 3.0 %collective-permute-start.19 = (f32[2,128]{1,0:T(2,128)S(1)}, f32[2,128]{1,0:T(2,128)S(1)}, u32[]{:S(2)}, u32[]{:S(2)}) collective-permute-start(f32[2,128]{1,0:T(2,128)S(1)} %get-tuple-element.86), channel_id=1, source_target_pairs={{0,1},{1,0},{2,3},{3,2},{4,8},{5,9},{6,10},{7,11},{8,4},{9,5},{10,... | collective-permute-start | bytes 3080 | tf_op jit(solution)/shard_map/ppermute | solution.py:680
  48.3 4.9 %collective-permute-start.20 = (f32[16,128]{1,0:T(8,128)S(1)}, f32[16,128]{1,0:T(8,128)S(1)}, u32[]{:S(2)}, u32[]{:S(2)}) collective-permute-start(f32[16,128]{1,0:T(8,128)S(1)} %get-tuple-element.88.image_ref.refs_4_.refs_1_), channel_id=1, source_target_pairs={{0,1},{1,0},{2,3},{3,2},{4,5},{5,4},{6,7},{7,6},{8,9},{9,8},{10,11... | collective-permute-start | bytes 24584 | tf_op jit(solution)/shard_map/ppermute | solution.py:684
  48.3 4.9 %collective-permute-start.21 = (f32[16,128]{1,0:T(8,128)S(1)}, f32[16,128]{1,0:T(8,128)S(1)}, u32[]{:S(2)}, u32[]{:S(2)}) collective-permute-start(f32[16,128]{1,0:T(8,128)S(1)} %get-tuple-element.88.image_ref.refs_4_.refs_1_), channel_id=1, source_target_pairs={{0,2},{1,3},{2,0},{3,1},{4,6},{5,7},{6,4},{7,5},{8,10},{9,11},{10,... | collective-permute-start | bytes 24584 | tf_op jit(solution)/shard_map/ppermute | solution.py:684
  49.0 4.2 %collective-permute-start.22 = (f32[16,128]{1,0:T(8,128)S(1)}, f32[16,128]{1,0:T(8,128)S(1)}, u32[]{:S(2)}, u32[]{:S(2)}) collective-permute-start(f32[16,128]{1,0:T(8,128)S(1)} %get-tuple-element.88.image_ref.refs_4_.refs_1_), channel_id=1, source_target_pairs={{0,3},{1,2},{2,1},{3,0},{4,7},{5,6},{6,5},{7,4},{8,11},{9,10},{10,... | collective-permute-start | bytes 24584 | tf_op jit(solution)/shard_map/ppermute | solution.py:684
  50.2 4.5 %collective-permute-start.23 = (f32[2,128]{1,0:T(2,128)S(1)}, f32[2,128]{1,0:T(2,128)S(1)}, u32[]{:S(2)}, u32[]{:S(2)}) collective-permute-start(f32[2,128]{1,0:T(2,128)S(1)} %get-tuple-element.89), channel_id=1, source_target_pairs={{0,4},{4,0},{8,12},{12,8},{16,20},{20,16},{24,28},{28,24},{1,5},{5... | collective-permute-start | bytes 3080 | tf_op jit(solution)/shard_map/ppermute | solution.py:681
  55.7 5.3 %collective-permute-start.25 = (f32[16,128]{1,0:T(8,128)S(1)}, f32[16,128]{1,0:T(8,128)S(1)}, u32[]{:S(2)}, u32[]{:S(2)}) collective-permute-start(f32[16,128]{1,0:T(8,128)S(1)} %get-tuple-element.92.image_ref.refs_5_.refs_2_), channel_id=1, source_target_pairs={{0,1},{1,0},{2,3},{3,2},{4,5},{5,4},{6,7},{7,6},{8,9},{9,8},{10,11... | collective-permute-start | bytes 24584 | tf_op jit(solution)/shard_map/ppermute | solution.py:684
  55.8 5.2 %collective-permute-start.26 = (f32[16,128]{1,0:T(8,128)S(1)}, f32[16,128]{1,0:T(8,128)S(1)}, u32[]{:S(2)}, u32[]{:S(2)}) collective-permute-start(f32[16,128]{1,0:T(8,128)S(1)} %get-tuple-element.92.image_ref.refs_5_.refs_2_), channel_id=1, source_target_pairs={{0,2},{1,3},{2,0},{3,1},{4,6},{5,7},{6,4},{7,5},{8,10},{9,11},{10,... | collective-permute-start | bytes 24584 | tf_op jit(solution)/shard_map/ppermute | solution.py:684
  56.3 4.8 %collective-permute-start.27 = (f32[16,128]{1,0:T(8,128)S(1)}, f32[16,128]{1,0:T(8,128)S(1)}, u32[]{:S(2)}, u32[]{:S(2)}) collective-permute-start(f32[16,128]{1,0:T(8,128)S(1)} %get-tuple-element.92.image_ref.refs_5_.refs_2_), channel_id=1, source_target_pairs={{0,3},{1,2},{2,1},{3,0},{4,7},{5,6},{6,5},{7,4},{8,11},{9,10},{10,... | collective-permute-start | bytes 24584 | tf_op jit(solution)/shard_map/ppermute | solution.py:684
  57.6 4.5 %collective-permute-start.28 = (f32[2,128]{1,0:T(2,128)S(1)}, f32[2,128]{1,0:T(2,128)S(1)}, u32[]{:S(2)}, u32[]{:S(2)}) collective-permute-start(f32[2,128]{1,0:T(2,128)S(1)} %get-tuple-element.93), channel_id=1, source_target_pairs={{0,4},{4,0},{8,12},{12,8},{16,20},{20,16},{24,28},{28,24},{1,5},{5... | collective-permute-start | bytes 3080 | tf_op jit(solution)/shard_map/ppermute | solution.py:681
  (7 other events, 18.8 us)
